TPU v7x, 256 devices: a whole 4x4x8 slice. The times are simulated.
256 devices in a mesh: tm: 128 (over z_hi, y, x, core), rows: 2 (over z_lo).
Axes of the slice: x: 4, y: 4, z: 8 (z_hi: 4, z_lo: 2; z = z_hi * 2 + z_lo), core: 2. Of those that a mesh axis runs over, the one named last changes fastest.
Arguments:
- resid: float32 [2, 128, 16, 512], P(None, 'tm', 'rows'), may hold values from -3 to 3
- basis: float32 [4, 2, 128, 16, 512], P(None, None, 'tm', 'rows'), may hold values from -0.0041432036 to 0.0041432036
Outputs:
- precond: float32 [2, 128, 16, 512], P(None, 'tm', 'rows')
- image: float32 [2, 128, 16, 512], P(None, 'tm', 'rows')
- gram: float32 [5], replicated
All inputs are finite; a program needn't handle non-finite values.
Results may differ from a plain program's by a relative error of at most 0.0005.
Values sent between devices are 32-bit elements; how exact they have to be, the bound alone decides.
No kernel may reach another device: no remote copies, remote signals or barrier semaphores. Data moves between devices by JAX's collectives and lax.ppermute only.
A program may use at most 64 MiB of HBM per device.

v0:
```python
import functools
import math

import jax
import jax.numpy as jnp
from jax import lax
from jax.sharding import Mesh
from jax.sharding import PartitionSpec as P

SWEEPS = 4
TM = ("tm_0", "tm_1", "tm_2", "tm_3")
TM_ROWS = ("tm_0", "tm_1", "tm_2", "tm_3", "rows")


ALPHA = 0.01


def in_blocks(shard, dim, count):
    before, after = (shard.shape[:dim], shard.shape[dim + 1 :])
    return jnp.moveaxis(shard.reshape(*before, count, -1, *after), dim, 0)


def joined_along(tiles, dim):
    tiles = jnp.moveaxis(tiles, 0, dim)
    dims = tiles.shape
    return tiles.reshape(*dims[:dim], dims[dim] * dims[dim + 1], *dims[dim + 2 :])


def moved_by_axis(tiles, axes, sequence):
    inside = tiles.shape[1:]
    whole = tiles.reshape(*(lax.axis_size(a) for a in axes), *inside)
    for k in sequence:
        whole = lax.all_to_all(whole, axes[k], k, k, tiled=True)
    return whole.reshape(-1, *inside)


def exchange_by_chip(shard, groups, sequence, split_dim, concat_dim):
    count = lax.axis_size(groups[0]) * lax.axis_size(groups[1])
    tiles = in_blocks(shard, split_dim, count)
    return joined_along(moved_by_axis(tiles, groups, sequence), concat_dim)


def padded_2(shard, sides, width):
    for axis, dim in sides:
        count, length = (lax.axis_size(axis), shard.shape[dim])
        up = [(i, (i + 1) % count) for i in range(count - 1)]
        down = [(j, i) for i, j in up]
        last = lax.slice_in_dim(shard, length - width, length, axis=dim)
        first = lax.slice_in_dim(shard, 0, width, axis=dim)
        before = lax.ppermute(last, axis, up)
        after = lax.ppermute(first, axis, down)
        shard = jnp.concatenate([before, shard, after], axis=dim)
    return shard


def shifted(value, axis, steps):
    count = lax.axis_size(axis)
    first, last = (max(0, -steps), min(count, count - steps))
    return lax.ppermute(value, axis, [(source, source + steps) for source in range(first, last)])


def over_axes(shard, axes):
    return functools.reduce(lax.psum, axes, shard)


def neighbours(padded):
    middle = padded[:, 1:-1]
    sides = jnp.pad(middle, ((0, 0), (0, 0), (1, 1)))
    return padded[:, 2:] + padded[:, :-2] + sides[:, :, 2:] + sides[:, :, :-2]


def cmul(left, right_re, right_im):
    return jnp.stack(
        [left[0] * right_re - left[1] * right_im, left[0] * right_im + left[1] * right_re]
    )


def phases(first, second, steps):
    turns = first * second % steps
    angle = turns.astype(jnp.float32) * (2.0 * math.pi / steps)
    return (jnp.cos(angle), jnp.sin(angle))


def on_device(resid, basis):
    steps = lax.axis_size(TM)
    coupling = 16.0 / (steps * steps)
    me = lax.axis_index(TM)
    rows_dev = resid.shape[2]
    cols = resid.shape[3]
    cells = rows_dev * cols
    piece = cells // steps
    mine = me.astype(jnp.float32)
    gamma = jnp.power(jnp.float32(ALPHA), mine / steps)
    scaled = resid[:, 0] * gamma
    ordinal = jnp.arange(steps, dtype=jnp.int32)
    cos_table, sin_table = phases(ordinal[:, None], ordinal[None, :], steps)
    blocks = exchange_by_chip(
        scaled.reshape(1, 2, cells), (("tm_0", "tm_1", "tm_2"), "tm_3"), (1, 0), 2, 0
    )
    flat = blocks.reshape(steps, 2 * piece)
    real_part = jnp.dot(cos_table, flat, precision=lax.Precision.HIGHEST)
    imag_part = -jnp.dot(sin_table, flat, precision=lax.Precision.HIGHEST)
    stacked = jnp.stack([real_part, imag_part], 1).reshape(steps, 2, 2, piece)
    spectrum = lax.all_to_all(stacked, TM, split_axis=0, concat_axis=3, tiled=True)
    rhat = spectrum[0].reshape(2, 2, rows_dev, cols)
    base = jnp.power(jnp.float32(ALPHA), jnp.float32(1.0) / steps)
    angle = mine * (2.0 * math.pi / steps)
    lam_re = 1.0 - base * jnp.cos(angle)
    lam_im = base * jnp.sin(angle)
    disp_spec = rhat[:, 0]
    right = cmul(disp_spec, lam_re, lam_im) + rhat[:, 1]
    den_re = lam_re * lam_re - lam_im * lam_im + 4.0 * coupling
    den_im = 2.0 * lam_re * lam_im
    magnitude = den_re * den_re + den_im * den_im
    inv_re = den_re / magnitude
    inv_im = -den_im / magnitude
    depth = SWEEPS
    wide = padded_2(right, (("rows", 1),), depth)
    total_rows = rows_dev * lax.axis_size("rows")
    place = (
        lax.axis_index("rows") * rows_dev
        - depth
        + jnp.arange(rows_dev + 2 * depth, dtype=jnp.int32)
    )
    inside = ((place >= 0) & (place < total_rows)).astype(jnp.float32)[None, :, None]
    uhat = cmul(wide, inv_re, inv_im) * inside
    for sweep in range(SWEEPS - 1):
        padded = jnp.pad(uhat, ((0, 0), (1, 1), (0, 0)))
        uhat = cmul(wide + coupling * neighbours(padded), inv_re, inv_im) * inside
    uhat = uhat[:, depth : depth + rows_dev]
    vhat = cmul(uhat, lam_re, lam_im) - disp_spec
    yhat = jnp.stack([uhat, vhat], 1)
    spread = exchange_by_chip(
        yhat.reshape(1, 2, 2, cells), (("tm_0", "tm_1", "tm_2"), "tm_3"), (1, 0), 3, 0
    )
    real_rows = spread[:, 0].reshape(steps, 2 * piece)
    imag_rows = spread[:, 1].reshape(steps, 2 * piece)
    undo = jnp.power(jnp.float32(ALPHA), -ordinal.astype(jnp.float32) / steps) / steps
    history = jnp.dot(cos_table, real_rows, precision=lax.Precision.HIGHEST) - jnp.dot(
        sin_table, imag_rows, precision=lax.Precision.HIGHEST
    )
    history = (history * undo[:, None]).reshape(steps, 2, piece)
    returned = exchange_by_chip(history, (("tm_0", "tm_1", "tm_2"), "tm_3"), (1, 0), 0, 2)
    precond = returned[0].reshape(2, rows_dev, cols)
    earlier = shifted(precond, TM, 1)
    disp_rim = padded_2(precond[0:1], (("rows", 1),), 1)
    laplace = neighbours(disp_rim)[0] - 4.0 * precond[0]
    first = precond[0] - earlier[0] - precond[1]
    second = precond[1] - earlier[1] - coupling * laplace
    image = jnp.stack([first, second])
    inner = jnp.sum(basis[:, :, 0] * image[None], axis=(1, 2, 3))
    count = 2.0 * steps * rows_dev * lax.axis_size("rows") * cols
    squares = jnp.sum(image * image) / count
    local_terms = jnp.concatenate([inner, squares[None]])
    gram = over_axes(local_terms, TM_ROWS)
    return (precond[:, None], image[:, None], gram)


def solution(mesh):
    split = Mesh(
        mesh.devices.reshape(4, 4, 4, 2, mesh.shape["rows"]),
        ("tm_0", "tm_1", "tm_2", "tm_3", "rows"),
    )
    return jax.shard_map(
        on_device,
        mesh=split,
        in_specs=(P(None, TM, "rows", None), P(None, None, TM, "rows", None)),
        out_specs=(P(None, TM, "rows", None), P(None, TM, "rows", None), P()),
        check_vma=False,
    )
```

profile of v0, /device:TPU:1, one launch (start us, length us, event | category | flops | bytes accessed | tf_op | source)
XLA Modules:
  0.0 160.9 jit_solution(3938874216098775222)
XLA Ops:
  0.7 0.7 copy-done.1
  1.7 6.6 %all_to_all.45 = f32[2,1,4096]{2,1,0:T(1,128)S(1)} all-to-all(f32[2,1,4096]{2,1,0:T(1,128)S(1)} %reshape.143), channel_id=1, replica_groups=mesh['tm_0'=4,'tm_1'=4,'tm_2'=4,'tm_3'=2,'rows'=2] {'tm_3'}, dimensions={0} | all-to-all | bytes 65536 | tf_op jit(solution)/shard_map/all_to_all | solution.py:33
  8.8 0.7 reduce
  10.0 23.1 %all_to_all.46 = f32[64,1,128]{2,1,0:T(1,128)S(1)} all-to-all(f32[64,1,128]{2,1,0:T(1,128)S(1)} %reshape.145), channel_id=1, replica_groups=mesh['tm_0'=4,'tm_1'=4,'tm_2'=4,'tm_3'=2,'rows'=2] {'tm_0','tm_1','tm_2'}, dimensions={0} | all-to-all | bytes 65536 | tf_op jit(solution)/shard_map/all_to_all | solution.py:33
  33.1 0.7 reduce.1
  35.4 0.9 reshape.147
  36.3 7.0 %all-to-all-start.2 = ((f32[128,1,128]{2,1,0:T(1,128)}), f32[128,1,128]{2,1,0:T(1,128)S(1)}, u32[]{:S(2)}, u32[]{:S(2)}) async-start(f32[128,1,128]{2,1,0:T(1,128)} %reshape.147), calls=%async_computation.2 | async-start | bytes 131072 | tf_op jit(solution)/shard_map/all_to_all | solution.py:104
  43.4 11.6 %all-to-all-done.2 = f32[128,1,128]{2,1,0:T(1,128)S(1)} async-done(((f32[128,1,128]{2,1,0:T(1,128)}), f32[128,1,128]{2,1,0:T(1,128)S(1)}, u32[]{:S(2)}, u32[]{:S(2)}) %all-to-all-start.2) | async-done | bytes 65568 | tf_op jit(solution)/shard_map/all_to_all | solution.py:104
  55.0 0.8 reduce.2
  56.3 2.8 %collective-permute-start = (f32[2,4,512]{2,1,0:T(4,128)S(1)}, f32[2,4,512]{2,1,0:T(4,128)S(1)}, u32[]{:S(2)}, u32[]{:S(2)}) collective-permute-start(f32[2,4,512]{2,1,0:T(4,128)S(1)} %get-tuple-element.36), channel_id=1, source_target_pairs={{0,1},{2,3},{4,5},{6,7},{8,9},{10,11},{12,13},{14,15},{16,17},{18,... | collective-permute-start | bytes 49160 | tf_op jit(solution)/shard_map/ppermute | solution.py:50
  59.0 1.3 collective-permute-start.1
  60.5 3.1 %collective-permute-done.1 = f32[2,4,512]{2,1,0:T(4,128)S(1)} collective-permute-done((f32[2,4,512]{2,1,0:T(4,128)S(1)}, f32[2,4,512]{2,1,0:T(4,128)S(1)}, u32[]{:S(2)}, u32[]{:S(2)}) %collective-permute-start.1) | collective-permute-done | bytes 16416 | tf_op jit(solution)/shard_map/ppermute | solution.py:51
  65.1 5.7 %all_to_all.47 = f32[2,1,8192]{2,1,0:T(1,128)S(1)} all-to-all(f32[2,1,8192]{2,1,0:T(1,128)S(1)} %reshape.149), channel_id=1, replica_groups=mesh['tm_0'=4,'tm_1'=4,'tm_2'=4,'tm_3'=2,'rows'=2] {'tm_3'}, dimensions={0} | all-to-all | bytes 131072 | tf_op jit(solution)/shard_map/all_to_all | solution.py:33
  70.8 0.8 reduce.3
  72.0 0.9 reshape.151
  72.9 4.6 %all-to-all-start.4 = ((f32[64,1,256]{2,1,0:T(1,128)}), f32[64,1,256]{2,1,0:T(1,128)S(1)}, u32[]{:S(2)}, u32[]{:S(2)}) async-start(f32[64,1,256]{2,1,0:T(1,128)} %reshape.151), calls=%async_computation.4 | async-start | bytes 131072 | tf_op jit(solution)/shard_map/all_to_all | solution.py:33
  77.5 10.8 %all-to-all-done.4 = f32[64,1,256]{2,1,0:T(1,128)S(1)} async-done(((f32[64,1,256]{2,1,0:T(1,128)}), f32[64,1,256]{2,1,0:T(1,128)S(1)}, u32[]{:S(2)}, u32[]{:S(2)}) %all-to-all-start.4) | async-done | bytes 65568 | tf_op jit(solution)/shard_map/all_to_all | solution.py:33
  88.3 0.8 reduce.4
  91.1 4.9 %all_to_all.48 = f32[2,1,4096]{2,1,0:T(1,128)S(1)} all-to-all(f32[2,1,4096]{2,1,0:T(1,128)S(1)} %reshape.153), channel_id=1, replica_groups=mesh['tm_0'=4,'tm_1'=4,'tm_2'=4,'tm_3'=2,'rows'=2] {'tm_3'}, dimensions={0} | all-to-all | bytes 65536 | tf_op jit(solution)/shard_map/all_to_all | solution.py:33
  96.0 0.7 reduce.5
  97.1 14.7 %all_to_all.49 = f32[64,1,128]{2,1,0:T(1,128)S(1)} all-to-all(f32[64,1,128]{2,1,0:T(1,128)S(1)} %reshape.155), channel_id=1, replica_groups=mesh['tm_0'=4,'tm_1'=4,'tm_2'=4,'tm_3'=2,'rows'=2] {'tm_0','tm_1','tm_2'}, dimensions={0} | all-to-all | bytes 65536 | tf_op jit(solution)/shard_map/all_to_all | solution.py:33
  111.8 0.7 reduce.6
  113.0 3.9 %collective-permute-start.2 = (f32[2,8,512]{2,1,0:T(8,128)S(1)}, f32[2,8,512]{2,1,0:T(8,128)S(1)}, u32[]{:S(2)}, u32[]{:S(2)}) collective-permute-start(f32[2,8,512]{2,1,0:T(8,128)S(1)} %reshape_squeeze_reshape.3), channel_id=1, source_target_pairs={{0,2},{2,4},{4,6},{6,8},{8,10},{10,12},{12,14},{14,16},{16,18},{18... | collective-permute-start | bytes 98312 | tf_op jit(solution)/shard_map/ppermute | solution.py:59
  116.9 1.3 collective-permute-start.3
  118.2 4.0 %collective-permute-start.4 = (f32[1,1,512]{2,1,0:T(1,128)S(1)}, f32[1,1,512]{2,1,0:T(1,128)S(1)}, u32[]{:S(2)}, u32[]{:S(2)}) collective-permute-start(f32[1,1,512]{2,1,0:T(1,128)S(1)} %get-tuple-element.39), channel_id=1, source_target_pairs={{0,1},{2,3},{4,5},{6,7},{8,9},{10,11},{12,13},{14,15},{16,17},{18,... | collective-permute-start | bytes 6152 | tf_op jit(solution)/shard_map/ppermute | solution.py:50
  123.0 1.2 pad_maximum_fusion.2
  125.1 7.6 %psum.35 = f32[5]{0:T(128)S(1)} all-reduce(f32[5]{0:T(128)S(1)} %pad_maximum_fusion.5), channel_id=1, replica_groups=mesh['tm_0'=4,'tm_1'=4,'tm_2'=4,'tm_3'=2,'rows'=2] {'tm_0'}, use_global_device_ids=true, to_apply=%region_2.3 | all-reduce | flops 5 | bytes 40 | tf_op jit(solution)/shard_map/psum | solution.py:63
  132.7 6.9 %psum.36 = f32[5]{0:T(128)S(1)} all-reduce(f32[5]{0:T(128)S(1)} %psum.35), channel_id=1, replica_groups=mesh['tm_0'=4,'tm_1'=4,'tm_2'=4,'tm_3'=2,'rows'=2] {'tm_1'}, use_global_device_ids=true, to_apply=%region_3.4 | all-reduce | flops 5 | bytes 40 | tf_op jit(solution)/shard_map/psum | solution.py:63
  139.6 9.6 %psum.37 = f32[5]{0:T(128)S(1)} all-reduce(f32[5]{0:T(128)S(1)} %psum.36), channel_id=1, replica_groups=mesh['tm_0'=4,'tm_1'=4,'tm_2'=4,'tm_3'=2,'rows'=2] {'tm_2'}, use_global_device_ids=true, to_apply=%region_4.5 | all-reduce | flops 5 | bytes 40 | tf_op jit(solution)/shard_map/psum | solution.py:63
  149.1 6.2 %psum.38 = f32[5]{0:T(128)S(1)} all-reduce(f32[5]{0:T(128)S(1)} %psum.37), channel_id=1, replica_groups=mesh['tm_0'=4,'tm_1'=4,'tm_2'=4,'tm_3'=2,'rows'=2] {'tm_3'}, use_global_device_ids=true, to_apply=%region_5.6 | all-reduce | flops 5 | bytes 40 | tf_op jit(solution)/shard_map/psum | solution.py:63
  155.4 0.7 broadcast_in_dim_reshape_squeeze_reshape.3
  156.1 4.8 %psum.39 = f32[5]{0:T(128)} all-reduce(f32[5]{0:T(128)S(1)} %psum.38), channel_id=1, replica_groups=mesh['tm_0'=4,'tm_1'=4,'tm_2'=4,'tm_3'=2,'rows'=2] {'rows'}, use_global_device_ids=true, to_apply=%region_6.7 | all-reduce | flops 5 | bytes 40 | tf_op jit(solution)/shard_map/psum | solution.py:63
  (79 shorter events, 8.6 us)
Async XLA Ops:
  0.6 0.8 copy-start.1
  36.3 18.7 %all-to-all-start.2 = ((f32[128,1,128]{2,1,0:T(1,128)}), f32[128,1,128]{2,1,0:T(1,128)S(1)}, u32[]{:S(2)}, u32[]{:S(2)}) async-start(f32[128,1,128]{2,1,0:T(1,128)} %reshape.147), calls=%async_computation.2 | async-start | bytes 131072 | tf_op jit(solution)/shard_map/all_to_all | solution.py:104
  56.3 4.2 %collective-permute-start = (f32[2,4,512]{2,1,0:T(4,128)S(1)}, f32[2,4,512]{2,1,0:T(4,128)S(1)}, u32[]{:S(2)}, u32[]{:S(2)}) collective-permute-start(f32[2,4,512]{2,1,0:T(4,128)S(1)} %get-tuple-element.36), channel_id=1, source_target_pairs={{0,1},{2,3},{4,5},{6,7},{8,9},{10,11},{12,13},{14,15},{16,17},{18,... | collective-permute-start | bytes 49160 | tf_op jit(solution)/shard_map/ppermute | solution.py:50
  59.0 4.5 %collective-permute-start.1 = (f32[2,4,512]{2,1,0:T(4,128)S(1)}, f32[2,4,512]{2,1,0:T(4,128)S(1)}, u32[]{:S(2)}, u32[]{:S(2)}) collective-permute-start(f32[2,4,512]{2,1,0:T(4,128)S(1)} %get-tuple-element.37), channel_id=1, source_target_pairs={{1,0},{3,2},{5,4},{7,6},{9,8},{11,10},{13,12},{15,14},{17,16},{19,... | collective-permute-start | bytes 49160 | tf_op jit(solution)/shard_map/ppermute | solution.py:51
  72.9 15.5 %all-to-all-start.4 = ((f32[64,1,256]{2,1,0:T(1,128)}), f32[64,1,256]{2,1,0:T(1,128)S(1)}, u32[]{:S(2)}, u32[]{:S(2)}) async-start(f32[64,1,256]{2,1,0:T(1,128)} %reshape.151), calls=%async_computation.4 | async-start | bytes 131072 | tf_op jit(solution)/shard_map/all_to_all | solution.py:33
  113.0 9.9 %collective-permute-start.2 = (f32[2,8,512]{2,1,0:T(8,128)S(1)}, f32[2,8,512]{2,1,0:T(8,128)S(1)}, u32[]{:S(2)}, u32[]{:S(2)}) collective-permute-start(f32[2,8,512]{2,1,0:T(8,128)S(1)} %reshape_squeeze_reshape.3), channel_id=1, source_target_pairs={{0,2},{2,4},{4,6},{6,8},{8,10},{10,12},{12,14},{14,16},{16,18},{18... | collective-permute-start | bytes 98312 | tf_op jit(solution)/shard_map/ppermute | solution.py:59
  116.9 5.4 %collective-permute-start.3 = (f32[1,1,512]{2,1,0:T(1,128)S(1)}, f32[1,1,512]{2,1,0:T(1,128)S(1)}, u32[]{:S(2)}, u32[]{:S(2)}) collective-permute-start(f32[1,1,512]{2,1,0:T(1,128)S(1)} %get-tuple-element.38), channel_id=1, source_target_pairs={{1,0},{3,2},{5,4},{7,6},{9,8},{11,10},{13,12},{15,14},{17,16},{19,... | collective-permute-start | bytes 6152 | tf_op jit(solution)/shard_map/ppermute | solution.py:51
  118.2 4.7 %collective-permute-start.4 = (f32[1,1,512]{2,1,0:T(1,128)S(1)}, f32[1,1,512]{2,1,0:T(1,128)S(1)}, u32[]{:S(2)}, u32[]{:S(2)}) collective-permute-start(f32[1,1,512]{2,1,0:T(1,128)S(1)} %get-tuple-element.39), channel_id=1, source_target_pairs={{0,1},{2,3},{4,5},{6,7},{8,9},{10,11},{12,13},{14,15},{16,17},{18,... | collective-permute-start | bytes 6152 | tf_op jit(solution)/shard_map/ppermute | solution.py:50
  122.2 2.7 %copy-start = (f32[4,2,1,8,512]{4,3,2,1,0:T(8,128)S(1)}, f32[4,2,1,8,512]{4,3,2,1,0:T(8,128)}, u32[]{:S(2)}) copy-start(f32[4,2,1,8,512]{4,3,2,1,0:T(8,128)} %param.3) | copy-start | bytes 393220
where the time goes:
time: 162 us; the launch traced here: 161 us
  blocking collectives  90.1 us (56%)
  waiting for transfers between devices  26.1 us (16%)
  starting transfers between devices  24.8 us (15%)
  local copies, waits for them, and re-layouts  8.2 us (5%)
  other arithmetic  7.61 us (5%)
  between operations  2.08 us (1%)
  matrix products  1.98 us (1%)
    all_to_all x5, blocking collectives, moved_by_axis(): whole = lax.all_to_all(whole, axes[k], k, k, tiled=True)  55 us
    psum x5, blocking collectives, over_axes(): return functools.reduce(lax.psum, axes, shard)  35.1 us
    all_to_all x1, waiting for transfers between devices, on_device(): lax.all_to_all(stacked, TM, split_axis=0, concat_axis=3, tiled=True)  11.6 us
    all_to_all x1, waiting for transfers between devices, moved_by_axis(): whole = lax.all_to_all(whole, axes[k], k, k, tiled=True)  10.8 us
    all_to_all x1, starting transfers between devices, on_device(): lax.all_to_all(stacked, TM, split_axis=0, concat_axis=3, tiled=True)  6.96 us
    ppermute x2, starting transfers between devices, padded_2(): before = lax.ppermute(last, axis, up)  6.76 us
    all_to_all x1, starting transfers between devices, moved_by_axis(): whole = lax.all_to_all(whole, axes[k], k, k, tiled=True)  4.61 us
    all_to_all x6, other arithmetic, moved_by_axis(): whole = lax.all_to_all(whole, axes[k], k, k, tiled=True)  4.55 us
  transfers between devices with their start and end apart: 7, of which 4 were waited for; matrix products, arithmetic and copies ran while one was open for 0% of the time, Pallas kernels for 0%

commit v1 on v0

v1 whole, which is shorter than its diff:
```python
import jax
import jax.numpy as jnp
import numpy as np
from jax import lax
from jax.experimental import pallas as pl
from jax.experimental.pallas import tpu as pltpu
from jax.sharding import PartitionSpec as P

ALPHA = 0.01
SWEEPS = 4
KRYLOV = 4
LANES = 128
ROWS = 8
SLOTS = 3
BASE = 80
FIELD = 2 * ROWS
OUT = 64


def roll(value, amount, axis):
    size = value.shape[axis]
    return pltpu.roll(value, amount % size, axis)


def time_tables(steps):
    kappa = 16.0 / (steps * steps)
    index = np.arange(steps)
    gamma = ALPHA ** (index / steps)
    lam = 1.0 - ALPHA ** (1.0 / steps) * np.exp(-2j * np.pi * index / steps)
    den = lam * lam + 4.0 * kappa
    turn = np.exp(-2j * np.pi * np.outer(index, index) / steps)
    tables = []
    for m in range(SWEEPS):
        inner = np.conj(turn) @ ((1.0 / den ** (m + 1))[:, None] * turn) / steps
        tables.append(kappa**m * (inner.real / gamma[:, None]) * gamma[None, :])
    return np.concatenate(tables, 1).astype(np.float32)


def space_table(steps):
    kappa = 16.0 / (steps * steps)
    rows = 2 * ROWS
    shift = np.eye(rows, k=1) + np.eye(rows, k=-1)
    table = np.zeros((2, LANES, 2 * LANES))
    for m in range(SWEEPS + 1):
        for k in range(m + 1):
            ways = float(np.prod(np.arange(m - k + 1, m + 1)) / np.prod(np.arange(1, k + 1)))
            part = ways * np.linalg.matrix_power(shift, m - k)
            for row in range(rows):
                for out in range(rows):
                    lane = m * 4 * ROWS + (out // ROWS) * 2 * ROWS + out % ROWS
                    for c in range(2):
                        source = k * 2 * ROWS + c * ROWS + row % ROWS
                        table[row // ROWS, source, lane] = part[row, out]
    return table.reshape(2 * LANES, 2 * LANES).astype(np.float32), kappa


def lane_of(shape):
    return lax.broadcasted_iota(jnp.int32, shape, len(shape) - 1)


def packed(resid, basis):
    cols = resid.shape[-1]
    half = cols // 2
    flat = resid.reshape(2 * ROWS, cols)
    lane = lane_of(flat.shape)
    powers = [flat]
    for _ in range(SWEEPS):
        last = powers[-1]
        right = jnp.where(lane == 0, 0.0, roll(last, 1, 1))
        left = jnp.where(lane == cols - 1, 0.0, roll(last, -1, 1))
        powers.append(right + left)
    disp, velo = flat[:ROWS], flat[ROWS:]
    pair = lambda v: [v[:, :half], v[:, half:]]
    first = [p[:, :half] for p in powers] + pair(-disp) + pair(disp) + pair(velo)
    second = [p[:, half:] for p in powers]
    second.append(jnp.zeros((LANES - BASE, half), jnp.float32))
    third = []
    for c in range(2):
        for i in range(KRYLOV):
            third += pair(basis[i, c])
    return [jnp.concatenate(rows, 0).T for rows in (first, second, third)]


def delayed(value):
    row = lax.broadcasted_iota(jnp.int32, value.shape, 0)
    moved = roll(value, 1, 0)
    return jnp.where(row == 0, ALPHA * moved, moved)


def dot(left, right):
    return jnp.dot(
        left, right, precision=lax.Precision.HIGHEST, preferred_element_type=jnp.float32
    )


def solved(parts, time_table, space, kappa, count):
    steps = parts[0][0].shape[0]
    shape = (steps, LANES)
    lane = lane_of(shape)
    row = lax.broadcasted_iota(jnp.int32, shape, 0)
    is_disp = (lane & ROWS) == 0
    mixed = []
    for dc in range(2):
        sides = []
        for h in range(2):
            x = parts[h][dc]
            sides.append(jnp.where(is_disp, x - delayed(x), x))
        mixed.append(jnp.concatenate(sides, 1))
    spread = dot(jnp.concatenate(mixed, 0), space)
    both = spread[:steps] + roll(spread[steps:], ROWS, 1)
    low, high = both[:, :LANES], both[:, LANES:]
    group = 4 * ROWS
    stack = [jnp.where(lane // group == m, low, 0.0) for m in range(SWEEPS)]
    disp = dot(time_table, jnp.concatenate(stack, 0))
    disp = disp + roll(disp, 2 * group, 1)
    disp = disp + roll(disp, group, 1)
    rest = dot(time_table[:, (SWEEPS - 1) * steps :], high) * kappa
    rest = rest + roll(rest, 2 * group, 1)
    rest = rest + roll(rest, group, 1)
    late = delayed(disp)
    rate = disp - late
    edge = jnp.where(row == 0, late, 0.0)
    place = (lane - OUT) // FIELD
    outs, sums, square = [], 0.0, 0.0
    for h in range(2):
        flip = lambda v, slot: roll(v, FIELD, 1) if (slot + h) % 2 else v
        add = jnp.where(place == 0, flip(disp, 0), 0.0)
        add = jnp.where(place == 1, flip(rate, 1), add)
        add = jnp.where(place == 2, flip(edge, 2), add)
        add = jnp.where(place == 3, flip(-rest, 3), add)
        out = jnp.where(lane >= BASE, parts[h][0], 0.0) + add
        wrap = jnp.where((row == 0) & (place == 3), delayed(roll(out, 2 * FIELD, 1)), 0.0)
        out = out + wrap
        outs.append(out)
        image = jnp.where(place >= 2, out, 0.0)
        square = square + jnp.sum(image * image, 0, keepdims=True)
        turns = []
        for slot in (2, 3):
            turn = jnp.where(place == slot, out, 0.0)
            for fold in (FIELD, 2 * FIELD, 4 * FIELD):
                turn = turn + roll(turn, fold, 1)
            turns.append(turn)
        wanted = jnp.where(lane < OUT, turns[0], turns[1])
        sums = sums + jnp.sum(parts[h][2] * wanted, 0, keepdims=True)
    sums = sums + roll(sums, OUT, 1)
    sums = sums + roll(sums, -ROWS, 1)
    square = square + roll(square, FIELD, 1)
    square = square + roll(square, ROWS, 1)
    at = lane_of((1, LANES))
    square = roll(square, ROWS - (OUT + 3 * FIELD + ROWS), 1) * (1.0 / count)
    gram = jnp.where((at >= ROWS) & (at < 2 * ROWS), square, sums)
    return [jnp.where(lane < OUT, jnp.broadcast_to(gram, shape), out) for out in outs]


def gram_of(totals):
    at = lane_of(totals.shape)
    picks = [(at // FIELD == i) & (at % FIELD < ROWS) for i in range(KRYLOV)]
    picks.append((at >= ROWS) & (at < FIELD))
    return [jnp.sum(jnp.where(pick, totals, 0.0)) for pick in picks]


def pack_kernel(resid_ref, basis_ref, send_ref):
    slabs = packed(resid_ref[:, 0], basis_ref[:, :, 0])
    for slot, slab in enumerate(slabs):
        send_ref[pl.ds(slot, slab.shape[0], stride=SLOTS), :] = slab


def solve_kernel(kappa, count, recv_ref, time_ref, space_ref, send_ref):
    steps = time_ref.shape[0]
    parts = [
        [recv_ref[pl.ds(h * SLOTS + s, steps, stride=2 * SLOTS), :] for s in range(SLOTS)]
        for h in range(2)
    ]
    outs = solved(parts, time_ref[...], space_ref[...], kappa, count)
    for h, out in enumerate(outs):
        send_ref[pl.ds(h, steps, stride=2), :] = out


def unpack_kernel(recv_ref, precond_ref, image_ref, gram_ref):
    received = recv_ref[...]
    half = received.shape[0]
    turned = received.T
    for slot, (ref, c) in enumerate(
        ((precond_ref, 0), (precond_ref, 1), (image_ref, 0), (image_ref, 1))
    ):
        for dc in range(2):
            start = OUT + slot * FIELD + dc * ROWS
            ref[c, 0, :, dc * half : (dc + 1) * half] = turned[start : start + ROWS]
    for i, value in enumerate(gram_of(jnp.sum(received, 0, keepdims=True))):
        gram_ref[i] = value


def solution(mesh):
    axes = ("tm", "rows")
    steps = mesh.shape["tm"]
    devices = steps * mesh.shape["rows"]

    def on_device(resid, basis):
        cols = resid.shape[3]
        count = 2.0 * steps * 2 * ROWS * cols
        time_table = jnp.asarray(time_tables(steps))
        space, kappa = space_table(steps)
        send = pl.pallas_call(
            pack_kernel,
            out_shape=jax.ShapeDtypeStruct((devices * SLOTS, LANES), jnp.float32),
            name="pack",
        )(resid, basis)
        send = send.reshape(devices, 1, SLOTS * LANES)
        recv = lax.all_to_all(send, axes, 0, 0, tiled=True)
        recv = recv.reshape(devices * SLOTS, LANES)
        back = pl.pallas_call(
            lambda *refs: solve_kernel(kappa, count, *refs),
            out_shape=jax.ShapeDtypeStruct((devices, LANES), jnp.float32),
            name="solve",
        )(recv, time_table, jnp.asarray(space))
        home = lax.all_to_all(back, axes, 0, 0, tiled=True)
        shard = jax.ShapeDtypeStruct(resid.shape, jnp.float32)
        vmem = pl.BlockSpec(memory_space=pltpu.VMEM)
        precond, image, gram = pl.pallas_call(
            unpack_kernel,
            out_shape=(shard, shard, jax.ShapeDtypeStruct((KRYLOV + 1,), jnp.float32)),
            out_specs=(vmem, vmem, pl.BlockSpec(memory_space=pltpu.SMEM)),
            name="unpack",
        )(home)
        return precond, image, gram

    return jax.shard_map(
        on_device,
        mesh=mesh,
        in_specs=(P(None, "tm", "rows", None), P(None, None, "tm", "rows", None)),
        out_specs=(P(None, "tm", "rows", None), P(None, "tm", "rows", None), P()),
        check_vma=False,
    )
```

time: 162 us -> 62.8 us (0.39)
  blocking collectives: 90.1 us -> 54.3 us
  waiting for transfers between devices: 26.1 us -> 0 us
  starting transfers between devices: 24.8 us -> 0 us
  local copies, waits for them, and re-layouts: 8.2 us -> 0 us
  Pallas kernels: 0 us -> 7.64 us
  other arithmetic: 7.61 us -> 0 us
  matrix products: 1.98 us -> 0 us
    psum x5 -> x0, blocking collectives: 35.1 us -> none  [over_axes(): return functools.reduce(lax.psum, axes, shard)]
    all_to_all x2 -> x0, waiting for transfers between devices: 22.4 us -> none  [the longest x1 11.6 us: on_device(): lax.all_to_all(stacked, TM, split_axis=0, concat_axis=3, tiled=True)]
    ppermute x5 -> x0, starting transfers between devices: 13.2 us -> none  [the longest x2 6.76 us: padded_2(): before = lax.ppermute(last, axis, up)]
    all_to_all x2 -> x0, starting transfers between devices: 11.6 us -> none  [the longest x1 6.96 us: on_device(): lax.all_to_all(stacked, TM, split_axis=0, concat_axis=3, tiled=True)]
    pallas_call x0 -> x3, Pallas kernels: none -> 7.64 us  [the longest x1 3.78 us: on_device(): pl.pallas_call(lambda *refs: solve_kernel(kappa, count, *refs), out_shape...]
    all_to_all x7 -> x0, other arithmetic: 5.35 us -> none  [the longest x6 4.55 us: moved_by_axis(): whole = lax.all_to_all(whole, axes[k], k, k, tiled=True)]
    unnamed x18 -> x0, local copies, waits for them, and re-layouts: 4.27 us -> none
    ppermute x5 -> x0, waiting for transfers between devices: 3.67 us -> none  [the longest x2 3.06 us: padded_2(): after = lax.ppermute(first, axis, down)]
  transfers between devices with their start and end apart: 7 -> 0, of which waited for: 4 -> 0; matrix products, arithmetic and copies ran while one was open for 0% -> 0% of each run, Pallas kernels for 0% -> 0%
where the time goes in v1:
time: 62.8 us; the launch traced here: 62.6 us
  blocking collectives  54.3 us (86%)
  Pallas kernels  7.64 us (12%)
  between operations  0.63 us (1%)
    all_to_all x1, blocking collectives, on_device(): recv = lax.all_to_all(send, axes, 0, 0, tiled=True)  33.2 us
    all_to_all x1, blocking collectives, on_device(): home = lax.all_to_all(back, axes, 0, 0, tiled=True)  21.1 us
    pallas_call x1, Pallas kernels, on_device(): pl.pallas_call(lambda *refs: solve_kernel(kappa, count, *refs), out_shape...  3.78 us
    pallas_call x1, Pallas kernels, on_device(): pl.pallas_call(pack_kernel, out_shape=jax.ShapeDtypeStruct((devices * SLO...  2.15 us
    pallas_call x1, Pallas kernels, on_device(): pl.pallas_call(unpack_kernel, out_shape=(shard, shard, jax.ShapeDtypeStru...  1.71 us

profile of v1, /device:TPU:1, one launch (start us, length us, event | category | flops | bytes accessed | tf_op | source)
XLA Modules:
  0.0 62.6 jit_solution(8673880597040133563)
XLA Ops:
  0.6 2.2 %pack.1 = f32[768,128]{1,0:T(8,128)} custom-call(f32[2,1,8,512]{3,2,1,0:T(8,128)} %resid_ref.1, f32[4,2,1,8,512]{4,3,2,1,0:T(8,128)} %basis_ref.1), custom_call_target="tpu_custom_call" | custom-call | tf_op jit(solution)/shard_map/pack/pallas_call | solution.py:203
  2.8 33.2 %all_to_all.16 = f32[256,1,384]{2,1,0:T(1,128)} all-to-all(f32[256,1,384]{2,1,0:T(1,128)} %bitcast.6), channel_id=1, replica_groups=mesh['tm'=128,'rows'=2] {'tm','rows'}, dimensions={0} | all-to-all | bytes 786432 | tf_op jit(solution)/shard_map/all_to_all | solution.py:209
  36.0 3.8 %solve.1 = f32[256,128]{1,0:T(8,128)} custom-call(f32[768,128]{1,0:T(8,128)} %bitcast.7, f32[128,512]{1,0:T(8,128)} %constant.4.clone.refs_1_, f32[256,256]{1,0:T(8,128)} %constant.5.clone.refs_2_), custom_call_target="tpu_custom_call" | custom-call | tf_op jit(solution)/shard_map/solve/pallas_call | solution.py:211
  39.8 21.1 %all_to_all.17 = f32[256,1,128]{2,1,0:T(1,128)} all-to-all(f32[256,1,128]{2,1,0:T(1,128)} %bitcast.9), channel_id=1, replica_groups=mesh['tm'=128,'rows'=2] {'tm','rows'}, dimensions={0} | all-to-all | bytes 262144 | tf_op jit(solution)/shard_map/all_to_all | solution.py:216
  60.9 1.7 %unpack.1 = (f32[2,1,8,512]{3,2,1,0:T(8,128)}, f32[2,1,8,512]{3,2,1,0:T(8,128)}, f32[5]{0:T(128)}) custom-call(f32[256,128]{1,0:T(8,128)} %bitcast.8), custom_call_target="tpu_custom_call" | custom-call | tf_op jit(solution)/shard_map/unpack/pallas_call | solution.py:219

commit v2 on v1

--- a/solution.py
+++ b/solution.py
@@ -195,6 +195,8 @@
     steps = mesh.shape["tm"]
     devices = steps * mesh.shape["rows"]
 
+    params = pltpu.CompilerParams(vmem_limit_bytes=12 * 2**20)
+
     def on_device(resid, basis):
         cols = resid.shape[3]
         count = 2.0 * steps * 2 * ROWS * cols
@@ -203,6 +205,7 @@
         send = pl.pallas_call(
             pack_kernel,
             out_shape=jax.ShapeDtypeStruct((devices * SLOTS, LANES), jnp.float32),
+            compiler_params=params,
             name="pack",
         )(resid, basis)
         send = send.reshape(devices, 1, SLOTS * LANES)
@@ -211,6 +214,7 @@
         back = pl.pallas_call(
             lambda *refs: solve_kernel(kappa, count, *refs),
             out_shape=jax.ShapeDtypeStruct((devices, LANES), jnp.float32),
+            compiler_params=params,
             name="solve",
         )(recv, time_table, jnp.asarray(space))
         home = lax.all_to_all(back, axes, 0, 0, tiled=True)
@@ -220,6 +224,7 @@
             unpack_kernel,
             out_shape=(shard, shard, jax.ShapeDtypeStruct((KRYLOV + 1,), jnp.float32)),
             out_specs=(vmem, vmem, pl.BlockSpec(memory_space=pltpu.SMEM)),
+            compiler_params=params,
             name="unpack",
         )(home)
         return precond, image, gram

time: 62.8 us -> 58 us (0.924)
  Pallas kernels: 7.64 us -> 3.27 us
  blocking collectives: 54.3 us -> 52.2 us
  local copies, waits for them, and re-layouts: 0 us -> 1.67 us
    all_to_all x1, blocking collectives: 21.1 us -> 19.3 us  [on_device(): home = lax.all_to_all(back, axes, 0, 0, tiled=True)]
    pallas_call x1, Pallas kernels: 3.78 us -> 1.99 us  [on_device(): pl.pallas_call(lambda *refs: solve_kernel(kappa, count, *refs), out_shape...]
    pallas_call x1, Pallas kernels: 2.15 us -> 0.47 us  [on_device(): pl.pallas_call(pack_kernel, out_shape=jax.ShapeDtypeStruct((devices * SLO...]
    unnamed x0 -> x8, local copies, waits for them, and re-layouts: none -> 1.67 us
    pallas_call x1, Pallas kernels: 1.71 us -> 0.8 us  [on_device(): pl.pallas_call(unpack_kernel, out_shape=(shard, shard, jax.ShapeDtypeStru...]
where the time goes in v2:
time: 58 us; the launch traced here: 57.8 us
  blocking collectives  52.2 us (90%)
  Pallas kernels  3.27 us (6%)
  local copies, waits for them, and re-layouts  1.67 us (3%)
  between operations  0.67 us (1%)
    all_to_all x1, blocking collectives, on_device(): recv = lax.all_to_all(send, axes, 0, 0, tiled=True)  32.9 us
    all_to_all x1, blocking collectives, on_device(): home = lax.all_to_all(back, axes, 0, 0, tiled=True)  19.3 us
    pallas_call x1, Pallas kernels, on_device(): pl.pallas_call(lambda *refs: solve_kernel(kappa, count, *refs), out_shape...  1.99 us
    unnamed x8, local copies, waits for them, and re-layouts  1.67 us

profile of v2, /device:TPU:1, one launch (start us, length us, event | category | flops | bytes accessed | tf_op | source)
XLA Modules:
  0.0 57.8 jit_solution(6714912121547006738)
XLA Ops:
  0.6 0.0 copy-start.2
  0.6 0.9 %copy-done.2 = f32[4,2,1,8,512]{4,3,2,1,0:T(8,128)S(1)} copy-done((f32[4,2,1,8,512]{4,3,2,1,0:T(8,128)S(1)}, f32[4,2,1,8,512]{4,3,2,1,0:T(8,128)}, u32[]{:S(2)}) %copy-start.2) | copy-done | bytes 131096
  1.5 0.0 copy-start.3
  1.5 0.8 %copy-done.3 = f32[2,1,8,512]{3,2,1,0:T(8,128)S(1)} copy-done((f32[2,1,8,512]{3,2,1,0:T(8,128)S(1)}, f32[2,1,8,512]{3,2,1,0:T(8,128)}, u32[]{:S(2)}) %copy-start.3) | copy-done | bytes 32792
  2.3 0.5 pack.1
  2.8 0.0 copy-start
  2.8 0.0 copy-start.1
  2.8 32.9 %all_to_all.16 = f32[256,1,384]{2,1,0:T(1,128)S(1)} all-to-all(f32[256,1,384]{2,1,0:T(1,128)S(1)} %bitcast.6), channel_id=1, replica_groups=mesh['tm'=128,'rows'=2] {'tm','rows'}, dimensions={0} | all-to-all | bytes 786432 | tf_op jit(solution)/shard_map/all_to_all | solution.py:212
  35.7 0.0 copy-done
  35.7 0.0 copy-done.1
  35.7 2.0 %solve.1 = f32[256,128]{1,0:T(8,128)S(1)} custom-call(f32[768,128]{1,0:T(8,128)S(1)} %bitcast.7, f32[128,512]{1,0:T(8,128)S(1)} %copy-done.1, f32[256,256]{1,0:T(8,128)S(1)} %copy-done), custom_call_target="tpu_custom_call" | custom-call | tf_op jit(solution)/shard_map/solve/pallas_call | solution.py:214
  37.7 19.3 %all_to_all.17 = f32[256,1,128]{2,1,0:T(1,128)S(1)} all-to-all(f32[256,1,128]{2,1,0:T(1,128)S(1)} %bitcast.9), channel_id=1, replica_groups=mesh['tm'=128,'rows'=2] {'tm','rows'}, dimensions={0} | all-to-all | bytes 262144 | tf_op jit(solution)/shard_map/all_to_all | solution.py:220
  57.0 0.8 %unpack.1 = (f32[2,1,8,512]{3,2,1,0:T(8,128)}, f32[2,1,8,512]{3,2,1,0:T(8,128)}, f32[5]{0:T(128)}) custom-call(f32[256,128]{1,0:T(8,128)S(1)} %bitcast.8), custom_call_target="tpu_custom_call" | custom-call | tf_op jit(solution)/shard_map/unpack/pallas_call | solution.py:223
Async XLA Ops:
  0.6 0.9 %copy-start.2 = (f32[4,2,1,8,512]{4,3,2,1,0:T(8,128)S(1)}, f32[4,2,1,8,512]{4,3,2,1,0:T(8,128)}, u32[]{:S(2)}) copy-start(f32[4,2,1,8,512]{4,3,2,1,0:T(8,128)} %basis_ref.1) | copy-start | bytes 393220
  1.5 0.8 %copy-start.3 = (f32[2,1,8,512]{3,2,1,0:T(8,128)S(1)}, f32[2,1,8,512]{3,2,1,0:T(8,128)}, u32[]{:S(2)}) copy-start(f32[2,1,8,512]{3,2,1,0:T(8,128)} %resid_ref.1) | copy-start | bytes 98308
  2.8 32.9 %copy-start = (f32[256,256]{1,0:T(8,128)S(1)}, f32[256,256]{1,0:T(8,128)}, u32[]{:S(2)}) copy-start(f32[256,256]{1,0:T(8,128)} %constant.5.clone.refs_2_) | copy-start | bytes 786436
  2.8 32.9 %copy-start.1 = (f32[128,512]{1,0:T(8,128)S(1)}, f32[128,512]{1,0:T(8,128)}, u32[]{:S(2)}) copy-start(f32[128,512]{1,0:T(8,128)} %constant.4.clone.refs_1_) | copy-start | bytes 786436

commit v3 on v2

v3 whole, which is shorter than its diff:
```python
import math

import jax
import jax.numpy as jnp
import numpy as np
from jax import lax
from jax.experimental import pallas as pl
from jax.experimental.pallas import tpu as pltpu
from jax.sharding import PartitionSpec as P

ALPHA = 0.01
SWEEPS = 4
KRYLOV = 4
LANES = 128
ROWS = 8
SLOTS = 2
FIELD = 2 * ROWS
OUT = 64


def roll(value, amount, axis):
    size = value.shape[axis]
    return pltpu.roll(value, amount % size, axis)


def time_tables(steps):
    kappa = 16.0 / (steps * steps)
    index = np.arange(steps)
    gamma = ALPHA ** (index / steps)
    lam = 1.0 - ALPHA ** (1.0 / steps) * np.exp(-2j * np.pi * index / steps)
    den = lam * lam + 4.0 * kappa
    turn = np.exp(-2j * np.pi * np.outer(index, index) / steps)
    tables = []
    for m in range(SWEEPS):
        inner = np.conj(turn) @ ((1.0 / den ** (m + 1))[:, None] * turn) / steps
        tables.append(kappa**m * (inner.real / gamma[:, None]) * gamma[None, :])
    return np.concatenate(tables, 1).astype(np.float32), kappa


def halves(value):
    high = value.astype(jnp.bfloat16)
    return high, (value - high.astype(jnp.float32)).astype(jnp.bfloat16)


def space_table():
    rows = 2 * ROWS
    shift = np.eye(rows, k=1) + np.eye(rows, k=-1)
    table = np.zeros((2, LANES, 2 * LANES))
    for m in range(SWEEPS + 1):
        for k in range(m + 1):
            part = math.comb(m, k) * np.linalg.matrix_power(shift, m - k)
            for row in range(rows):
                for out in range(rows):
                    h, at = divmod(out, ROWS)
                    lanes = [m * 4 * ROWS + h * 2 * ROWS + at]
                    if m == SWEEPS:
                        lanes = [LANES + (h * 8 + i) * ROWS + at for i in range(KRYLOV)]
                    for c in range(2):
                        source = (k * 2 + c) * ROWS + row % ROWS
                        table[row // ROWS, source, lanes] = part[row, out]
    return table.reshape(2 * LANES, 2 * LANES)


def lane_of(shape):
    return lax.broadcasted_iota(jnp.int32, shape, len(shape) - 1)


def powers_of(flat):
    cols = flat.shape[-1]
    lane = lane_of(flat.shape)
    powers = [flat]
    for _ in range(SWEEPS):
        last = powers[-1]
        right = jnp.where(lane == 0, 0.0, roll(last, 1, 1))
        left = jnp.where(lane == cols - 1, 0.0, roll(last, -1, 1))
        powers.append(right + left)
    return powers


def packed(powers, basis, lent, odd):
    half = powers[0].shape[-1] // 2
    fields = powers + [basis[i, 1] for i in range(KRYLOV)]
    fields += [jnp.where(odd, lent[i], basis[i, 0]) for i in range(2)]
    whole = jnp.concatenate(fields, 0)
    return [whole[:, dc * half : (dc + 1) * half].T for dc in range(2)]


def own_products(flat, basis):
    sums = []
    for i in range(KRYLOV):
        both = basis[i, 0] * flat[:ROWS] + basis[i, 1] * flat[ROWS:]
        sums.append(sum(both[:, at : at + LANES] for at in range(0, both.shape[1], LANES)))
    return jnp.concatenate(sums, 0)


def delayed(value):
    row = lax.broadcasted_iota(jnp.int32, value.shape, 0)
    moved = roll(value, 1, 0)
    return jnp.where(row == 0, ALPHA * moved, moved)


def dot(left, right):
    return jnp.dot(left, right, preferred_element_type=jnp.float32)


def spread_over(value, group):
    size = group
    while size < LANES:
        value = value + roll(value, size, 1)
        size *= 2
    return value


def solved(parts, own, time_high, time_low, space, kappa, count):
    steps = parts[0][0].shape[0]
    shape = (steps, LANES)
    lane = lane_of(shape)
    row = lax.broadcasted_iota(jnp.int32, shape, 0)
    is_disp = (lane & ROWS) == 0
    mixed = []
    for dc in range(2):
        sides = []
        for h in range(2):
            x = parts[h][dc]
            sides.append(jnp.where(is_disp, x - delayed(x), x))
        mixed.append(jnp.concatenate(sides, 1))
    mixed = jnp.concatenate(mixed, 0)
    high, low = halves(mixed)
    rest = (mixed - high.astype(jnp.float32) - low.astype(jnp.float32)).astype(jnp.bfloat16)
    spread = dot(high, space) + dot(low, space) + dot(rest, space)
    group = 4 * ROWS
    early = spread[:steps, :LANES] + roll(spread[steps:, :LANES], ROWS, 1)
    last = spread[:steps, LANES:] + roll(spread[steps:, LANES:], group, 1)
    stack = [jnp.where(lane // group == m, early, 0.0) for m in range(SWEEPS)]
    high, low = halves(jnp.concatenate(stack, 0))
    disp = dot(time_high, high) + (dot(time_high, low) + dot(time_low, high))
    disp = disp + roll(disp, 2 * group, 1)
    disp = disp + roll(disp, group, 1)
    high, low = halves(last)
    cut_high = time_high[:, (SWEEPS - 1) * steps :]
    cut_low = time_low[:, (SWEEPS - 1) * steps :]
    gone = dot(cut_high, high) + (dot(cut_high, low) + dot(cut_low, high))
    gone = gone * -kappa
    late = delayed(disp)
    rate = disp - late
    edge = jnp.where(row == 0, late, 0.0)
    place = (lane - OUT) // FIELD
    outs, square = [], 0.0
    for h in range(2):
        flip = lambda v, slot: roll(v, FIELD, 1) if (slot + h) % 2 else v
        add = jnp.where(place == 0, flip(disp, 0), 0.0)
        add = jnp.where(place == 1, flip(rate, 1), add)
        add = jnp.where(place == 2, flip(edge, 2), add)
        first_lane = h * 8 * ROWS + 3 * ROWS
        add = jnp.where(place == 3, roll(gone, OUT + 3 * FIELD - first_lane, 1), add)
        for dc in range(2):
            x = parts[h][dc]
            spot = (lane - OUT) // ROWS - dc
            base = OUT + dc * ROWS
            add = add - jnp.where(spot == 2, roll(x, base + FIELD, 1), 0.0)
            add = add + jnp.where(spot == 4, roll(x, base + 2 * FIELD, 1), 0.0)
            add = add + jnp.where(spot == 6, roll(x, base + 3 * FIELD - ROWS, 1), 0.0)
        wrap = jnp.where((row == 0) & (place == 3), delayed(roll(add, 2 * FIELD, 1)), 0.0)
        out = add + wrap
        outs.append(out)
        square = square + jnp.sum(jnp.where(place >= 2, out * out, 0.0), 0, keepdims=True)
    start = 10 * ROWS
    line = lane_of((1, LANES))
    where_basis = jnp.zeros(shape, jnp.float32)
    gram = jnp.zeros((1, LANES), jnp.float32)
    for h in range(2):
        ending = ALPHA * outs[h][steps - 1 :]
        for dc in range(2):
            x = parts[h][dc]
            at = (2 * h + dc) * group
            where_basis = jnp.where(lane // group == 2 * h + dc, roll(x, at - start, 1), where_basis)
            spot = (line - OUT) // ROWS - dc
            disp_row = spread_over(jnp.where(spot == 0, ending, 0.0), ROWS)
            rate_row = spread_over(jnp.where(spot == 2, ending, 0.0), ROWS)
            gram = gram + jnp.where(line < group, roll(x[:1] * rate_row, -start, 1), 0.0)
            gram = gram + jnp.where(line < FIELD, roll(x[:1] * disp_row, FIELD, 1), 0.0)
            second = (line >= FIELD) & (line < 2 * FIELD)
            gram = gram + jnp.where(second, roll(x[1:2] * disp_row, 2 * FIELD, 1), 0.0)
    product = jnp.sum(where_basis * gone, 0, keepdims=True)
    product = product + roll(product, 2 * group, 1)
    product = product + roll(product, group, 1)
    gram = gram + jnp.where(line < group, product, 0.0)
    for i in range(KRYLOV):
        total = jnp.sum(jnp.sum(own[i * ROWS : (i + 1) * ROWS], 0, keepdims=True), 1, keepdims=True)
        gram = gram + jnp.where(line == i * ROWS, total, 0.0)
    square = square + roll(square, FIELD, 1)
    square = square + roll(square, ROWS, 1)
    square = roll(square, group - (OUT + 3 * FIELD + ROWS), 1) * (1.0 / count)
    gram = jnp.where(line // ROWS == KRYLOV, square, gram)
    return [jnp.where(lane < OUT, jnp.broadcast_to(gram, shape), out) for out in outs]


def gram_of(totals):
    line = lane_of(totals.shape)
    return [jnp.sum(jnp.where(line // ROWS == i, totals, 0.0)) for i in range(KRYLOV + 1)]


def pack_kernel(resid_hbm, basis_hbm, lent_ref, send_ref, own_ref, resid_ref, basis_ref, sems):
    copies = [
        pltpu.make_async_copy(resid_hbm, resid_ref, sems.at[0]),
        pltpu.make_async_copy(basis_hbm, basis_ref, sems.at[1]),
    ]
    for copy in copies:
        copy.start()
    odd = lax.axis_index("tm") % 2 == 1
    copies[0].wait()
    flat = resid_ref[...].reshape(2 * ROWS, resid_ref.shape[-1])
    powers = powers_of(flat)
    copies[1].wait()
    basis = basis_ref[:, :, 0]
    for slot, slab in enumerate(packed(powers, basis, lent_ref[:, 0], odd)):
        send_ref[pl.ds(slot, slab.shape[0], stride=SLOTS), :] = slab
    own_ref[...] = own_products(flat, basis)


def solve_kernel(kappa, count, recv_ref, own_ref, high_ref, low_ref, space_ref, send_ref):
    steps = high_ref.shape[0]
    parts = [
        [recv_ref[pl.ds(h * SLOTS + s, steps, stride=2 * SLOTS), :] for s in range(SLOTS)]
        for h in range(2)
    ]
    tables = [own_ref[...], high_ref[...], low_ref[...], space_ref[...]]
    outs = solved(parts, *tables, kappa, count)
    for h, out in enumerate(outs):
        send_ref[pl.ds(h, steps, stride=2), :] = out


def unpack_kernel(recv_ref, precond_ref, image_ref, gram_ref):
    received = recv_ref[...]
    half = received.shape[0]
    turned = received.T
    for slot, (ref, c) in enumerate(
        ((precond_ref, 0), (precond_ref, 1), (image_ref, 0), (image_ref, 1))
    ):
        for dc in range(2):
            start = OUT + slot * FIELD + dc * ROWS
            ref[c, 0, :, dc * half : (dc + 1) * half] = turned[start : start + ROWS]
    for i, value in enumerate(gram_of(jnp.sum(received, 0, keepdims=True))):
        gram_ref[i] = value


def solution(mesh):
    axes = ("tm", "rows")
    steps = mesh.shape["tm"]
    devices = steps * mesh.shape["rows"]

    params = pltpu.CompilerParams(vmem_limit_bytes=12 * 2**20)

    def on_device(resid, basis):
        cols = resid.shape[3]
        count = 2.0 * steps * 2 * ROWS * cols
        table, kappa = time_tables(steps)
        time_high = jnp.asarray(table.astype(jnp.bfloat16))
        time_low = jnp.asarray((table - table.astype(jnp.bfloat16)).astype(jnp.bfloat16))
        space = jnp.asarray(space_table().astype(jnp.bfloat16))
        pairs = [(j, j + 1) for j in range(0, steps, 2)]
        lent = lax.ppermute(basis[2:, 0], "tm", pairs)
        vmem = pl.BlockSpec(memory_space=pltpu.VMEM)
        hbm = pl.BlockSpec(memory_space=pltpu.HBM)
        send, own = pl.pallas_call(
            pack_kernel,
            in_specs=[hbm, hbm, vmem],
            out_shape=(
                jax.ShapeDtypeStruct((devices * SLOTS, LANES), jnp.float32),
                jax.ShapeDtypeStruct((KRYLOV * ROWS, LANES), jnp.float32),
            ),
            scratch_shapes=[
                pltpu.VMEM((2, 1, ROWS, cols), jnp.float32),
                pltpu.VMEM((KRYLOV, 2, 1, ROWS, cols), jnp.float32),
                pltpu.SemaphoreType.DMA((2,)),
            ],
            compiler_params=params,
            name="pack",
        )(*(pltpu.with_memory_space_constraint(a, pltpu.HBM) for a in (resid, basis)), lent)
        send = send.reshape(devices, 1, SLOTS * LANES)
        recv = lax.all_to_all(send, axes, 0, 0, tiled=True)
        recv = recv.reshape(devices * SLOTS, LANES)
        back = pl.pallas_call(
            lambda *refs: solve_kernel(kappa, count, *refs),
            out_shape=jax.ShapeDtypeStruct((devices, LANES), jnp.float32),
            compiler_params=params,
            name="solve",
        )(recv, own, time_high, time_low, space)
        home = lax.all_to_all(back, axes, 0, 0, tiled=True)
        shard = jax.ShapeDtypeStruct(resid.shape, jnp.float32)
        precond, image, gram = pl.pallas_call(
            unpack_kernel,
            out_shape=(shard, shard, jax.ShapeDtypeStruct((KRYLOV + 1,), jnp.float32)),
            out_specs=(vmem, vmem, pl.BlockSpec(memory_space=pltpu.SMEM)),
            compiler_params=params,
            name="unpack",
        )(home)
        return precond, image, gram

    return jax.shard_map(
        on_device,
        mesh=mesh,
        in_specs=(P(None, "tm", "rows", None), P(None, None, "tm", "rows", None)),
        out_specs=(P(None, "tm", "rows", None), P(None, "tm", "rows", None), P()),
        check_vma=False,
    )
```

time: 58 us -> 57.2 us (0.986)
  blocking collectives: 52.2 us -> 46.9 us
  waiting for transfers between devices: 0 us -> 3.88 us
  starting transfers between devices: 0 us -> 1.28 us
  local copies, waits for them, and re-layouts: 1.67 us -> 0.78 us
    all_to_all x1, blocking collectives: 32.9 us -> 28 us  [on_device(): recv = lax.all_to_all(send, axes, 0, 0, tiled=True)]
    ppermute x0 -> x1, waiting for transfers between devices: none -> 3.88 us  [on_device(): lent = lax.ppermute(basis[2:, 0], 'tm', pairs)]
    unnamed x8 -> x6, local copies, waits for them, and re-layouts: 1.67 us -> 0.02 us
    ppermute x0 -> x1, starting transfers between devices: none -> 1.28 us  [on_device(): lent = lax.ppermute(basis[2:, 0], 'tm', pairs)]
    pallas_call x1, Pallas kernels: 0.47 us -> 1.24 us  [on_device(): pl.pallas_call(pack_kernel, in_specs=[hbm, hbm, vmem], out_shape=(jax.Sha...]
    squeeze x0 -> x1, local copies, waits for them, and re-layouts: none -> 0.76 us  [on_device(): lent = lax.ppermute(basis[2:, 0], 'tm', pairs)]
  transfers between devices with their start and end apart: 0 -> 1, of which waited for: 0 -> 1; matrix products, arithmetic and copies ran while one was open for 0% -> 0% of each run, Pallas kernels for 0% -> 0%
where the time goes in v3:
time: 57.2 us; the launch traced here: 57 us
  blocking collectives  46.9 us (82%)
  waiting for transfers between devices  3.88 us (7%)
  Pallas kernels  3.48 us (6%)
  starting transfers between devices  1.28 us (2%)
  local copies, waits for them, and re-layouts  0.78 us (1%)
  between operations  0.68 us (1%)
    all_to_all x1, blocking collectives, on_device(): recv = lax.all_to_all(send, axes, 0, 0, tiled=True)  28 us
    all_to_all x1, blocking collectives, on_device(): home = lax.all_to_all(back, axes, 0, 0, tiled=True)  18.9 us
    ppermute x1, waiting for transfers between devices, on_device(): lent = lax.ppermute(basis[2:, 0], 'tm', pairs)  3.88 us
    pallas_call x1, Pallas kernels, on_device(): pl.pallas_call(lambda *refs: solve_kernel(kappa, count, *refs), out_shape...  1.44 us
    ppermute x1, starting transfers between devices, on_device(): lent = lax.ppermute(basis[2:, 0], 'tm', pairs)  1.28 us
    pallas_call x1, Pallas kernels, on_device(): pl.pallas_call(pack_kernel, in_specs=[hbm, hbm, vmem], out_shape=(jax.Sha...  1.24 us
  transfers between devices with their start and end apart: 1, of which 1 were waited for; matrix products, arithmetic and copies ran while one was open for 0% of the time, Pallas kernels for 0%

profile of v3, /device:TPU:1, one launch (start us, length us, event | category | flops | bytes accessed | tf_op | source)
XLA Modules:
  0.0 57.0 jit_solution(5064801997236733284)
XLA Ops:
  0.6 0.8 %slice_bitcast_fusion = f32[2,1,8,512]{3,2,1,0:T(8,128)S(1)} fusion(f32[4,2,1,8,512]{4,3,2,1,0:T(8,128)} %basis_hbm.1), kind=kLoop, calls=%fused_computation | loop fusion | bytes 65536 | tf_op jit(solution)/shard_map/squeeze | solution.py:262
  1.4 1.3 %collective-permute-start = (f32[2,1,8,512]{3,2,1,0:T(8,128)S(1)}, f32[2,1,8,512]{3,2,1,0:T(8,128)S(1)}, u32[]{:S(2)}, u32[]{:S(2)}) collective-permute-start(f32[2,1,8,512]{3,2,1,0:T(8,128)S(1)} %slice_bitcast_fusion), channel_id=1, source_target_pairs={{0,2},{4,6},{8,10},{12,14},{16,18},{20,22},{24,26},{28,30},{32,34}... | collective-permute-start | bytes 98312 | tf_op jit(solution)/shard_map/ppermute | solution.py:262
  2.7 3.9 %collective-permute-done.lent_ref = f32[2,1,8,512]{3,2,1,0:T(8,128)S(1)} collective-permute-done((f32[2,1,8,512]{3,2,1,0:T(8,128)S(1)}, f32[2,1,8,512]{3,2,1,0:T(8,128)S(1)}, u32[]{:S(2)}, u32[]{:S(2)}) %collective-permute-start) | collective-permute-done | bytes 32800 | tf_op jit(solution)/shard_map/ppermute | solution.py:262
  6.6 1.2 %pack.1 = (f32[512,128]{1,0:T(8,128)S(1)}, f32[32,128]{1,0:T(8,128)S(1)}) custom-call(f32[2,1,8,512]{3,2,1,0:T(8,128)} %resid_hbm.1, f32[4,2,1,8,512]{4,3,2,1,0:T(8,128)} %basis_hbm.1, f32[2,1,8,512]{3,2,1,0:T(8,128)S(1)} %collective-permute-done.lent_ref), custom_call_target="tpu_custom_call" | custom-call | tf_op jit(solution)/shard_map/pack/pallas_call | solution.py:265
  7.8 0.0 copy-start
  7.8 0.0 copy-start.1
  7.8 0.0 copy-start.2
  7.8 28.0 %all_to_all.16 = f32[256,1,256]{2,1,0:T(1,128)S(1)} all-to-all(f32[256,1,256]{2,1,0:T(1,128)S(1)} %bitcast.13), channel_id=1, replica_groups=mesh['tm'=128,'rows'=2] {'tm','rows'}, dimensions={0} | all-to-all | bytes 524288 | tf_op jit(solution)/shard_map/all_to_all | solution.py:281
  35.9 0.0 copy-done
  35.9 0.0 copy-done.1
  35.9 0.0 copy-done.2
  35.9 1.4 %solve.1 = f32[256,128]{1,0:T(8,128)S(1)} custom-call(f32[512,128]{1,0:T(8,128)S(1)} %bitcast.10, f32[32,128]{1,0:T(8,128)S(1)} %get-tuple-element.6.refs_1_, bf16[128,512]{1,0:T(8,128)(2,1)S(1)} %copy-done.2, bf16[128,512]{1,0:T(8,128)(2,1)S(1)} %copy-done.1, bf16[256,256]{1,0:T(8,128)(2,1)S(1)} %copy-done), custom_call_target="tpu_custom_call" | custom-call | tf_op jit(solution)/shard_map/solve/pallas_call | solution.py:283
  37.3 18.9 %all_to_all.17 = f32[256,1,128]{2,1,0:T(1,128)S(1)} all-to-all(f32[256,1,128]{2,1,0:T(1,128)S(1)} %bitcast.11), channel_id=1, replica_groups=mesh['tm'=128,'rows'=2] {'tm','rows'}, dimensions={0} | all-to-all | bytes 262144 | tf_op jit(solution)/shard_map/all_to_all | solution.py:289
  56.2 0.8 %unpack.1 = (f32[2,1,8,512]{3,2,1,0:T(8,128)}, f32[2,1,8,512]{3,2,1,0:T(8,128)}, f32[5]{0:T(128)}) custom-call(f32[256,128]{1,0:T(8,128)S(1)} %bitcast.12), custom_call_target="tpu_custom_call" | custom-call | tf_op jit(solution)/shard_map/unpack/pallas_call | solution.py:291
Async XLA Ops:
  1.4 5.2 %collective-permute-start = (f32[2,1,8,512]{3,2,1,0:T(8,128)S(1)}, f32[2,1,8,512]{3,2,1,0:T(8,128)S(1)}, u32[]{:S(2)}, u32[]{:S(2)}) collective-permute-start(f32[2,1,8,512]{3,2,1,0:T(8,128)S(1)} %slice_bitcast_fusion), channel_id=1, source_target_pairs={{0,2},{4,6},{8,10},{12,14},{16,18},{20,22},{24,26},{28,30},{32,34}... | collective-permute-start | bytes 98312 | tf_op jit(solution)/shard_map/ppermute | solution.py:262
  7.8 28.1 %copy-start = (bf16[256,256]{1,0:T(8,128)(2,1)S(1)}, bf16[256,256]{1,0:T(8,128)(2,1)}, u32[]{:S(2)}) copy-start(bf16[256,256]{1,0:T(8,128)(2,1)} %constant.8.clone.refs_4_) | copy-start | bytes 393220
  7.8 28.1 %copy-start.1 = (bf16[128,512]{1,0:T(8,128)(2,1)S(1)}, bf16[128,512]{1,0:T(8,128)(2,1)}, u32[]{:S(2)}) copy-start(bf16[128,512]{1,0:T(8,128)(2,1)} %constant.7.clone.refs_3_) | copy-start | bytes 393220
  7.8 28.0 %copy-start.2 = (bf16[128,512]{1,0:T(8,128)(2,1)S(1)}, bf16[128,512]{1,0:T(8,128)(2,1)}, u32[]{:S(2)}) copy-start(bf16[128,512]{1,0:T(8,128)(2,1)} %constant.6.clone.refs_2_) | copy-start | bytes 393220

commit v4 on v3

--- a/solution.py
+++ b/solution.py
@@ -207,13 +207,13 @@
     ]
     for copy in copies:
         copy.start()
-    odd = lax.axis_index("tm") % 2 == 1
+    odd = lax.axis_index("tm") == 1
     copies[0].wait()
     flat = resid_ref[...].reshape(2 * ROWS, resid_ref.shape[-1])
     powers = powers_of(flat)
     copies[1].wait()
     basis = basis_ref[:, :, 0]
-    for slot, slab in enumerate(packed(powers, basis, lent_ref[:, 0], odd)):
+    for slot, slab in enumerate(packed(powers, basis, lent_ref[2:, 0, 0], odd)):
         send_ref[pl.ds(slot, slab.shape[0], stride=SLOTS), :] = slab
     own_ref[...] = own_products(flat, basis)
 
@@ -258,8 +258,7 @@
         time_high = jnp.asarray(table.astype(jnp.bfloat16))
         time_low = jnp.asarray((table - table.astype(jnp.bfloat16)).astype(jnp.bfloat16))
         space = jnp.asarray(space_table().astype(jnp.bfloat16))
-        pairs = [(j, j + 1) for j in range(0, steps, 2)]
-        lent = lax.ppermute(basis[2:, 0], "tm", pairs)
+        lent = lax.ppermute(basis, "tm", [(0, 1)])
         vmem = pl.BlockSpec(memory_space=pltpu.VMEM)
         hbm = pl.BlockSpec(memory_space=pltpu.HBM)
         send, own = pl.pallas_call(

time: 57.2 us -> 54.5 us (0.953)
  blocking collectives: 46.9 us -> 44.6 us
  local copies, waits for them, and re-layouts: 0.78 us -> 0.02 us
    all_to_all x1, blocking collectives: 28 us -> 25.8 us  [on_device(): recv = lax.all_to_all(send, axes, 0, 0, tiled=True)]
    squeeze x1 -> x0, local copies, waits for them, and re-layouts: 0.76 us -> none  [on_device(): lent = lax.ppermute(basis[2:, 0], 'tm', pairs)]
where the time goes in v4:
time: 54.5 us; the launch traced here: 54.3 us
  blocking collectives  44.6 us (82%)
  waiting for transfers between devices  4.23 us (8%)
  Pallas kernels  3.48 us (6%)
  starting transfers between devices  1.29 us (2%)
  between operations  0.68 us (1%)
    all_to_all x1, blocking collectives, on_device(): recv = lax.all_to_all(send, axes, 0, 0, tiled=True)  25.8 us
    all_to_all x1, blocking collectives, on_device(): home = lax.all_to_all(back, axes, 0, 0, tiled=True)  18.9 us
    ppermute x1, waiting for transfers between devices, on_device(): lent = lax.ppermute(basis, 'tm', [(0, 1)])  4.23 us
    pallas_call x1, Pallas kernels, on_device(): pl.pallas_call(lambda *refs: solve_kernel(kappa, count, *refs), out_shape...  1.44 us
    ppermute x1, starting transfers between devices, on_device(): lent = lax.ppermute(basis, 'tm', [(0, 1)])  1.29 us
    pallas_call x1, Pallas kernels, on_device(): pl.pallas_call(pack_kernel, in_specs=[hbm, hbm, vmem], out_shape=(jax.Sha...  1.24 us
  transfers between devices with their start and end apart: 1, of which 1 were waited for; matrix products, arithmetic and copies ran while one was open for 0% of the time, Pallas kernels for 0%

profile of v4, /device:TPU:1, one launch (start us, length us, event | category | flops | bytes accessed | tf_op | source)
XLA Modules:
  0.0 54.3 jit_solution(7465087790187524215)
XLA Ops:
  0.6 1.3 %collective-permute-start = (f32[4,2,1,8,512]{4,3,2,1,0:T(8,128)}, f32[4,2,1,8,512]{4,3,2,1,0:T(8,128)S(1)}, u32[]{:S(2)}, u32[]{:S(2)}) collective-permute-start(f32[4,2,1,8,512]{4,3,2,1,0:T(8,128)} %basis_hbm.1), channel_id=1, source_target_pairs={{0,2},{1,3}} | collective-permute-start | bytes 393224 | tf_op jit(solution)/shard_map/ppermute | solution.py:261
  1.9 4.2 %collective-permute-done.lent_ref = f32[4,2,1,8,512]{4,3,2,1,0:T(8,128)S(1)} collective-permute-done((f32[4,2,1,8,512]{4,3,2,1,0:T(8,128)}, f32[4,2,1,8,512]{4,3,2,1,0:T(8,128)S(1)}, u32[]{:S(2)}, u32[]{:S(2)}) %collective-permute-start) | collective-permute-done | bytes 131104 | tf_op jit(solution)/shard_map/ppermute | solution.py:261
  6.2 1.2 %pack.1 = (f32[512,128]{1,0:T(8,128)S(1)}, f32[32,128]{1,0:T(8,128)S(1)}) custom-call(f32[2,1,8,512]{3,2,1,0:T(8,128)} %resid_hbm.1, f32[4,2,1,8,512]{4,3,2,1,0:T(8,128)} %basis_hbm.1, f32[4,2,1,8,512]{4,3,2,1,0:T(8,128)S(1)} %collective-permute-done.lent_ref), custom_call_target="tpu_custom_call" | custom-call | tf_op jit(solution)/shard_map/pack/pallas_call | solution.py:264
  7.4 0.0 copy-start
  7.4 0.0 copy-start.1
  7.4 0.0 copy-start.2
  7.4 25.8 %all_to_all.16 = f32[256,1,256]{2,1,0:T(1,128)S(1)} all-to-all(f32[256,1,256]{2,1,0:T(1,128)S(1)} %bitcast.9), channel_id=1, replica_groups=mesh['tm'=128,'rows'=2] {'tm','rows'}, dimensions={0} | all-to-all | bytes 524288 | tf_op jit(solution)/shard_map/all_to_all | solution.py:280
  33.2 0.0 copy-done
  33.2 0.0 copy-done.1
  33.2 0.0 copy-done.2
  33.2 1.4 %solve.1 = f32[256,128]{1,0:T(8,128)S(1)} custom-call(f32[512,128]{1,0:T(8,128)S(1)} %bitcast.6, f32[32,128]{1,0:T(8,128)S(1)} %get-tuple-element.6.refs_1_, bf16[128,512]{1,0:T(8,128)(2,1)S(1)} %copy-done.2, bf16[128,512]{1,0:T(8,128)(2,1)S(1)} %copy-done.1, bf16[256,256]{1,0:T(8,128)(2,1)S(1)} %copy-done), custom_call_target="tpu_custom_call" | custom-call | tf_op jit(solution)/shard_map/solve/pallas_call | solution.py:282
  34.7 18.9 %all_to_all.17 = f32[256,1,128]{2,1,0:T(1,128)S(1)} all-to-all(f32[256,1,128]{2,1,0:T(1,128)S(1)} %bitcast.7), channel_id=1, replica_groups=mesh['tm'=128,'rows'=2] {'tm','rows'}, dimensions={0} | all-to-all | bytes 262144 | tf_op jit(solution)/shard_map/all_to_all | solution.py:288
  53.5 0.8 %unpack.1 = (f32[2,1,8,512]{3,2,1,0:T(8,128)}, f32[2,1,8,512]{3,2,1,0:T(8,128)}, f32[5]{0:T(128)}) custom-call(f32[256,128]{1,0:T(8,128)S(1)} %bitcast.8), custom_call_target="tpu_custom_call" | custom-call | tf_op jit(solution)/shard_map/unpack/pallas_call | solution.py:290
Async XLA Ops:
  0.6 5.5 %collective-permute-start = (f32[4,2,1,8,512]{4,3,2,1,0:T(8,128)}, f32[4,2,1,8,512]{4,3,2,1,0:T(8,128)S(1)}, u32[]{:S(2)}, u32[]{:S(2)}) collective-permute-start(f32[4,2,1,8,512]{4,3,2,1,0:T(8,128)} %basis_hbm.1), channel_id=1, source_target_pairs={{0,2},{1,3}} | collective-permute-start | bytes 393224 | tf_op jit(solution)/shard_map/ppermute | solution.py:261
  7.4 25.8 %copy-start = (bf16[256,256]{1,0:T(8,128)(2,1)S(1)}, bf16[256,256]{1,0:T(8,128)(2,1)}, u32[]{:S(2)}) copy-start(bf16[256,256]{1,0:T(8,128)(2,1)} %constant.8.clone.refs_4_) | copy-start | bytes 393220
  7.4 25.8 %copy-start.1 = (bf16[128,512]{1,0:T(8,128)(2,1)S(1)}, bf16[128,512]{1,0:T(8,128)(2,1)}, u32[]{:S(2)}) copy-start(bf16[128,512]{1,0:T(8,128)(2,1)} %constant.7.clone.refs_3_) | copy-start | bytes 393220
  7.4 25.8 %copy-start.2 = (bf16[128,512]{1,0:T(8,128)(2,1)S(1)}, bf16[128,512]{1,0:T(8,128)(2,1)}, u32[]{:S(2)}) copy-start(bf16[128,512]{1,0:T(8,128)(2,1)} %constant.6.clone.refs_2_) | copy-start | bytes 393220

commit v5 on v2

v5 whole, which is shorter than its diff:
```python
import jax
import jax.numpy as jnp
import numpy as np
from jax import lax
from jax.experimental import pallas as pl
from jax.experimental.pallas import tpu as pltpu
from jax.sharding import PartitionSpec as P

ALPHA = 0.01
SWEEPS = 4
KRYLOV = 4
LANES = 128
ROWS = 8
SIDE = LANES // 2
MODES = 2 * ROWS
GROUP = 2 * MODES


def roll(value, amount, axis):
    size = value.shape[axis]
    return pltpu.roll(value, amount % size, axis)


def reversed_lanes(value):
    parts = [value[:, at : at + LANES] for at in range(0, value.shape[1], LANES)]
    index = LANES - 1 - lane_of(parts[0].shape)
    taken = [jnp.take_along_axis(p, index, axis=1, mode="promise_in_bounds") for p in parts]
    return jnp.concatenate(taken[::-1], 1)


def lane_of(shape):
    return lax.broadcasted_iota(jnp.int32, shape, len(shape) - 1)


def row_of(shape):
    return lax.broadcasted_iota(jnp.int32, shape, 0)


def sines(number, place, length):
    turn = np.outer(number, place + 1.0) / (length + 1)
    return np.sqrt(2.0 / (length + 1)) * np.sin(np.pi * turn)


def coupling(steps):
    return 16.0 / (steps * steps)


def time_table(steps):
    kappa = coupling(steps)
    index = np.arange(steps)
    gamma = ALPHA ** (index / steps)
    lam = 1.0 - ALPHA ** (1.0 / steps) * np.exp(-2j * np.pi * index / steps)
    den = lam * lam + 4.0 * kappa
    turn = np.exp(-2j * np.pi * np.outer(index, index) / steps)
    tables = []
    for m in range(SWEEPS):
        inner = np.conj(turn) @ ((1.0 / den ** (m + 1))[:, None] * turn) / steps
        tables.append(kappa**m * (inner.real / gamma[:, None]) * gamma[None, :])
    return np.concatenate(tables, 1)


def column_numbers(cols):
    return [2.0 * np.arange(cols // 2) + 1 + dc for dc in range(2)]


def column_tables(cols):
    return np.stack([sines(n, np.arange(cols // 2), cols) for n in column_numbers(cols)])


def symbol_table(cols):
    rows = 2.0 * np.cos(np.pi * (np.arange(MODES) + 1) / (MODES + 1))
    sums = []
    for number in column_numbers(cols):
        sums.append(2.0 * np.cos(np.pi * number / (cols + 1))[:, None] + rows[None, :])
    return np.tile(np.concatenate(sums, 1), (1, LANES // GROUP)).astype(np.float32)


def row_tables():
    wave = sines(np.arange(MODES) + 1, np.arange(MODES), MODES)
    enter = np.zeros((2, LANES, LANES))
    leave = np.zeros((LANES, 2, 2, LANES))
    for h in range(2):
        for row in range(ROWS):
            for dc in range(2):
                value = wave[:, h * ROWS + row]
                modes = dc * MODES + np.arange(MODES)
                for group in range(0, LANES, GROUP):
                    for c in range(2):
                        enter[h, dc * SIDE + c * ROWS + row, group + modes] = value
                for field, group in enumerate((0, 2, 1, 3)):
                    leave[group * GROUP + modes, 0, h, dc * SIDE + field * ROWS + row] = value
                for slot in range(1, 2 + KRYLOV):
                    leave[GROUP + modes, 1, h, dc * SIDE + slot * ROWS + row] = value
    return enter.reshape(2 * LANES, LANES), leave.reshape(LANES, 4 * LANES)


def halves(value):
    high = value.astype(jnp.bfloat16)
    return high, (value - high.astype(jnp.float32)).astype(jnp.bfloat16)


def both_halves(table):
    high = table.astype(jnp.bfloat16)
    return jnp.asarray(np.stack([high, (table - high.astype(np.float64)).astype(jnp.bfloat16)]))


def product(left, right, contract=((1,), (0,))):
    total = 0.0
    for i, j in ((1, 0), (0, 1), (0, 0)):
        total = total + lax.dot_general(
            left[i], right[j], (contract, ((), ())), preferred_element_type=jnp.float32
        )
    return total


def packed(flat, basis, lent, second, tables):
    half = flat.shape[1] // 2
    fields = [flat] + [basis[i, 1] for i in range(KRYLOV)]
    fields += [jnp.where(second, lent[i], basis[i, 0]) for i in range(2)]
    whole = jnp.concatenate(fields, 0)
    left, right = whole[:, :half], reversed_lanes(whole[:, half:])
    sides = []
    for dc, folded in enumerate((left + right, left - right)):
        table = (tables[0, dc], tables[1, dc])
        sides.append(product(table, halves(folded), ((1,), (1,))))
    return jnp.concatenate(sides, 1)


def own_products(flat, basis):
    disp, velo = flat[:ROWS], flat[ROWS:]
    terms = [basis[i, 0] * disp + basis[i, 1] * velo for i in range(KRYLOV)]
    terms.append(disp * disp + velo * velo)
    sums = [sum(t[:, at : at + LANES] for at in range(0, t.shape[1], LANES)) for t in terms]
    return jnp.concatenate(sums, 0)


def delayed(value):
    moved = roll(value, 1, 0)
    return jnp.where(row_of(value.shape) == 0, ALPHA * moved, moved)


def solved(parts, own, symbol, time, enter, leave, kappa, count):
    steps = parts[0].shape[0]
    shape = (steps, LANES)
    lane, row = lane_of(shape), row_of(shape)
    is_disp = lane % SIDE < ROWS
    mixed = [jnp.where(is_disp, x - delayed(x), x) for x in parts]
    source = product(halves(jnp.concatenate(mixed, 1)), enter)
    line = lane_of((1, LANES))
    cut = line // GROUP == 1
    power, weights = jnp.ones((1, LANES), jnp.float32), []
    for m in range(SWEEPS):
        last = -kappa * power * symbol if m == SWEEPS - 1 else 0.0
        weights.append(jnp.where(cut, last, power))
        power = power * symbol
    stack = jnp.concatenate([source * weight for weight in weights], 0)
    found = product(time, halves(stack))
    late = delayed(found)
    group = lane // GROUP
    found = jnp.where(group == 2, found - late, found)
    found = jnp.where(group == 3, jnp.where(row == 0, late, 0.0), found)
    spread = product(halves(found), leave)
    at = line % SIDE
    slot = at // ROWS
    outs, gram, square = [], 0.0, 0.0
    for h, x in enumerate(parts):
        out = spread[:, h * LANES : (h + 1) * LANES]
        gone = spread[:, (2 + h) * LANES : (3 + h) * LANES]
        ended = roll(out[steps - 1 :], ROWS, 1) - roll(x[steps - 1 :], 2 * ROWS, 1)
        rate = jnp.where(slot == 2, ALPHA * ended, 0.0)
        outs.append(jnp.where((row == 0) & (slot == 2), out + rate, out))
        disp = jnp.where(slot == 3, out[:1], 0.0)
        inner = jnp.sum(jnp.where(slot[:1] >= 2, x * gone, gone * (2.0 * x + gone)), 0, keepdims=True)
        wide = rate + roll(rate, ROWS, 1)
        wide = wide + roll(wide, 2 * ROWS, 1)
        tail = roll(disp, 3 * ROWS, 1)
        tail = tail + roll(tail, ROWS, 1)
        gram = gram + jnp.where((slot >= 2) & (slot < 2 + KRYLOV), inner + x[:1] * wide, 0.0)
        gram = gram + jnp.where((slot == 2) | (slot == 3), roll(x[:1] * tail, -4 * ROWS, 1), 0.0)
        gram = gram + jnp.where((slot == 4) | (slot == 5), roll(x[1:2] * tail, -2 * ROWS, 1), 0.0)
        rate, disp = roll(rate, -ROWS, 1), roll(disp, -3 * ROWS, 1)
        square = square + jnp.where(slot == 1, inner + rate * (2.0 * (x[:1] + gone[:1]) + rate), 0.0)
        square = square + jnp.where(slot == 0, disp * (2.0 * x[:1] + disp), 0.0)
    totals = [
        jnp.sum(jnp.sum(own[i * ROWS : (i + 1) * ROWS], 0, keepdims=True), 1, keepdims=True)
        for i in range(KRYLOV + 1)
    ]
    gram = gram + roll(gram, SIDE, 1)
    for i in range(KRYLOV):
        gram = gram + jnp.where(line == (2 + i) * ROWS, totals[i], 0.0)
    square = square + roll(square, SIDE, 1)
    square = square + roll(square, ROWS, 1)
    square = (square + jnp.where(line == SIDE + ROWS, totals[KRYLOV], 0.0)) * (1.0 / count)
    gram = roll(gram, GROUP - 2 * ROWS, 1)
    square = roll(square, GROUP - ROWS, 1)
    gram = jnp.where(line < SIDE, gram, square)
    return [jnp.where(lane % SIDE >= GROUP, jnp.broadcast_to(gram, shape), out) for out in outs]


def gram_of(totals):
    place = lane_of(totals.shape) // ROWS
    wanted = [GROUP // ROWS + i for i in range(KRYLOV)] + [(SIDE + GROUP) // ROWS]
    return [jnp.sum(jnp.where(place == at, totals, 0.0)) for at in wanted]


def unpacked(received, flat, tables):
    turned = received.T
    sides = []
    for dc in range(2):
        fields = turned[dc * SIDE : dc * SIDE + GROUP]
        sides.append(product(halves(fields), (tables[0, dc], tables[1, dc])))
    whole = jnp.concatenate([sides[0] + sides[1], reversed_lanes(sides[0] - sides[1])], 1)
    disp, rate, cut, edge = [whole[i * ROWS : (i + 1) * ROWS] for i in range(4)]
    return disp, rate - flat[:ROWS], flat[:ROWS] + edge, flat[ROWS:] + cut


def pack_kernel(
    resid_hbm, basis_hbm, tables_hbm, lent_ref, send_ref, own_ref, resid_ref, basis_ref, tables_ref, sems
):
    pairs = ((resid_hbm, resid_ref), (basis_hbm, basis_ref), (tables_hbm, tables_ref))
    copies = [pltpu.make_async_copy(a, b, sems.at[i]) for i, (a, b) in enumerate(pairs)]
    for copy in copies:
        copy.start()
    second = lax.axis_index("tm") == 1
    for copy in copies:
        copy.wait()
    flat = resid_ref[...].reshape(MODES, resid_ref.shape[-1])
    basis = basis_ref[:, :, 0]
    send_ref[...] = packed(flat, basis, lent_ref[2:, 0, 0], second, tables_ref)
    own_ref[...] = own_products(flat, basis)


def solve_kernel(
    kappa, count, recv_ref, own_ref, symbol_ref, time_ref, enter_ref, leave_ref, send_ref
):
    steps = time_ref.shape[1]
    here = lax.axis_index("tm") * 2 + lax.axis_index("rows")
    parts = [recv_ref[pl.ds(h, steps, stride=2), :] for h in range(2)]
    outs = solved(
        parts, own_ref[...], symbol_ref[pl.ds(here, 1), :], time_ref, enter_ref, leave_ref, kappa, count
    )
    for h, out in enumerate(outs):
        send_ref[pl.ds(h, steps, stride=2), :] = out


def unpack_kernel(recv_ref, resid_ref, tables_ref, precond_ref, image_ref, gram_ref):
    received = recv_ref[...]
    flat = resid_ref[...].reshape(MODES, resid_ref.shape[-1])
    fields = unpacked(received, flat, tables_ref)
    for slot, field in enumerate(fields):
        (precond_ref, image_ref)[slot // 2][slot % 2, 0] = field
    for i, value in enumerate(gram_of(jnp.sum(received, 0, keepdims=True))):
        gram_ref[i] = value


def solution(mesh):
    axes = ("tm", "rows")
    steps = mesh.shape["tm"]
    devices = steps * mesh.shape["rows"]
    params = pltpu.CompilerParams(vmem_limit_bytes=12 * 2**20)

    def on_device(resid, basis):
        cols = resid.shape[3]
        kappa = coupling(steps)
        count = 2.0 * steps * MODES * cols
        tables = both_halves(column_tables(cols))
        enter, leave = (both_halves(t) for t in row_tables())
        lent = lax.ppermute(basis, "tm", [(0, 1)])
        vmem = pl.BlockSpec(memory_space=pltpu.VMEM)
        hbm = pl.BlockSpec(memory_space=pltpu.HBM)
        fixed = [pltpu.with_memory_space_constraint(a, pltpu.HBM) for a in (resid, basis, tables)]
        message = jax.ShapeDtypeStruct((devices, LANES), jnp.float32)
        send, own = pl.pallas_call(
            pack_kernel,
            in_specs=[hbm, hbm, hbm, vmem],
            out_shape=(message, jax.ShapeDtypeStruct(((KRYLOV + 1) * ROWS, LANES), jnp.float32)),
            scratch_shapes=[
                pltpu.VMEM(resid.shape, jnp.float32),
                pltpu.VMEM(basis.shape, jnp.float32),
                pltpu.VMEM(tables.shape, jnp.bfloat16),
                pltpu.SemaphoreType.DMA((3,)),
            ],
            compiler_params=params,
            name="pack",
        )(*fixed, lent)
        recv = lax.all_to_all(send, axes, 0, 0, tiled=True)
        back = pl.pallas_call(
            lambda *refs: solve_kernel(kappa, count, *refs),
            out_shape=message,
            compiler_params=params,
            name="solve",
        )(recv, own, jnp.asarray(symbol_table(cols)), both_halves(time_table(steps)), enter, leave)
        home = lax.all_to_all(back, axes, 0, 0, tiled=True)
        shard = jax.ShapeDtypeStruct(resid.shape, jnp.float32)
        precond, image, gram = pl.pallas_call(
            unpack_kernel,
            out_shape=(shard, shard, jax.ShapeDtypeStruct((KRYLOV + 1,), jnp.float32)),
            out_specs=(vmem, vmem, pl.BlockSpec(memory_space=pltpu.SMEM)),
            compiler_params=params,
            name="unpack",
        )(home, resid, tables)
        return precond, image, gram

    return jax.shard_map(
        on_device,
        mesh=mesh,
        in_specs=(P(None, "tm", "rows", None), P(None, None, "tm", "rows", None)),
        out_specs=(P(None, "tm", "rows", None), P(None, "tm", "rows", None), P()),
        check_vma=False,
    )
```

time: 58 us -> 52.3 us (0.902)
  blocking collectives: 52.2 us -> 42.1 us
  waiting for transfers between devices: 0 us -> 4.23 us
  local copies, waits for them, and re-layouts: 1.67 us -> 0.03 us
  starting transfers between devices: 0 us -> 1.29 us
    all_to_all x1, blocking collectives: 32.9 us -> 23.4 us  [on_device(): recv = lax.all_to_all(send, axes, 0, 0, tiled=True)]
    ppermute x0 -> x1, waiting for transfers between devices: none -> 4.23 us  [on_device(): lent = lax.ppermute(basis, 'tm', [(0, 1)])]
    unnamed x8 -> x12, local copies, waits for them, and re-layouts: 1.67 us -> 0.03 us
    ppermute x0 -> x1, starting transfers between devices: none -> 1.29 us  [on_device(): lent = lax.ppermute(basis, 'tm', [(0, 1)])]
    pallas_call x1, Pallas kernels: 0.47 us -> 1.71 us  [on_device(): pl.pallas_call(pack_kernel, in_specs=[hbm, hbm, hbm, vmem], out_shape=(me...]
    pallas_call x1, Pallas kernels: 1.99 us -> 1.06 us  [on_device(): pl.pallas_call(lambda *refs: solve_kernel(kappa, count, *refs), out_shape...]
    all_to_all x1, blocking collectives: 19.3 us -> 18.6 us  [on_device(): home = lax.all_to_all(back, axes, 0, 0, tiled=True)]
  transfers between devices with their start and end apart: 0 -> 1, of which waited for: 0 -> 1; matrix products, arithmetic and copies ran while one was open for 0% -> 0% of each run, Pallas kernels for 0% -> 0%
where the time goes in v5:
time: 52.3 us; the launch traced here: 52.1 us
  blocking collectives  42.1 us (80%)
  waiting for transfers between devices  4.23 us (8%)
  Pallas kernels  3.77 us (7%)
  starting transfers between devices  1.29 us (2%)
  between operations  0.69 us (1%)
    all_to_all x1, blocking collectives, on_device(): recv = lax.all_to_all(send, axes, 0, 0, tiled=True)  23.4 us
    all_to_all x1, blocking collectives, on_device(): home = lax.all_to_all(back, axes, 0, 0, tiled=True)  18.6 us
    ppermute x1, waiting for transfers between devices, on_device(): lent = lax.ppermute(basis, 'tm', [(0, 1)])  4.23 us
    pallas_call x1, Pallas kernels, on_device(): pl.pallas_call(pack_kernel, in_specs=[hbm, hbm, hbm, vmem], out_shape=(me...  1.71 us
    ppermute x1, starting transfers between devices, on_device(): lent = lax.ppermute(basis, 'tm', [(0, 1)])  1.29 us
    pallas_call x1, Pallas kernels, on_device(): pl.pallas_call(lambda *refs: solve_kernel(kappa, count, *refs), out_shape...  1.06 us
  transfers between devices with their start and end apart: 1, of which 1 were waited for; matrix products, arithmetic and copies ran while one was open for 0% of the time, Pallas kernels for 0%

profile of v5, /device:TPU:1, one launch (start us, length us, event | category | flops | bytes accessed | tf_op | source)
XLA Modules:
  0.0 52.1 jit_solution(3479697198225660510)
XLA Ops:
  0.6 1.3 %collective-permute-start = (f32[4,2,1,8,512]{4,3,2,1,0:T(8,128)}, f32[4,2,1,8,512]{4,3,2,1,0:T(8,128)S(1)}, u32[]{:S(2)}, u32[]{:S(2)}) collective-permute-start(f32[4,2,1,8,512]{4,3,2,1,0:T(8,128)} %basis_hbm.1), channel_id=1, source_target_pairs={{0,2},{1,3}} | collective-permute-start | bytes 393224 | tf_op jit(solution)/shard_map/ppermute | solution.py:268
  1.9 4.2 %collective-permute-done.lent_ref = f32[4,2,1,8,512]{4,3,2,1,0:T(8,128)S(1)} collective-permute-done((f32[4,2,1,8,512]{4,3,2,1,0:T(8,128)}, f32[4,2,1,8,512]{4,3,2,1,0:T(8,128)S(1)}, u32[]{:S(2)}, u32[]{:S(2)}) %collective-permute-start) | collective-permute-done | bytes 131104 | tf_op jit(solution)/shard_map/ppermute | solution.py:268
  6.2 0.0 copy-start.2
  6.2 0.0 copy-start.3
  6.2 0.0 copy-start.4
  6.2 1.7 %pack.1 = (f32[256,128]{1,0:T(8,128)S(1)}, f32[40,128]{1,0:T(8,128)S(1)}) custom-call(f32[2,1,8,512]{3,2,1,0:T(8,128)} %resid_ref.1, f32[4,2,1,8,512]{4,3,2,1,0:T(8,128)} %basis_hbm.1, bf16[2,2,256,256]{3,2,1,0:T(8,128)(2,1)} %constant.10.clone.tables_hbm.tables_ref, f32[4,2,1,8,512]{4,3,2,1,0:T(8,128)S(1)} %collective-permute-done.lent_ref), custom_call_target="tpu_custom_call" | custom-call | tf_op jit(solution)/shard_map/pack/pallas_call | solution.py:273
  7.9 0.0 copy-start.1
  7.9 23.4 %all_to_all.22 = f32[256,1,128]{2,1,0:T(1,128)S(1)} all-to-all(f32[256,1,128]{2,1,0:T(1,128)S(1)} %bitcast.11), channel_id=1, replica_groups=mesh['tm'=128,'rows'=2] {'tm','rows'}, dimensions={0} | all-to-all | bytes 262144 | tf_op jit(solution)/shard_map/all_to_all | solution.py:286
  31.3 0.0 copy-done.2
  31.3 0.0 copy-done.3
  31.3 0.0 copy-done.4
  31.3 0.0 copy-done.1
  31.3 0.0 copy-start
  31.3 1.1 %solve.1 = f32[256,128]{1,0:T(8,128)S(1)} custom-call(f32[256,128]{1,0:T(8,128)S(1)} %bitcast.9, f32[40,128]{1,0:T(8,128)S(1)} %get-tuple-element.6.refs_1_, f32[256,128]{1,0:T(8,128)S(1)} %copy-done.3, bf16[2,128,512]{2,1,0:T(8,128)(2,1)S(1)} %copy-done.1, bf16[2,256,128]{2,1,0:T(8,128)(2,1)S(1)} %copy-done.4, bf16[2,128,512]{2,1,0:T(8,128)(2,1)S(1)} %copy-done.2), custom_call_target="tpu_custom_call" | custom-call | tf_op jit(solution)/shard_map/solve/pallas_call | solution.py:287
  32.4 0.0 copy-start.5
  32.4 18.6 %all_to_all.23 = f32[256,1,128]{2,1,0:T(1,128)S(1)} all-to-all(f32[256,1,128]{2,1,0:T(1,128)S(1)} %bitcast.10), channel_id=1, replica_groups=mesh['tm'=128,'rows'=2] {'tm','rows'}, dimensions={0} | all-to-all | bytes 262144 | tf_op jit(solution)/shard_map/all_to_all | solution.py:293
  51.1 0.0 copy-done
  51.1 0.0 copy-done.5
  51.1 1.0 %unpack.1 = (f32[2,1,8,512]{3,2,1,0:T(8,128)}, f32[2,1,8,512]{3,2,1,0:T(8,128)}, f32[5]{0:T(128)}) custom-call(f32[256,128]{1,0:T(8,128)S(1)} %bitcast.8, f32[2,1,8,512]{3,2,1,0:T(8,128)S(1)} %copy-done.5, bf16[2,2,256,256]{3,2,1,0:T(8,128)(2,1)S(1)} %copy-done), custom_call_target="tpu_custom_call" | custom-call | tf_op jit(solution)/shard_map/unpack/pallas_call | solution.py:295
Async XLA Ops:
  0.6 5.5 %collective-permute-start = (f32[4,2,1,8,512]{4,3,2,1,0:T(8,128)}, f32[4,2,1,8,512]{4,3,2,1,0:T(8,128)S(1)}, u32[]{:S(2)}, u32[]{:S(2)}) collective-permute-start(f32[4,2,1,8,512]{4,3,2,1,0:T(8,128)} %basis_hbm.1), channel_id=1, source_target_pairs={{0,2},{1,3}} | collective-permute-start | bytes 393224 | tf_op jit(solution)/shard_map/ppermute | solution.py:268
  6.2 25.2 %copy-start.2 = (bf16[2,128,512]{2,1,0:T(8,128)(2,1)S(1)}, bf16[2,128,512]{2,1,0:T(8,128)(2,1)}, u32[]{:S(2)}) copy-start(bf16[2,128,512]{2,1,0:T(8,128)(2,1)} %constant.12.clone.refs_5_) | copy-start | bytes 786436
  6.2 25.2 %copy-start.3 = (f32[256,128]{1,0:T(8,128)S(1)}, f32[256,128]{1,0:T(8,128)}, u32[]{:S(2)}) copy-start(f32[256,128]{1,0:T(8,128)} %constant.13.clone.refs_2_) | copy-start | bytes 393220
  6.2 25.2 %copy-start.4 = (bf16[2,256,128]{2,1,0:T(8,128)(2,1)S(1)}, bf16[2,256,128]{2,1,0:T(8,128)(2,1)}, u32[]{:S(2)}) copy-start(bf16[2,256,128]{2,1,0:T(8,128)(2,1)} %constant.11.clone.refs_4_) | copy-start | bytes 393220
  7.9 23.4 %copy-start.1 = (bf16[2,128,512]{2,1,0:T(8,128)(2,1)S(1)}, bf16[2,128,512]{2,1,0:T(8,128)(2,1)}, u32[]{:S(2)}) copy-start(bf16[2,128,512]{2,1,0:T(8,128)(2,1)} %constant.14.clone.refs_3_) | copy-start | bytes 786436
  31.3 19.7 %copy-start = (bf16[2,2,256,256]{3,2,1,0:T(8,128)(2,1)S(1)}, bf16[2,2,256,256]{3,2,1,0:T(8,128)(2,1)}, u32[]{:S(2)}) copy-start(bf16[2,2,256,256]{3,2,1,0:T(8,128)(2,1)} %constant.10.clone.tables_hbm.tables_ref) | copy-start | bytes 1572868
  32.4 18.7 %copy-start.5 = (f32[2,1,8,512]{3,2,1,0:T(8,128)S(1)}, f32[2,1,8,512]{3,2,1,0:T(8,128)}, u32[]{:S(2)}) copy-start(f32[2,1,8,512]{3,2,1,0:T(8,128)} %resid_ref.1) | copy-start | bytes 98308

commit v6 on v5

--- a/solution.py
+++ b/solution.py
@@ -113,11 +113,10 @@
     return total
 
 
-def packed(flat, basis, lent, second, tables):
-    half = flat.shape[1] // 2
-    fields = [flat] + [basis[i, 1] for i in range(KRYLOV)]
-    fields += [jnp.where(second, lent[i], basis[i, 0]) for i in range(2)]
-    whole = jnp.concatenate(fields, 0)
+def packed(fields, lent, second, tables):
+    half = fields.shape[1] // 2
+    kept = fields.shape[0] - lent.shape[0]
+    whole = jnp.concatenate([fields[:kept], jnp.where(second, lent, fields[kept:])], 0)
     left, right = whole[:, :half], reversed_lanes(whole[:, half:])
     sides = []
     for dc, folded in enumerate((left + right, left - right)):
@@ -126,9 +125,11 @@
     return jnp.concatenate(sides, 1)
 
 
-def own_products(flat, basis):
-    disp, velo = flat[:ROWS], flat[ROWS:]
-    terms = [basis[i, 0] * disp + basis[i, 1] * velo for i in range(KRYLOV)]
+def own_products(fields, given):
+    rows = [fields[at : at + ROWS] for at in range(0, fields.shape[0], ROWS)]
+    rows += [given[at : at + ROWS] for at in range(0, given.shape[0], ROWS)]
+    disp, velo, rest = rows[0], rows[1], rows[2:]
+    terms = [rest[KRYLOV + i] * disp + rest[i] * velo for i in range(KRYLOV)]
     terms.append(disp * disp + velo * velo)
     sums = [sum(t[:, at : at + LANES] for at in range(0, t.shape[1], LANES)) for t in terms]
     return jnp.concatenate(sums, 0)
@@ -214,38 +215,52 @@
     return disp, rate - flat[:ROWS], flat[:ROWS] + edge, flat[ROWS:] + cut
 
 
-def pack_kernel(
-    resid_hbm, basis_hbm, tables_hbm, lent_ref, send_ref, own_ref, resid_ref, basis_ref, tables_ref, sems
+def device_index():
+    return lax.axis_index("tm") * 2 + lax.axis_index("rows")
+
+
+def load_kernel(
+    resid_hbm, basis_hbm, tables_hbm, symbol_hbm,
+    fields_ref, give_ref, own_ref, tables_ref, symbol_ref, sems,
 ):
-    pairs = ((resid_hbm, resid_ref), (basis_hbm, basis_ref), (tables_hbm, tables_ref))
+    pairs = [(resid_hbm.at[c, 0], fields_ref.at[pl.ds(c * ROWS, ROWS)]) for c in range(2)]
+    for i in range(KRYLOV):
+        pairs.append((basis_hbm.at[i, 1, 0], fields_ref.at[pl.ds((2 + i) * ROWS, ROWS)]))
+    for i in range(KRYLOV):
+        place = fields_ref.at[pl.ds((6 + i) * ROWS, ROWS)] if i < 2 else give_ref.at[pl.ds((i - 2) * ROWS, ROWS)]
+        pairs.append((basis_hbm.at[i, 0, 0], place))
+    pairs.append((symbol_hbm.at[pl.ds(device_index(), 1)], symbol_ref))
+    pairs.append((tables_hbm, tables_ref))
     copies = [pltpu.make_async_copy(a, b, sems.at[i]) for i, (a, b) in enumerate(pairs)]
     for copy in copies:
         copy.start()
+    for copy in copies[:-2]:
+        copy.wait()
+    own_ref[...] = own_products(fields_ref[...], give_ref[...])
+    for copy in copies[-2:]:
+        copy.wait()
+
+
+def pack_kernel(fields_ref, lent_ref, tables_ref, send_ref):
     second = lax.axis_index("tm") == 1
-    for copy in copies:
-        copy.wait()
-    flat = resid_ref[...].reshape(MODES, resid_ref.shape[-1])
-    basis = basis_ref[:, :, 0]
-    send_ref[...] = packed(flat, basis, lent_ref[2:, 0, 0], second, tables_ref)
-    own_ref[...] = own_products(flat, basis)
+    send_ref[...] = packed(fields_ref[...], lent_ref[...], second, tables_ref)
 
 
 def solve_kernel(
     kappa, count, recv_ref, own_ref, symbol_ref, time_ref, enter_ref, leave_ref, send_ref
 ):
     steps = time_ref.shape[1]
-    here = lax.axis_index("tm") * 2 + lax.axis_index("rows")
     parts = [recv_ref[pl.ds(h, steps, stride=2), :] for h in range(2)]
     outs = solved(
-        parts, own_ref[...], symbol_ref[pl.ds(here, 1), :], time_ref, enter_ref, leave_ref, kappa, count
+        parts, own_ref[...], symbol_ref[...], time_ref, enter_ref, leave_ref, kappa, count
     )
     for h, out in enumerate(outs):
         send_ref[pl.ds(h, steps, stride=2), :] = out
 
 
-def unpack_kernel(recv_ref, resid_ref, tables_ref, precond_ref, image_ref, gram_ref):
+def unpack_kernel(recv_ref, fields_ref, tables_ref, precond_ref, image_ref, gram_ref):
     received = recv_ref[...]
-    flat = resid_ref[...].reshape(MODES, resid_ref.shape[-1])
+    flat = fields_ref[:MODES]
     fields = unpacked(received, flat, tables_ref)
     for slot, field in enumerate(fields):
         (precond_ref, image_ref)[slot // 2][slot % 2, 0] = field
@@ -265,31 +280,39 @@
         count = 2.0 * steps * MODES * cols
         tables = both_halves(column_tables(cols))
         enter, leave = (both_halves(t) for t in row_tables())
-        lent = lax.ppermute(basis, "tm", [(0, 1)])
         vmem = pl.BlockSpec(memory_space=pltpu.VMEM)
         hbm = pl.BlockSpec(memory_space=pltpu.HBM)
-        fixed = [pltpu.with_memory_space_constraint(a, pltpu.HBM) for a in (resid, basis, tables)]
+        symbol = jnp.asarray(symbol_table(cols))
+        placed = [pltpu.with_memory_space_constraint(a, pltpu.HBM) for a in (resid, basis, tables, symbol)]
         message = jax.ShapeDtypeStruct((devices, LANES), jnp.float32)
-        send, own = pl.pallas_call(
+        fields, give, own, tables, symbol = pl.pallas_call(
+            load_kernel,
+            in_specs=[hbm] * 4,
+            out_shape=(
+                jax.ShapeDtypeStruct((SIDE, cols), jnp.float32),
+                jax.ShapeDtypeStruct((MODES, cols), jnp.float32),
+                jax.ShapeDtypeStruct(((KRYLOV + 1) * ROWS, LANES), jnp.float32),
+                jax.ShapeDtypeStruct(tables.shape, tables.dtype),
+                jax.ShapeDtypeStruct((1, LANES), jnp.float32),
+            ),
+            scratch_shapes=[pltpu.SemaphoreType.DMA((2 + 2 * KRYLOV + 2,))],
+            compiler_params=params,
+            name="load",
+        )(*placed)
+        lent = lax.ppermute(give, "tm", [(0, 1)])
+        send = pl.pallas_call(
             pack_kernel,
-            in_specs=[hbm, hbm, hbm, vmem],
-            out_shape=(message, jax.ShapeDtypeStruct(((KRYLOV + 1) * ROWS, LANES), jnp.float32)),
-            scratch_shapes=[
-                pltpu.VMEM(resid.shape, jnp.float32),
-                pltpu.VMEM(basis.shape, jnp.float32),
-                pltpu.VMEM(tables.shape, jnp.bfloat16),
-                pltpu.SemaphoreType.DMA((3,)),
-            ],
+            out_shape=message,
             compiler_params=params,
             name="pack",
-        )(*fixed, lent)
+        )(fields, lent, tables)
         recv = lax.all_to_all(send, axes, 0, 0, tiled=True)
         back = pl.pallas_call(
             lambda *refs: solve_kernel(kappa, count, *refs),
             out_shape=message,
             compiler_params=params,
             name="solve",
-        )(recv, own, jnp.asarray(symbol_table(cols)), both_halves(time_table(steps)), enter, leave)
+        )(recv, own, symbol, both_halves(time_table(steps)), enter, leave)
         home = lax.all_to_all(back, axes, 0, 0, tiled=True)
         shard = jax.ShapeDtypeStruct(resid.shape, jnp.float32)
         precond, image, gram = pl.pallas_call(
@@ -298,7 +321,7 @@
             out_specs=(vmem, vmem, pl.BlockSpec(memory_space=pltpu.SMEM)),
             compiler_params=params,
             name="unpack",
-        )(home, resid, tables)
+        )(home, fields, tables)
         return precond, image, gram
 
     return jax.shard_map(

time: 52.3 us -> 52.3 us (level)
    pallas_call x1 -> x2, Pallas kernels: 1.71 us -> 1.8 us  [the longest x1 1.3 us: on_device(): pl.pallas_call(load_kernel, in_specs=[hbm] * 4, out_shape=(jax.ShapeDtype...]
where the time goes in v6:
time: 52.3 us; the launch traced here: 52.1 us
  blocking collectives  42.4 us (81%)
  waiting for transfers between devices  3.88 us (7%)
  Pallas kernels  3.86 us (7%)
  starting transfers between devices  1.29 us (2%)
  between operations  0.67 us (1%)
    all_to_all x1, blocking collectives, on_device(): recv = lax.all_to_all(send, axes, 0, 0, tiled=True)  23.8 us
    all_to_all x1, blocking collectives, on_device(): home = lax.all_to_all(back, axes, 0, 0, tiled=True)  18.6 us
    ppermute x1, waiting for transfers between devices, on_device(): lent = lax.ppermute(give, 'tm', [(0, 1)])  3.88 us
    pallas_call x1, Pallas kernels, on_device(): pl.pallas_call(load_kernel, in_specs=[hbm] * 4, out_shape=(jax.ShapeDtype...  1.3 us
    ppermute x1, starting transfers between devices, on_device(): lent = lax.ppermute(give, 'tm', [(0, 1)])  1.29 us
    pallas_call x1, Pallas kernels, on_device(): pl.pallas_call(lambda *refs: solve_kernel(kappa, count, *refs), out_shape...  1.06 us
  transfers between devices with their start and end apart: 1, of which 1 were waited for; matrix products, arithmetic and copies ran while one was open for 0% of the time, Pallas kernels for 0%

profile of v6, /device:TPU:1, one launch (start us, length us, event | category | flops | bytes accessed | tf_op | source)
XLA Modules:
  0.0 52.1 jit_solution(6973014244562845803)
XLA Ops:
  0.6 1.3 %load.1 = (f32[64,512]{1,0:T(8,128)S(1)}, f32[16,512]{1,0:T(8,128)S(1)}, f32[40,128]{1,0:T(8,128)S(1)}, bf16[2,2,256,256]{3,2,1,0:T(8,128)(2,1)S(1)}, f32[1,128]{1,0:T(1,128)S(1)}) custom-call(f32[2,1,8,512]{3,2,1,0:T(8,128)} %resid_hbm.1, f32[4,2,1,8,512]{4,3,2,1,0:T(8,128)} %basis_hbm.1, bf16[2,2,256,256]{3,2,1,0:T(8,128)(2,1)} %constant.10.clone.tables_hbm, ...), custom_call_target="tpu_custom_call" | custom-call | tf_op jit(solution)/shard_map/load/pallas_call | solution.py:288
  1.9 1.3 %collective-permute-start = (f32[16,512]{1,0:T(8,128)S(1)}, f32[16,512]{1,0:T(8,128)S(1)}, u32[]{:S(2)}, u32[]{:S(2)}) collective-permute-start(f32[16,512]{1,0:T(8,128)S(1)} %get-tuple-element.9), channel_id=1, source_target_pairs={{0,2},{1,3}} | collective-permute-start | bytes 98312 | tf_op jit(solution)/shard_map/ppermute | solution.py:302
  3.2 3.9 %collective-permute-done.lent_ref = f32[16,512]{1,0:T(8,128)S(1)} collective-permute-done((f32[16,512]{1,0:T(8,128)S(1)}, f32[16,512]{1,0:T(8,128)S(1)}, u32[]{:S(2)}, u32[]{:S(2)}) %collective-permute-start) | collective-permute-done | bytes 32800 | tf_op jit(solution)/shard_map/ppermute | solution.py:302
  7.1 0.0 copy-start.1
  7.1 0.0 copy-start.2
  7.1 0.5 pack.1
  7.6 0.0 copy-start
  7.6 23.8 %all_to_all.22 = f32[256,1,128]{2,1,0:T(1,128)S(1)} all-to-all(f32[256,1,128]{2,1,0:T(1,128)S(1)} %bitcast.10), channel_id=1, replica_groups=mesh['tm'=128,'rows'=2] {'tm','rows'}, dimensions={0} | all-to-all | bytes 262144 | tf_op jit(solution)/shard_map/all_to_all | solution.py:309
  31.4 0.0 copy-done.1
  31.4 0.0 copy-done.2
  31.4 0.0 copy-done
  31.4 1.1 %solve.1 = f32[256,128]{1,0:T(8,128)S(1)} custom-call(f32[256,128]{1,0:T(8,128)S(1)} %bitcast.8, f32[40,128]{1,0:T(8,128)S(1)} %get-tuple-element.11.refs_1_, f32[1,128]{1,0:T(1,128)S(1)} %get-tuple-element.12.refs_2_, bf16[2,128,512]{2,1,0:T(8,128)(2,1)S(1)} %copy-done, bf16[2,256,128]{2,1,0:T(8,128)(2,1)S(1)} %copy-done.2, bf16[2,128,512]{2,1,0:T(8,128)(2,1)S(1)} %copy-done.1), custom_call_target="tpu_custom_call" | custom-call | tf_op jit(solution)/shard_map/solve/pallas_call | solution.py:310
  32.5 18.6 %all_to_all.23 = f32[256,1,128]{2,1,0:T(1,128)S(1)} all-to-all(f32[256,1,128]{2,1,0:T(1,128)S(1)} %bitcast.9), channel_id=1, replica_groups=mesh['tm'=128,'rows'=2] {'tm','rows'}, dimensions={0} | all-to-all | bytes 262144 | tf_op jit(solution)/shard_map/all_to_all | solution.py:316
  51.1 1.0 %unpack.1 = (f32[2,1,8,512]{3,2,1,0:T(8,128)}, f32[2,1,8,512]{3,2,1,0:T(8,128)}, f32[5]{0:T(128)}) custom-call(f32[256,128]{1,0:T(8,128)S(1)} %bitcast.11, f32[64,512]{1,0:T(8,128)S(1)} %get-tuple-element.8.fields_ref, bf16[2,2,256,256]{3,2,1,0:T(8,128)(2,1)S(1)} %get-tuple-element.10.tables_ref), custom_call_target="tpu_custom_call" | custom-call | tf_op jit(solution)/shard_map/unpack/pallas_call | solution.py:318
Async XLA Ops:
  1.9 5.2 %collective-permute-start = (f32[16,512]{1,0:T(8,128)S(1)}, f32[16,512]{1,0:T(8,128)S(1)}, u32[]{:S(2)}, u32[]{:S(2)}) collective-permute-start(f32[16,512]{1,0:T(8,128)S(1)} %get-tuple-element.9), channel_id=1, source_target_pairs={{0,2},{1,3}} | collective-permute-start | bytes 98312 | tf_op jit(solution)/shard_map/ppermute | solution.py:302
  7.1 24.3 %copy-start.1 = (bf16[2,128,512]{2,1,0:T(8,128)(2,1)S(1)}, bf16[2,128,512]{2,1,0:T(8,128)(2,1)}, u32[]{:S(2)}) copy-start(bf16[2,128,512]{2,1,0:T(8,128)(2,1)} %constant.12.clone.refs_5_) | copy-start | bytes 786436
  7.1 24.3 %copy-start.2 = (bf16[2,256,128]{2,1,0:T(8,128)(2,1)S(1)}, bf16[2,256,128]{2,1,0:T(8,128)(2,1)}, u32[]{:S(2)}) copy-start(bf16[2,256,128]{2,1,0:T(8,128)(2,1)} %constant.11.clone.refs_4_) | copy-start | bytes 393220
  7.6 23.8 %copy-start = (bf16[2,128,512]{2,1,0:T(8,128)(2,1)S(1)}, bf16[2,128,512]{2,1,0:T(8,128)(2,1)}, u32[]{:S(2)}) copy-start(bf16[2,128,512]{2,1,0:T(8,128)(2,1)} %constant.14.clone.refs_3_) | copy-start | bytes 786436

commit v7 on v6

--- a/solution.py
+++ b/solution.py
@@ -64,7 +64,7 @@
 
 
 def column_tables(cols):
-    return np.stack([sines(n, np.arange(cols // 2), cols) for n in column_numbers(cols)])
+    return [sines(n, np.arange(cols // 2), cols) for n in column_numbers(cols)]
 
 
 def symbol_table(cols):
@@ -89,7 +89,7 @@
                         enter[h, dc * SIDE + c * ROWS + row, group + modes] = value
                 for field, group in enumerate((0, 2, 1, 3)):
                     leave[group * GROUP + modes, 0, h, dc * SIDE + field * ROWS + row] = value
-                for slot in range(1, 2 + KRYLOV):
+                for slot in (1, *range(KRYLOV, 2 * KRYLOV)):
                     leave[GROUP + modes, 1, h, dc * SIDE + slot * ROWS + row] = value
     return enter.reshape(2 * LANES, LANES), leave.reshape(LANES, 4 * LANES)
 
@@ -113,23 +113,23 @@
     return total
 
 
-def packed(fields, lent, second, tables):
+def folded(fields, lent, second):
     half = fields.shape[1] // 2
-    kept = fields.shape[0] - lent.shape[0]
-    whole = jnp.concatenate([fields[:kept], jnp.where(second, lent, fields[kept:])], 0)
+    mixed = jnp.where(second, lent, fields[MODES : 2 * MODES])
+    whole = jnp.concatenate([fields[:MODES], mixed, fields[2 * MODES :]], 0)
     left, right = whole[:, :half], reversed_lanes(whole[:, half:])
-    sides = []
-    for dc, folded in enumerate((left + right, left - right)):
-        table = (tables[0, dc], tables[1, dc])
-        sides.append(product(table, halves(folded), ((1,), (1,))))
-    return jnp.concatenate(sides, 1)
+    return [halves(left + right), halves(left - right)]
+
+
+def turned_to_modes(fold, table):
+    return product(table, fold, ((1,), (1,)))
 
 
 def own_products(fields, given):
     rows = [fields[at : at + ROWS] for at in range(0, fields.shape[0], ROWS)]
-    rows += [given[at : at + ROWS] for at in range(0, given.shape[0], ROWS)]
-    disp, velo, rest = rows[0], rows[1], rows[2:]
-    terms = [rest[KRYLOV + i] * disp + rest[i] * velo for i in range(KRYLOV)]
+    given = [given[at : at + ROWS] for at in range(0, given.shape[0], ROWS)]
+    disp, velo, firsts, seconds = rows[0], rows[1], rows[2:4] + given, rows[4:]
+    terms = [f * disp + s * velo for f, s in zip(firsts, seconds)]
     terms.append(disp * disp + velo * velo)
     sums = [sum(t[:, at : at + LANES] for at in range(0, t.shape[1], LANES)) for t in terms]
     return jnp.concatenate(sums, 0)
@@ -171,14 +171,13 @@
         rate = jnp.where(slot == 2, ALPHA * ended, 0.0)
         outs.append(jnp.where((row == 0) & (slot == 2), out + rate, out))
         disp = jnp.where(slot == 3, out[:1], 0.0)
-        inner = jnp.sum(jnp.where(slot[:1] >= 2, x * gone, gone * (2.0 * x + gone)), 0, keepdims=True)
-        wide = rate + roll(rate, ROWS, 1)
+        inner = jnp.sum(jnp.where(slot >= KRYLOV, x * gone, gone * (2.0 * x + gone)), 0, keepdims=True)
+        wide = roll(rate, 2 * ROWS, 1) + roll(rate, 3 * ROWS, 1)
         wide = wide + roll(wide, 2 * ROWS, 1)
-        tail = roll(disp, 3 * ROWS, 1)
-        tail = tail + roll(tail, ROWS, 1)
-        gram = gram + jnp.where((slot >= 2) & (slot < 2 + KRYLOV), inner + x[:1] * wide, 0.0)
-        gram = gram + jnp.where((slot == 2) | (slot == 3), roll(x[:1] * tail, -4 * ROWS, 1), 0.0)
-        gram = gram + jnp.where((slot == 4) | (slot == 5), roll(x[1:2] * tail, -2 * ROWS, 1), 0.0)
+        tail = roll(disp, -ROWS, 1) + disp
+        gram = gram + jnp.where(slot >= KRYLOV, inner + x[:1] * wide, 0.0)
+        gram = gram + jnp.where((slot == 4) | (slot == 5), roll(x[:1] * tail, 2 * ROWS, 1), 0.0)
+        gram = gram + jnp.where((slot == 6) | (slot == 7), roll(x[1:2] * tail, 4 * ROWS, 1), 0.0)
         rate, disp = roll(rate, -ROWS, 1), roll(disp, -3 * ROWS, 1)
         square = square + jnp.where(slot == 1, inner + rate * (2.0 * (x[:1] + gone[:1]) + rate), 0.0)
         square = square + jnp.where(slot == 0, disp * (2.0 * x[:1] + disp), 0.0)
@@ -186,22 +185,20 @@
         jnp.sum(jnp.sum(own[i * ROWS : (i + 1) * ROWS], 0, keepdims=True), 1, keepdims=True)
         for i in range(KRYLOV + 1)
     ]
-    gram = gram + roll(gram, SIDE, 1)
+    extra = jnp.where(line == SIDE + GROUP, totals[KRYLOV] * (1.0 / count), 0.0)
     for i in range(KRYLOV):
-        gram = gram + jnp.where(line == (2 + i) * ROWS, totals[i], 0.0)
-    square = square + roll(square, SIDE, 1)
-    square = square + roll(square, ROWS, 1)
-    square = (square + jnp.where(line == SIDE + ROWS, totals[KRYLOV], 0.0)) * (1.0 / count)
-    gram = roll(gram, GROUP - 2 * ROWS, 1)
-    square = roll(square, GROUP - ROWS, 1)
-    gram = jnp.where(line < SIDE, gram, square)
+        extra = extra + jnp.where(line == GROUP + i * ROWS, totals[i], 0.0)
+    square = square * (1.0 / count)
+    square = roll(square, GROUP + SIDE, 1) + roll(square, GROUP, 1)
+    gram = jnp.where(line < SIDE, gram + roll(gram, SIDE, 1), square) + extra
     return [jnp.where(lane % SIDE >= GROUP, jnp.broadcast_to(gram, shape), out) for out in outs]
 
 
 def gram_of(totals):
-    place = lane_of(totals.shape) // ROWS
-    wanted = [GROUP // ROWS + i for i in range(KRYLOV)] + [(SIDE + GROUP) // ROWS]
-    return [jnp.sum(jnp.where(place == at, totals, 0.0)) for at in wanted]
+    line = lane_of(totals.shape)
+    masks = [line // ROWS == GROUP // ROWS + i for i in range(KRYLOV)]
+    masks.append(line // MODES == (SIDE + GROUP) // MODES)
+    return [jnp.sum(jnp.where(mask, totals, 0.0)) for mask in masks]
 
 
 def unpacked(received, flat, tables):
@@ -209,7 +206,7 @@
     sides = []
     for dc in range(2):
         fields = turned[dc * SIDE : dc * SIDE + GROUP]
-        sides.append(product(halves(fields), (tables[0, dc], tables[1, dc])))
+        sides.append(product(halves(fields), tables[dc]))
     whole = jnp.concatenate([sides[0] + sides[1], reversed_lanes(sides[0] - sides[1])], 1)
     disp, rate, cut, edge = [whole[i * ROWS : (i + 1) * ROWS] for i in range(4)]
     return disp, rate - flat[:ROWS], flat[:ROWS] + edge, flat[ROWS:] + cut
@@ -219,31 +216,34 @@
     return lax.axis_index("tm") * 2 + lax.axis_index("rows")
 
 
-def load_kernel(
-    resid_hbm, basis_hbm, tables_hbm, symbol_hbm,
-    fields_ref, give_ref, own_ref, tables_ref, symbol_ref, sems,
+def pack_kernel(
+    resid_hbm, basis_hbm, tables_hbm, symbol_hbm, lent_ref,
+    send_ref, own_ref, fields_ref, tables_ref, symbol_ref, given_ref, sems,
 ):
-    pairs = [(resid_hbm.at[c, 0], fields_ref.at[pl.ds(c * ROWS, ROWS)]) for c in range(2)]
+    slabs = [fields_ref.at[pl.ds(at, ROWS)] for at in range(0, SIDE, ROWS)]
+    pairs = [(resid_hbm.at[c, 0], slabs[c]) for c in range(2)]
     for i in range(KRYLOV):
-        pairs.append((basis_hbm.at[i, 1, 0], fields_ref.at[pl.ds((2 + i) * ROWS, ROWS)]))
-    for i in range(KRYLOV):
-        place = fields_ref.at[pl.ds((6 + i) * ROWS, ROWS)] if i < 2 else give_ref.at[pl.ds((i - 2) * ROWS, ROWS)]
+        place = slabs[2 + i] if i < 2 else given_ref.at[pl.ds((i - 2) * ROWS, ROWS)]
         pairs.append((basis_hbm.at[i, 0, 0], place))
+        pairs.append((basis_hbm.at[i, 1, 0], slabs[4 + i]))
+    for dc in range(2):
+        pairs.append((tables_hbm.at[dc], tables_ref.at[dc]))
     pairs.append((symbol_hbm.at[pl.ds(device_index(), 1)], symbol_ref))
-    pairs.append((tables_hbm, tables_ref))
     copies = [pltpu.make_async_copy(a, b, sems.at[i]) for i, (a, b) in enumerate(pairs)]
     for copy in copies:
         copy.start()
-    for copy in copies[:-2]:
+    second = lax.axis_index("tm") == 1
+    for copy in copies[:-3]:
         copy.wait()
-    own_ref[...] = own_products(fields_ref[...], give_ref[...])
-    for copy in copies[-2:]:
-        copy.wait()
-
-
-def pack_kernel(fields_ref, lent_ref, tables_ref, send_ref):
-    second = lax.axis_index("tm") == 1
-    send_ref[...] = packed(fields_ref[...], lent_ref[...], second, tables_ref)
+    fields = fields_ref[...]
+    folds = folded(fields, lent_ref[2:, 0, 0].reshape(MODES, fields.shape[1]), second)
+    own_ref[...] = own_products(fields, given_ref[...])
+    sides = []
+    for dc in range(2):
+        copies[dc - 3].wait()
+        sides.append(turned_to_modes(folds[dc], tables_ref[dc]))
+    send_ref[...] = jnp.concatenate(sides, 1)
+    copies[-1].wait()
 
 
 def solve_kernel(
@@ -258,14 +258,23 @@
         send_ref[pl.ds(h, steps, stride=2), :] = out
 
 
-def unpack_kernel(recv_ref, fields_ref, tables_ref, precond_ref, image_ref, gram_ref):
+def unpack_kernel(
+    recv_ref, fields_ref, tables_ref, precond_hbm, image_hbm, gram_hbm, whole_ref, gram_ref, sems
+):
     received = recv_ref[...]
-    flat = fields_ref[:MODES]
-    fields = unpacked(received, flat, tables_ref)
+    fields = unpacked(received, fields_ref[:MODES], tables_ref)
+    copies = []
     for slot, field in enumerate(fields):
-        (precond_ref, image_ref)[slot // 2][slot % 2, 0] = field
+        whole_ref[slot] = field
+        target = (precond_hbm, image_hbm)[slot // 2].at[slot % 2, 0]
+        copies.append(pltpu.make_async_copy(whole_ref.at[slot], target, sems.at[slot]))
+        copies[-1].start()
     for i, value in enumerate(gram_of(jnp.sum(received, 0, keepdims=True))):
         gram_ref[i] = value
+    copies.append(pltpu.make_async_copy(gram_ref, gram_hbm, sems.at[len(fields)]))
+    copies[-1].start()
+    for copy in copies:
+        copy.wait()
 
 
 def solution(mesh):
@@ -278,34 +287,31 @@
         cols = resid.shape[3]
         kappa = coupling(steps)
         count = 2.0 * steps * MODES * cols
-        tables = both_halves(column_tables(cols))
+        tables = jnp.stack([both_halves(t) for t in column_tables(cols)])
         enter, leave = (both_halves(t) for t in row_tables())
         vmem = pl.BlockSpec(memory_space=pltpu.VMEM)
         hbm = pl.BlockSpec(memory_space=pltpu.HBM)
         symbol = jnp.asarray(symbol_table(cols))
         placed = [pltpu.with_memory_space_constraint(a, pltpu.HBM) for a in (resid, basis, tables, symbol)]
         message = jax.ShapeDtypeStruct((devices, LANES), jnp.float32)
-        fields, give, own, tables, symbol = pl.pallas_call(
-            load_kernel,
-            in_specs=[hbm] * 4,
+        lent = lax.ppermute(basis, "tm", [(0, 1)])
+        send, own, fields, tables, symbol = pl.pallas_call(
+            pack_kernel,
+            in_specs=[hbm] * 4 + [vmem],
             out_shape=(
+                message,
+                jax.ShapeDtypeStruct(((KRYLOV + 1) * ROWS, LANES), jnp.float32),
                 jax.ShapeDtypeStruct((SIDE, cols), jnp.float32),
-                jax.ShapeDtypeStruct((MODES, cols), jnp.float32),
-                jax.ShapeDtypeStruct(((KRYLOV + 1) * ROWS, LANES), jnp.float32),
                 jax.ShapeDtypeStruct(tables.shape, tables.dtype),
                 jax.ShapeDtypeStruct((1, LANES), jnp.float32),
             ),
-            scratch_shapes=[pltpu.SemaphoreType.DMA((2 + 2 * KRYLOV + 2,))],
-            compiler_params=params,
-            name="load",
-        )(*placed)
-        lent = lax.ppermute(give, "tm", [(0, 1)])
-        send = pl.pallas_call(
-            pack_kernel,
-            out_shape=message,
+            scratch_shapes=[
+                pltpu.VMEM((MODES, cols), jnp.float32),
+                pltpu.SemaphoreType.DMA((2 + 2 * KRYLOV + 3,)),
+            ],
             compiler_params=params,
             name="pack",
-        )(fields, lent, tables)
+        )(*placed, lent)
         recv = lax.all_to_all(send, axes, 0, 0, tiled=True)
         back = pl.pallas_call(
             lambda *refs: solve_kernel(kappa, count, *refs),
@@ -318,7 +324,13 @@
         precond, image, gram = pl.pallas_call(
             unpack_kernel,
             out_shape=(shard, shard, jax.ShapeDtypeStruct((KRYLOV + 1,), jnp.float32)),
-            out_specs=(vmem, vmem, pl.BlockSpec(memory_space=pltpu.SMEM)),
+            in_specs=[vmem] * 3,
+            out_specs=[hbm] * 3,
+            scratch_shapes=[
+                pltpu.VMEM((4, ROWS, cols), jnp.float32),
+                pltpu.SMEM((KRYLOV + 1,), jnp.float32),
+                pltpu.SemaphoreType.DMA((5,)),
+            ],
             compiler_params=params,
             name="unpack",
         )(home, fields, tables)

time: 52.3 us -> 52.4 us (level)
    pallas_call x2 -> x1, Pallas kernels: 1.8 us -> 1.97 us  [on_device(): pl.pallas_call(pack_kernel, in_specs=[hbm] * 4 + [vmem], out_shape=(messa...]
where the time goes in v7:
time: 52.4 us; the launch traced here: 52.2 us
  blocking collectives  42 us (80%)
  waiting for transfers between devices  4.23 us (8%)
  Pallas kernels  3.99 us (8%)
  starting transfers between devices  1.29 us (2%)
  between operations  0.67 us (1%)
    all_to_all x1, blocking collectives, on_device(): recv = lax.all_to_all(send, axes, 0, 0, tiled=True)  23.4 us
    all_to_all x1, blocking collectives, on_device(): home = lax.all_to_all(back, axes, 0, 0, tiled=True)  18.6 us
    ppermute x1, waiting for transfers between devices, on_device(): lent = lax.ppermute(basis, 'tm', [(0, 1)])  4.23 us
    pallas_call x1, Pallas kernels, on_device(): pl.pallas_call(pack_kernel, in_specs=[hbm] * 4 + [vmem], out_shape=(messa...  1.97 us
    ppermute x1, starting transfers between devices, on_device(): lent = lax.ppermute(basis, 'tm', [(0, 1)])  1.29 us
  transfers between devices with their start and end apart: 1, of which 1 were waited for; matrix products, arithmetic and copies ran while one was open for 0% of the time, Pallas kernels for 0%

profile of v7, /device:TPU:1, one launch (start us, length us, event | category | flops | bytes accessed | tf_op | source)
XLA Modules:
  0.0 52.2 jit_solution(8090733117574382125)
XLA Ops:
  0.6 1.3 %collective-permute-start = (f32[4,2,1,8,512]{4,3,2,1,0:T(8,128)}, f32[4,2,1,8,512]{4,3,2,1,0:T(8,128)S(1)}, u32[]{:S(2)}, u32[]{:S(2)}) collective-permute-start(f32[4,2,1,8,512]{4,3,2,1,0:T(8,128)} %basis_hbm.1), channel_id=1, source_target_pairs={{0,2},{1,3}} | collective-permute-start | bytes 393224 | tf_op jit(solution)/shard_map/ppermute | solution.py:297
  1.9 4.2 %collective-permute-done.lent_ref = f32[4,2,1,8,512]{4,3,2,1,0:T(8,128)S(1)} collective-permute-done((f32[4,2,1,8,512]{4,3,2,1,0:T(8,128)}, f32[4,2,1,8,512]{4,3,2,1,0:T(8,128)S(1)}, u32[]{:S(2)}, u32[]{:S(2)}) %collective-permute-start) | collective-permute-done | bytes 131104 | tf_op jit(solution)/shard_map/ppermute | solution.py:297
  6.2 0.0 copy-start.1
  6.2 0.0 copy-start.2
  6.2 2.0 %pack.1 = (f32[256,128]{1,0:T(8,128)S(1)}, f32[40,128]{1,0:T(8,128)S(1)}, f32[64,512]{1,0:T(8,128)S(1)}, bf16[2,2,256,256]{3,2,1,0:T(8,128)(2,1)S(1)}, f32[1,128]{1,0:T(1,128)S(1)}) custom-call(f32[2,1,8,512]{3,2,1,0:T(8,128)} %resid_hbm.1, f32[4,2,1,8,512]{4,3,2,1,0:T(8,128)} %basis_hbm.1, bf16[2,2,256,256]{3,2,1,0:T(8,128)(2,1)} %constant.22.tables_hbm, ...), custom_call_target="tpu_custom_call" | custom-call | tf_op jit(solution)/shard_map/pack/pallas_call | solution.py:298
  8.1 0.0 copy-start
  8.2 23.4 %all_to_all.22 = f32[256,1,128]{2,1,0:T(1,128)S(1)} all-to-all(f32[256,1,128]{2,1,0:T(1,128)S(1)} %bitcast.11), channel_id=1, replica_groups=mesh['tm'=128,'rows'=2] {'tm','rows'}, dimensions={0} | all-to-all | bytes 262144 | tf_op jit(solution)/shard_map/all_to_all | solution.py:315
  31.6 0.0 copy-done.1
  31.6 0.0 copy-done.2
  31.6 0.0 copy-done
  31.6 1.0 %solve.1 = f32[256,128]{1,0:T(8,128)S(1)} custom-call(f32[256,128]{1,0:T(8,128)S(1)} %bitcast.8, f32[40,128]{1,0:T(8,128)S(1)} %get-tuple-element.9.refs_1_, f32[1,128]{1,0:T(1,128)S(1)} %get-tuple-element.10.refs_2_, bf16[2,128,512]{2,1,0:T(8,128)(2,1)S(1)} %copy-done, bf16[2,256,128]{2,1,0:T(8,128)(2,1)S(1)} %copy-done.2, bf16[2,128,512]{2,1,0:T(8,128)(2,1)S(1)} %copy-done.1), custom_call_target="tpu_custom_call" | custom-call | tf_op jit(solution)/shard_map/solve/pallas_call | solution.py:316
  32.6 18.6 %all_to_all.23 = f32[256,1,128]{2,1,0:T(1,128)S(1)} all-to-all(f32[256,1,128]{2,1,0:T(1,128)S(1)} %bitcast.9), channel_id=1, replica_groups=mesh['tm'=128,'rows'=2] {'tm','rows'}, dimensions={0} | all-to-all | bytes 262144 | tf_op jit(solution)/shard_map/all_to_all | solution.py:322
  51.2 1.0 %unpack.1 = (f32[2,1,8,512]{3,2,1,0:T(8,128)}, f32[2,1,8,512]{3,2,1,0:T(8,128)}, f32[5]{0:T(128)}) custom-call(f32[256,128]{1,0:T(8,128)S(1)} %bitcast.10, f32[64,512]{1,0:T(8,128)S(1)} %get-tuple-element.11.fields_ref, bf16[2,2,256,256]{3,2,1,0:T(8,128)(2,1)S(1)} %get-tuple-element.12.tables_ref), custom_call_target="tpu_custom_call" | custom-call | tf_op jit(solution)/shard_map/unpack/pallas_call | solution.py:324
Async XLA Ops:
  0.6 5.5 %collective-permute-start = (f32[4,2,1,8,512]{4,3,2,1,0:T(8,128)}, f32[4,2,1,8,512]{4,3,2,1,0:T(8,128)S(1)}, u32[]{:S(2)}, u32[]{:S(2)}) collective-permute-start(f32[4,2,1,8,512]{4,3,2,1,0:T(8,128)} %basis_hbm.1), channel_id=1, source_target_pairs={{0,2},{1,3}} | collective-permute-start | bytes 393224 | tf_op jit(solution)/shard_map/ppermute | solution.py:297
  6.2 25.4 %copy-start.1 = (bf16[2,128,512]{2,1,0:T(8,128)(2,1)S(1)}, bf16[2,128,512]{2,1,0:T(8,128)(2,1)}, u32[]{:S(2)}) copy-start(bf16[2,128,512]{2,1,0:T(8,128)(2,1)} %constant.15.clone.refs_5_) | copy-start | bytes 786436
  6.2 25.4 %copy-start.2 = (bf16[2,256,128]{2,1,0:T(8,128)(2,1)S(1)}, bf16[2,256,128]{2,1,0:T(8,128)(2,1)}, u32[]{:S(2)}) copy-start(bf16[2,256,128]{2,1,0:T(8,128)(2,1)} %constant.14.clone.refs_4_) | copy-start | bytes 393220
  8.1 23.4 %copy-start = (bf16[2,128,512]{2,1,0:T(8,128)(2,1)S(1)}, bf16[2,128,512]{2,1,0:T(8,128)(2,1)}, u32[]{:S(2)}) copy-start(bf16[2,128,512]{2,1,0:T(8,128)(2,1)} %constant.17.clone.refs_3_) | copy-start | bytes 786436

commit v8 on v7

--- a/solution.py
+++ b/solution.py
@@ -91,7 +91,8 @@
                     leave[group * GROUP + modes, 0, h, dc * SIDE + field * ROWS + row] = value
                 for slot in (1, *range(KRYLOV, 2 * KRYLOV)):
                     leave[GROUP + modes, 1, h, dc * SIDE + slot * ROWS + row] = value
-    return enter.reshape(2 * LANES, LANES), leave.reshape(LANES, 4 * LANES)
+    enter = enter.reshape(4, SIDE, LANES).transpose(1, 0, 2).reshape(SIDE, 4 * LANES)
+    return leave.reshape(LANES, 4 * LANES), enter
 
 
 def halves(value):
@@ -113,10 +114,10 @@
     return total
 
 
-def folded(fields, lent, second):
-    half = fields.shape[1] // 2
-    mixed = jnp.where(second, lent, fields[MODES : 2 * MODES])
-    whole = jnp.concatenate([fields[:MODES], mixed, fields[2 * MODES :]], 0)
+def folded(flat, basis, lent, second):
+    half = flat.shape[1] // 2
+    mixed = [jnp.where(second, lent[i], basis[i, 0]) for i in range(2)]
+    whole = jnp.concatenate([flat] + mixed + [basis[i, 1] for i in range(KRYLOV)], 0)
     left, right = whole[:, :half], reversed_lanes(whole[:, half:])
     return [halves(left + right), halves(left - right)]
 
@@ -125,11 +126,9 @@
     return product(table, fold, ((1,), (1,)))
 
 
-def own_products(fields, given):
-    rows = [fields[at : at + ROWS] for at in range(0, fields.shape[0], ROWS)]
-    given = [given[at : at + ROWS] for at in range(0, given.shape[0], ROWS)]
-    disp, velo, firsts, seconds = rows[0], rows[1], rows[2:4] + given, rows[4:]
-    terms = [f * disp + s * velo for f, s in zip(firsts, seconds)]
+def own_products(flat, basis):
+    disp, velo = flat[:ROWS], flat[ROWS:]
+    terms = [basis[i, 0] * disp + basis[i, 1] * velo for i in range(KRYLOV)]
     terms.append(disp * disp + velo * velo)
     sums = [sum(t[:, at : at + LANES] for at in range(0, t.shape[1], LANES)) for t in terms]
     return jnp.concatenate(sums, 0)
@@ -218,63 +217,51 @@
 
 def pack_kernel(
     resid_hbm, basis_hbm, tables_hbm, symbol_hbm, lent_ref,
-    send_ref, own_ref, fields_ref, tables_ref, symbol_ref, given_ref, sems,
+    send_ref, own_ref, resid_ref, tables_ref, symbol_ref, basis_ref, sems,
 ):
-    slabs = [fields_ref.at[pl.ds(at, ROWS)] for at in range(0, SIDE, ROWS)]
-    pairs = [(resid_hbm.at[c, 0], slabs[c]) for c in range(2)]
-    for i in range(KRYLOV):
-        place = slabs[2 + i] if i < 2 else given_ref.at[pl.ds((i - 2) * ROWS, ROWS)]
-        pairs.append((basis_hbm.at[i, 0, 0], place))
-        pairs.append((basis_hbm.at[i, 1, 0], slabs[4 + i]))
-    for dc in range(2):
-        pairs.append((tables_hbm.at[dc], tables_ref.at[dc]))
-    pairs.append((symbol_hbm.at[pl.ds(device_index(), 1)], symbol_ref))
+    pairs = (
+        (resid_hbm, resid_ref),
+        (basis_hbm, basis_ref),
+        (tables_hbm, tables_ref),
+        (symbol_hbm.at[pl.ds(device_index(), 1)], symbol_ref),
+    )
     copies = [pltpu.make_async_copy(a, b, sems.at[i]) for i, (a, b) in enumerate(pairs)]
     for copy in copies:
         copy.start()
     second = lax.axis_index("tm") == 1
-    for copy in copies[:-3]:
-        copy.wait()
-    fields = fields_ref[...]
-    folds = folded(fields, lent_ref[2:, 0, 0].reshape(MODES, fields.shape[1]), second)
-    own_ref[...] = own_products(fields, given_ref[...])
-    sides = []
-    for dc in range(2):
-        copies[dc - 3].wait()
-        sides.append(turned_to_modes(folds[dc], tables_ref[dc]))
+    copies[0].wait()
+    copies[1].wait()
+    flat = resid_ref[...].reshape(MODES, resid_ref.shape[-1])
+    basis = basis_ref[:, :, 0]
+    folds = folded(flat, basis, lent_ref[2:, 0, 0], second)
+    own_ref[...] = own_products(flat, basis)
+    copies[2].wait()
+    sides = [turned_to_modes(folds[dc], tables_ref[dc]) for dc in range(2)]
     send_ref[...] = jnp.concatenate(sides, 1)
-    copies[-1].wait()
+    copies[3].wait()
 
 
 def solve_kernel(
-    kappa, count, recv_ref, own_ref, symbol_ref, time_ref, enter_ref, leave_ref, send_ref
+    kappa, count, steps, recv_ref, own_ref, symbol_ref, tables_ref, send_ref
 ):
-    steps = time_ref.shape[1]
+    time, leave = tables_ref[:, :steps], tables_ref[:, steps : steps + LANES]
+    stored = tables_ref[:, steps + LANES :]
+    enter = jnp.concatenate([stored[:, :, at : at + LANES] for at in range(0, 4 * LANES, LANES)], 1)
     parts = [recv_ref[pl.ds(h, steps, stride=2), :] for h in range(2)]
     outs = solved(
-        parts, own_ref[...], symbol_ref[...], time_ref, enter_ref, leave_ref, kappa, count
+        parts, own_ref[...], symbol_ref[...], time, enter, leave, kappa, count
     )
     for h, out in enumerate(outs):
         send_ref[pl.ds(h, steps, stride=2), :] = out
 
 
-def unpack_kernel(
-    recv_ref, fields_ref, tables_ref, precond_hbm, image_hbm, gram_hbm, whole_ref, gram_ref, sems
-):
+def unpack_kernel(recv_ref, resid_ref, tables_ref, precond_ref, image_ref, gram_ref):
     received = recv_ref[...]
-    fields = unpacked(received, fields_ref[:MODES], tables_ref)
-    copies = []
-    for slot, field in enumerate(fields):
-        whole_ref[slot] = field
-        target = (precond_hbm, image_hbm)[slot // 2].at[slot % 2, 0]
-        copies.append(pltpu.make_async_copy(whole_ref.at[slot], target, sems.at[slot]))
-        copies[-1].start()
+    flat = resid_ref[...].reshape(MODES, resid_ref.shape[-1])
+    for slot, field in enumerate(unpacked(received, flat, tables_ref)):
+        (precond_ref, image_ref)[slot // 2][slot % 2, 0] = field
     for i, value in enumerate(gram_of(jnp.sum(received, 0, keepdims=True))):
         gram_ref[i] = value
-    copies.append(pltpu.make_async_copy(gram_ref, gram_hbm, sems.at[len(fields)]))
-    copies[-1].start()
-    for copy in copies:
-        copy.wait()
 
 
 def solution(mesh):
@@ -288,52 +275,46 @@
         kappa = coupling(steps)
         count = 2.0 * steps * MODES * cols
         tables = jnp.stack([both_halves(t) for t in column_tables(cols)])
-        enter, leave = (both_halves(t) for t in row_tables())
+        solve_tables = both_halves(np.concatenate([time_table(steps), *row_tables()], 0))
         vmem = pl.BlockSpec(memory_space=pltpu.VMEM)
         hbm = pl.BlockSpec(memory_space=pltpu.HBM)
         symbol = jnp.asarray(symbol_table(cols))
         placed = [pltpu.with_memory_space_constraint(a, pltpu.HBM) for a in (resid, basis, tables, symbol)]
         message = jax.ShapeDtypeStruct((devices, LANES), jnp.float32)
         lent = lax.ppermute(basis, "tm", [(0, 1)])
-        send, own, fields, tables, symbol = pl.pallas_call(
+        send, own, kept, tables, symbol = pl.pallas_call(
             pack_kernel,
             in_specs=[hbm] * 4 + [vmem],
             out_shape=(
                 message,
                 jax.ShapeDtypeStruct(((KRYLOV + 1) * ROWS, LANES), jnp.float32),
-                jax.ShapeDtypeStruct((SIDE, cols), jnp.float32),
+                jax.ShapeDtypeStruct(resid.shape, jnp.float32),
                 jax.ShapeDtypeStruct(tables.shape, tables.dtype),
                 jax.ShapeDtypeStruct((1, LANES), jnp.float32),
             ),
             scratch_shapes=[
-                pltpu.VMEM((MODES, cols), jnp.float32),
-                pltpu.SemaphoreType.DMA((2 + 2 * KRYLOV + 3,)),
+                pltpu.VMEM(basis.shape, jnp.float32),
+                pltpu.SemaphoreType.DMA((4,)),
             ],
             compiler_params=params,
             name="pack",
         )(*placed, lent)
         recv = lax.all_to_all(send, axes, 0, 0, tiled=True)
         back = pl.pallas_call(
-            lambda *refs: solve_kernel(kappa, count, *refs),
+            lambda *refs: solve_kernel(kappa, count, steps, *refs),
             out_shape=message,
             compiler_params=params,
             name="solve",
-        )(recv, own, symbol, both_halves(time_table(steps)), enter, leave)
+        )(recv, own, symbol, solve_tables)
         home = lax.all_to_all(back, axes, 0, 0, tiled=True)
         shard = jax.ShapeDtypeStruct(resid.shape, jnp.float32)
         precond, image, gram = pl.pallas_call(
             unpack_kernel,
             out_shape=(shard, shard, jax.ShapeDtypeStruct((KRYLOV + 1,), jnp.float32)),
-            in_specs=[vmem] * 3,
-            out_specs=[hbm] * 3,
-            scratch_shapes=[
-                pltpu.VMEM((4, ROWS, cols), jnp.float32),
-                pltpu.SMEM((KRYLOV + 1,), jnp.float32),
-                pltpu.SemaphoreType.DMA((5,)),
-            ],
+            out_specs=(vmem, vmem, pl.BlockSpec(memory_space=pltpu.SMEM)),
             compiler_params=params,
             name="unpack",
-        )(home, fields, tables)
+        )(home, kept, tables)
         return precond, image, gram
 
     return jax.shard_map(

time: 52.4 us -> 52.1 us (level)
  no operation moved by 1% of the time
where the time goes in v8:
time: 52.1 us; the launch traced here: 51.9 us
  blocking collectives  42 us (81%)
  waiting for transfers between devices  4.23 us (8%)
  Pallas kernels  3.56 us (7%)
  starting transfers between devices  1.42 us (3%)
  between operations  0.66 us (1%)
    all_to_all x1, blocking collectives, on_device(): recv = lax.all_to_all(send, axes, 0, 0, tiled=True)  23.4 us
    all_to_all x1, blocking collectives, on_device(): home = lax.all_to_all(back, axes, 0, 0, tiled=True)  18.6 us
    ppermute x1, waiting for transfers between devices, on_device(): lent = lax.ppermute(basis, 'tm', [(0, 1)])  4.23 us
    pallas_call x1, Pallas kernels, on_device(): pl.pallas_call(pack_kernel, in_specs=[hbm] * 4 + [vmem], out_shape=(messa...  1.57 us
    ppermute x1, starting transfers between devices, on_device(): lent = lax.ppermute(basis, 'tm', [(0, 1)])  1.42 us
  transfers between devices with their start and end apart: 1, of which 1 were waited for; matrix products, arithmetic and copies ran while one was open for 0% of the time, Pallas kernels for 0%

profile of v8, /device:TPU:1, one launch (start us, length us, event | category | flops | bytes accessed | tf_op | source)
XLA Modules:
  0.0 51.9 jit_solution(11622993911831863592)
XLA Ops:
  0.6 0.0 copy-start
  0.6 1.4 %collective-permute-start = (f32[4,2,1,8,512]{4,3,2,1,0:T(8,128)}, f32[4,2,1,8,512]{4,3,2,1,0:T(8,128)S(1)}, u32[]{:S(2)}, u32[]{:S(2)}) collective-permute-start(f32[4,2,1,8,512]{4,3,2,1,0:T(8,128)} %basis_hbm.1), channel_id=1, source_target_pairs={{0,2},{1,3}} | collective-permute-start | bytes 393224 | tf_op jit(solution)/shard_map/ppermute | solution.py:284
  2.1 4.2 %collective-permute-done.lent_ref = f32[4,2,1,8,512]{4,3,2,1,0:T(8,128)S(1)} collective-permute-done((f32[4,2,1,8,512]{4,3,2,1,0:T(8,128)}, f32[4,2,1,8,512]{4,3,2,1,0:T(8,128)S(1)}, u32[]{:S(2)}, u32[]{:S(2)}) %collective-permute-start) | collective-permute-done | bytes 131104 | tf_op jit(solution)/shard_map/ppermute | solution.py:284
  6.3 1.6 %pack.1 = (f32[256,128]{1,0:T(8,128)S(1)}, f32[40,128]{1,0:T(8,128)S(1)}, f32[2,1,8,512]{3,2,1,0:T(8,128)S(1)}, bf16[2,2,256,256]{3,2,1,0:T(8,128)(2,1)S(1)}, f32[1,128]{1,0:T(1,128)S(1)}) custom-call(f32[2,1,8,512]{3,2,1,0:T(8,128)} %resid_hbm.1, f32[4,2,1,8,512]{4,3,2,1,0:T(8,128)} %basis_hbm.1, bf16[2,2,256,256]{3,2,1,0:T(8,128)(2,1)} %constant.16.tables_hbm, ...), custom_call_target="tpu_custom_call" | custom-call | tf_op jit(solution)/shard_map/pack/pallas_call | solution.py:285
  7.9 23.4 %all_to_all.22 = f32[256,1,128]{2,1,0:T(1,128)S(1)} all-to-all(f32[256,1,128]{2,1,0:T(1,128)S(1)} %bitcast.11), channel_id=1, replica_groups=mesh['tm'=128,'rows'=2] {'tm','rows'}, dimensions={0} | all-to-all | bytes 262144 | tf_op jit(solution)/shard_map/all_to_all | solution.py:302
  31.3 0.0 copy-done
  31.3 1.0 %solve.1 = f32[256,128]{1,0:T(8,128)S(1)} custom-call(f32[256,128]{1,0:T(8,128)S(1)} %bitcast.8, f32[40,128]{1,0:T(8,128)S(1)} %get-tuple-element.9.refs_1_, f32[1,128]{1,0:T(1,128)S(1)} %get-tuple-element.10.refs_2_, bf16[2,320,512]{2,1,0:T(8,128)(2,1)S(1)} %copy-done), custom_call_target="tpu_custom_call" | custom-call | tf_op jit(solution)/shard_map/solve/pallas_call | solution.py:303
  32.3 18.6 %all_to_all.23 = f32[256,1,128]{2,1,0:T(1,128)S(1)} all-to-all(f32[256,1,128]{2,1,0:T(1,128)S(1)} %bitcast.9), channel_id=1, replica_groups=mesh['tm'=128,'rows'=2] {'tm','rows'}, dimensions={0} | all-to-all | bytes 262144 | tf_op jit(solution)/shard_map/all_to_all | solution.py:309
  50.9 1.0 %unpack.1 = (f32[2,1,8,512]{3,2,1,0:T(8,128)}, f32[2,1,8,512]{3,2,1,0:T(8,128)}, f32[5]{0:T(128)}) custom-call(f32[256,128]{1,0:T(8,128)S(1)} %bitcast.10, f32[2,1,8,512]{3,2,1,0:T(8,128)S(1)} %get-tuple-element.11.resid_ref, bf16[2,2,256,256]{3,2,1,0:T(8,128)(2,1)S(1)} %get-tuple-element.12.tables_ref), custom_call_target="tpu_custom_call" | custom-call | tf_op jit(solution)/shard_map/unpack/pallas_call | solution.py:311
Async XLA Ops:
  0.6 30.7 %copy-start = (bf16[2,320,512]{2,1,0:T(8,128)(2,1)S(1)}, bf16[2,320,512]{2,1,0:T(8,128)(2,1)}, u32[]{:S(2)}) copy-start(bf16[2,320,512]{2,1,0:T(8,128)(2,1)} %constant.10.clone.refs_3_) | copy-start | bytes 1966084
  0.6 5.7 %collective-permute-start = (f32[4,2,1,8,512]{4,3,2,1,0:T(8,128)}, f32[4,2,1,8,512]{4,3,2,1,0:T(8,128)S(1)}, u32[]{:S(2)}, u32[]{:S(2)}) collective-permute-start(f32[4,2,1,8,512]{4,3,2,1,0:T(8,128)} %basis_hbm.1), channel_id=1, source_target_pairs={{0,2},{1,3}} | collective-permute-start | bytes 393224 | tf_op jit(solution)/shard_map/ppermute | solution.py:284

commit v9 on v8

--- a/solution.py
+++ b/solution.py
@@ -105,13 +105,14 @@
     return jnp.asarray(np.stack([high, (table - high.astype(np.float64)).astype(jnp.bfloat16)]))
 
 
+def dot(left, right, contract):
+    return lax.dot_general(left, right, (contract, ((), ())), preferred_element_type=jnp.float32)
+
+
 def product(left, right, contract=((1,), (0,))):
-    total = 0.0
-    for i, j in ((1, 0), (0, 1), (0, 0)):
-        total = total + lax.dot_general(
-            left[i], right[j], (contract, ((), ())), preferred_element_type=jnp.float32
-        )
-    return total
+    rows = left[0].shape[0]
+    both = dot(jnp.concatenate([left[0], left[1]], 0), right[0], contract)
+    return both[:rows] + (both[rows:] + dot(left[0], right[1], contract))
 
 
 def folded(flat, basis, lent, second):

time: 52.1 us -> 52.1 us (level)
  no operation moved by 1% of the time
where the time goes in v9:
time: 52.1 us; the launch traced here: 51.9 us
  blocking collectives  42 us (81%)
  waiting for transfers between devices  4.23 us (8%)
  Pallas kernels  3.52 us (7%)
  starting transfers between devices  1.42 us (3%)
  between operations  0.66 us (1%)
    all_to_all x1, blocking collectives, on_device(): recv = lax.all_to_all(send, axes, 0, 0, tiled=True)  23.4 us
    all_to_all x1, blocking collectives, on_device(): home = lax.all_to_all(back, axes, 0, 0, tiled=True)  18.6 us
    ppermute x1, waiting for transfers between devices, on_device(): lent = lax.ppermute(basis, 'tm', [(0, 1)])  4.23 us
    pallas_call x1, Pallas kernels, on_device(): pl.pallas_call(pack_kernel, in_specs=[hbm] * 4 + [vmem], out_shape=(messa...  1.57 us
    ppermute x1, starting transfers between devices, on_device(): lent = lax.ppermute(basis, 'tm', [(0, 1)])  1.42 us
  transfers between devices with their start and end apart: 1, of which 1 were waited for; matrix products, arithmetic and copies ran while one was open for 0% of the time, Pallas kernels for 0%

profile of v9, /device:TPU:1, one launch (start us, length us, event | category | flops | bytes accessed | tf_op | source)
XLA Modules:
  0.0 51.9 jit_solution(8407179003969172922)
XLA Ops:
  0.6 0.0 copy-start
  0.6 1.4 %collective-permute-start = (f32[4,2,1,8,512]{4,3,2,1,0:T(8,128)}, f32[4,2,1,8,512]{4,3,2,1,0:T(8,128)S(1)}, u32[]{:S(2)}, u32[]{:S(2)}) collective-permute-start(f32[4,2,1,8,512]{4,3,2,1,0:T(8,128)} %basis_hbm.1), channel_id=1, source_target_pairs={{0,2},{1,3}} | collective-permute-start | bytes 393224 | tf_op jit(solution)/shard_map/ppermute | solution.py:285
  2.1 4.2 %collective-permute-done.lent_ref = f32[4,2,1,8,512]{4,3,2,1,0:T(8,128)S(1)} collective-permute-done((f32[4,2,1,8,512]{4,3,2,1,0:T(8,128)}, f32[4,2,1,8,512]{4,3,2,1,0:T(8,128)S(1)}, u32[]{:S(2)}, u32[]{:S(2)}) %collective-permute-start) | collective-permute-done | bytes 131104 | tf_op jit(solution)/shard_map/ppermute | solution.py:285
  6.3 1.6 %pack.1 = (f32[256,128]{1,0:T(8,128)S(1)}, f32[40,128]{1,0:T(8,128)S(1)}, f32[2,1,8,512]{3,2,1,0:T(8,128)S(1)}, bf16[2,2,256,256]{3,2,1,0:T(8,128)(2,1)S(1)}, f32[1,128]{1,0:T(1,128)S(1)}) custom-call(f32[2,1,8,512]{3,2,1,0:T(8,128)} %resid_hbm.1, f32[4,2,1,8,512]{4,3,2,1,0:T(8,128)} %basis_hbm.1, bf16[2,2,256,256]{3,2,1,0:T(8,128)(2,1)} %constant.16.tables_hbm, ...), custom_call_target="tpu_custom_call" | custom-call | tf_op jit(solution)/shard_map/pack/pallas_call | solution.py:286
  7.9 23.4 %all_to_all.22 = f32[256,1,128]{2,1,0:T(1,128)S(1)} all-to-all(f32[256,1,128]{2,1,0:T(1,128)S(1)} %bitcast.11), channel_id=1, replica_groups=mesh['tm'=128,'rows'=2] {'tm','rows'}, dimensions={0} | all-to-all | bytes 262144 | tf_op jit(solution)/shard_map/all_to_all | solution.py:303
  31.3 0.0 copy-done
  31.3 1.0 %solve.1 = f32[256,128]{1,0:T(8,128)S(1)} custom-call(f32[256,128]{1,0:T(8,128)S(1)} %bitcast.8, f32[40,128]{1,0:T(8,128)S(1)} %get-tuple-element.9.refs_1_, f32[1,128]{1,0:T(1,128)S(1)} %get-tuple-element.10.refs_2_, bf16[2,320,512]{2,1,0:T(8,128)(2,1)S(1)} %copy-done), custom_call_target="tpu_custom_call" | custom-call | tf_op jit(solution)/shard_map/solve/pallas_call | solution.py:304
  32.3 18.6 %all_to_all.23 = f32[256,1,128]{2,1,0:T(1,128)S(1)} all-to-all(f32[256,1,128]{2,1,0:T(1,128)S(1)} %bitcast.9), channel_id=1, replica_groups=mesh['tm'=128,'rows'=2] {'tm','rows'}, dimensions={0} | all-to-all | bytes 262144 | tf_op jit(solution)/shard_map/all_to_all | solution.py:310
  50.9 1.0 %unpack.1 = (f32[2,1,8,512]{3,2,1,0:T(8,128)}, f32[2,1,8,512]{3,2,1,0:T(8,128)}, f32[5]{0:T(128)}) custom-call(f32[256,128]{1,0:T(8,128)S(1)} %bitcast.10, f32[2,1,8,512]{3,2,1,0:T(8,128)S(1)} %get-tuple-element.11.resid_ref, bf16[2,2,256,256]{3,2,1,0:T(8,128)(2,1)S(1)} %get-tuple-element.12.tables_ref), custom_call_target="tpu_custom_call" | custom-call | tf_op jit(solution)/shard_map/unpack/pallas_call | solution.py:312
Async XLA Ops:
  0.6 30.7 %copy-start = (bf16[2,320,512]{2,1,0:T(8,128)(2,1)S(1)}, bf16[2,320,512]{2,1,0:T(8,128)(2,1)}, u32[]{:S(2)}) copy-start(bf16[2,320,512]{2,1,0:T(8,128)(2,1)} %constant.10.clone.refs_3_) | copy-start | bytes 1966084
  0.6 5.7 %collective-permute-start = (f32[4,2,1,8,512]{4,3,2,1,0:T(8,128)}, f32[4,2,1,8,512]{4,3,2,1,0:T(8,128)S(1)}, u32[]{:S(2)}, u32[]{:S(2)}) collective-permute-start(f32[4,2,1,8,512]{4,3,2,1,0:T(8,128)} %basis_hbm.1), channel_id=1, source_target_pairs={{0,2},{1,3}} | collective-permute-start | bytes 393224 | tf_op jit(solution)/shard_map/ppermute | solution.py:285

commit v10 on v9

--- a/solution.py
+++ b/solution.py
@@ -59,20 +59,32 @@
     return np.concatenate(tables, 1)
 
 
-def column_numbers(cols):
-    return [2.0 * np.arange(cols // 2) + 1 + dc for dc in range(2)]
-
-
-def column_tables(cols):
-    return [sines(n, np.arange(cols // 2), cols) for n in column_numbers(cols)]
-
-
-def symbol_table(cols):
-    rows = 2.0 * np.cos(np.pi * (np.arange(MODES) + 1) / (MODES + 1))
-    sums = []
-    for number in column_numbers(cols):
-        sums.append(2.0 * np.cos(np.pi * number / (cols + 1))[:, None] + rows[None, :])
-    return np.tile(np.concatenate(sums, 1), (1, LANES // GROUP)).astype(np.float32)
+def sine(turns, half):
+    left = turns - jnp.floor(turns * (0.5 / half)) * (2.0 * half) - half
+    near = jnp.abs(left)
+    angle = jnp.minimum(near, half - near) * (np.pi / half)
+    square = angle * angle
+    series = jnp.full_like(square, -2.3889859e-8)
+    for term in (2.7525562e-6, -1.9840874e-4, 8.3333310e-3, -1.6666667e-1, 1.0):
+        series = series * square + term
+    value = angle * series
+    return jnp.where(left < 0.0, value, -value)
+
+
+def column_table(half, dc):
+    shape = (half, half)
+    number = (2 * row_of(shape) + 1 + dc).astype(jnp.float32)
+    place = (lane_of(shape) + 1).astype(jnp.float32)
+    length = 2.0 * half + 1.0
+    return sine(number * place, length) * np.sqrt(2.0 / length)
+
+
+def symbol_of(block, cols):
+    lane = lane_of((1, LANES))
+    number = (2 * block + 1 + lane % GROUP // MODES).astype(jnp.float32)
+    mode = (lane % MODES + 1).astype(jnp.float32)
+    length, height = cols + 1.0, MODES + 1.0
+    return 2.0 * (sine(number + 0.5 * length, length) + sine(mode + 0.5 * height, height))
 
 
 def row_tables():
@@ -217,40 +229,39 @@
 
 
 def pack_kernel(
-    resid_hbm, basis_hbm, tables_hbm, symbol_hbm, lent_ref,
-    send_ref, own_ref, resid_ref, tables_ref, symbol_ref, basis_ref, sems,
+    resid_hbm, basis_hbm, later_hbm, lent_ref,
+    send_ref, own_ref, resid_ref, tables_ref, later_ref, basis_ref, sems,
 ):
-    pairs = (
-        (resid_hbm, resid_ref),
-        (basis_hbm, basis_ref),
-        (tables_hbm, tables_ref),
-        (symbol_hbm.at[pl.ds(device_index(), 1)], symbol_ref),
-    )
+    pairs = ((resid_hbm, resid_ref), (basis_hbm, basis_ref), (later_hbm, later_ref))
     copies = [pltpu.make_async_copy(a, b, sems.at[i]) for i, (a, b) in enumerate(pairs)]
     for copy in copies:
         copy.start()
     second = lax.axis_index("tm") == 1
-    copies[0].wait()
-    copies[1].wait()
+    tables = []
+    for dc in range(2):
+        tables.append(halves(column_table(tables_ref.shape[2], dc)))
+        for part in range(2):
+            tables_ref[dc, part] = tables[dc][part]
+    for copy in copies[:2]:
+        copy.wait()
     flat = resid_ref[...].reshape(MODES, resid_ref.shape[-1])
     basis = basis_ref[:, :, 0]
     folds = folded(flat, basis, lent_ref[2:, 0, 0], second)
     own_ref[...] = own_products(flat, basis)
-    copies[2].wait()
     sides = [turned_to_modes(folds[dc], tables_ref[dc]) for dc in range(2)]
     send_ref[...] = jnp.concatenate(sides, 1)
-    copies[3].wait()
+    copies[2].wait()
 
 
 def solve_kernel(
-    kappa, count, steps, recv_ref, own_ref, symbol_ref, tables_ref, send_ref
+    kappa, count, steps, cols, recv_ref, own_ref, tables_ref, send_ref
 ):
     time, leave = tables_ref[:, :steps], tables_ref[:, steps : steps + LANES]
     stored = tables_ref[:, steps + LANES :]
     enter = jnp.concatenate([stored[:, :, at : at + LANES] for at in range(0, 4 * LANES, LANES)], 1)
     parts = [recv_ref[pl.ds(h, steps, stride=2), :] for h in range(2)]
     outs = solved(
-        parts, own_ref[...], symbol_ref[...], time, enter, leave, kappa, count
+        parts, own_ref[...], symbol_of(device_index(), cols), time, enter, leave, kappa, count
     )
     for h, out in enumerate(outs):
         send_ref[pl.ds(h, steps, stride=2), :] = out
@@ -275,38 +286,36 @@
         cols = resid.shape[3]
         kappa = coupling(steps)
         count = 2.0 * steps * MODES * cols
-        tables = jnp.stack([both_halves(t) for t in column_tables(cols)])
         solve_tables = both_halves(np.concatenate([time_table(steps), *row_tables()], 0))
         vmem = pl.BlockSpec(memory_space=pltpu.VMEM)
         hbm = pl.BlockSpec(memory_space=pltpu.HBM)
-        symbol = jnp.asarray(symbol_table(cols))
-        placed = [pltpu.with_memory_space_constraint(a, pltpu.HBM) for a in (resid, basis, tables, symbol)]
+        placed = [pltpu.with_memory_space_constraint(a, pltpu.HBM) for a in (resid, basis, solve_tables)]
         message = jax.ShapeDtypeStruct((devices, LANES), jnp.float32)
         lent = lax.ppermute(basis, "tm", [(0, 1)])
-        send, own, kept, tables, symbol = pl.pallas_call(
+        send, own, kept, tables, solve_tables = pl.pallas_call(
             pack_kernel,
-            in_specs=[hbm] * 4 + [vmem],
+            in_specs=[hbm, hbm, hbm, vmem],
             out_shape=(
                 message,
                 jax.ShapeDtypeStruct(((KRYLOV + 1) * ROWS, LANES), jnp.float32),
                 jax.ShapeDtypeStruct(resid.shape, jnp.float32),
-                jax.ShapeDtypeStruct(tables.shape, tables.dtype),
-                jax.ShapeDtypeStruct((1, LANES), jnp.float32),
+                jax.ShapeDtypeStruct((2, 2, cols // 2, cols // 2), jnp.bfloat16),
+                jax.ShapeDtypeStruct(solve_tables.shape, jnp.bfloat16),
             ),
             scratch_shapes=[
                 pltpu.VMEM(basis.shape, jnp.float32),
-                pltpu.SemaphoreType.DMA((4,)),
+                pltpu.SemaphoreType.DMA((3,)),
             ],
             compiler_params=params,
             name="pack",
         )(*placed, lent)
         recv = lax.all_to_all(send, axes, 0, 0, tiled=True)
         back = pl.pallas_call(
-            lambda *refs: solve_kernel(kappa, count, steps, *refs),
+            lambda *refs: solve_kernel(kappa, count, steps, cols, *refs),
             out_shape=message,
             compiler_params=params,
             name="solve",
-        )(recv, own, symbol, solve_tables)
+        )(recv, own, solve_tables)
         home = lax.all_to_all(back, axes, 0, 0, tiled=True)
         shard = jax.ShapeDtypeStruct(resid.shape, jnp.float32)
         precond, image, gram = pl.pallas_call(

time: 52.1 us -> 51.8 us (level)
  no operation moved by 1% of the time
where the time goes in v10:
time: 51.8 us; the launch traced here: 51.6 us
  blocking collectives  42 us (81%)
  waiting for transfers between devices  4.23 us (8%)
  Pallas kernels  3.39 us (7%)
  starting transfers between devices  1.29 us (2%)
  between operations  0.66 us (1%)
    all_to_all x1, blocking collectives, on_device(): recv = lax.all_to_all(send, axes, 0, 0, tiled=True)  23.4 us
    all_to_all x1, blocking collectives, on_device(): home = lax.all_to_all(back, axes, 0, 0, tiled=True)  18.6 us
    ppermute x1, waiting for transfers between devices, on_device(): lent = lax.ppermute(basis, 'tm', [(0, 1)])  4.23 us
    pallas_call x1, Pallas kernels, on_device(): pl.pallas_call(pack_kernel, in_specs=[hbm, hbm, hbm, vmem], out_shape=(me...  1.44 us
    ppermute x1, starting transfers between devices, on_device(): lent = lax.ppermute(basis, 'tm', [(0, 1)])  1.29 us
  transfers between devices with their start and end apart: 1, of which 1 were waited for; matrix products, arithmetic and copies ran while one was open for 0% of the time, Pallas kernels for 0%

profile of v10, /device:TPU:1, one launch (start us, length us, event | category | flops | bytes accessed | tf_op | source)
XLA Modules:
  0.0 51.6 jit_solution(3855879360342568511)
XLA Ops:
  0.6 1.3 %collective-permute-start = (f32[4,2,1,8,512]{4,3,2,1,0:T(8,128)}, f32[4,2,1,8,512]{4,3,2,1,0:T(8,128)S(1)}, u32[]{:S(2)}, u32[]{:S(2)}) collective-permute-start(f32[4,2,1,8,512]{4,3,2,1,0:T(8,128)} %basis_hbm.1), channel_id=1, source_target_pairs={{0,2},{1,3}} | collective-permute-start | bytes 393224 | tf_op jit(solution)/shard_map/ppermute | solution.py:294
  1.9 4.2 %collective-permute-done.lent_ref = f32[4,2,1,8,512]{4,3,2,1,0:T(8,128)S(1)} collective-permute-done((f32[4,2,1,8,512]{4,3,2,1,0:T(8,128)}, f32[4,2,1,8,512]{4,3,2,1,0:T(8,128)S(1)}, u32[]{:S(2)}, u32[]{:S(2)}) %collective-permute-start) | collective-permute-done | bytes 131104 | tf_op jit(solution)/shard_map/ppermute | solution.py:294
  6.2 1.4 %pack.1 = (f32[256,128]{1,0:T(8,128)S(1)}, f32[40,128]{1,0:T(8,128)S(1)}, f32[2,1,8,512]{3,2,1,0:T(8,128)S(1)}, bf16[2,2,256,256]{3,2,1,0:T(8,128)(2,1)S(1)}, bf16[2,320,512]{2,1,0:T(8,128)(2,1)S(1)}) custom-call(f32[2,1,8,512]{3,2,1,0:T(8,128)} %resid_hbm.1, f32[4,2,1,8,512]{4,3,2,1,0:T(8,128)} %basis_hbm.1, bf16[2,320,512]{2,1,0:T(8,128)(2,1)} %constant.2.clone.later_hbm, ...), custom_call_target="tpu_custom_call" | custom-call | tf_op jit(solution)/shard_map/pack/pallas_call | solution.py:295
  7.6 23.4 %all_to_all.22 = f32[256,1,128]{2,1,0:T(1,128)S(1)} all-to-all(f32[256,1,128]{2,1,0:T(1,128)S(1)} %bitcast.11), channel_id=1, replica_groups=mesh['tm'=128,'rows'=2] {'tm','rows'}, dimensions={0} | all-to-all | bytes 262144 | tf_op jit(solution)/shard_map/all_to_all | solution.py:312
  31.0 1.0 %solve.1 = f32[256,128]{1,0:T(8,128)S(1)} custom-call(f32[256,128]{1,0:T(8,128)S(1)} %bitcast.8, f32[40,128]{1,0:T(8,128)S(1)} %get-tuple-element.9.refs_1_, bf16[2,320,512]{2,1,0:T(8,128)(2,1)S(1)} %get-tuple-element.10.refs_2_), custom_call_target="tpu_custom_call" | custom-call | tf_op jit(solution)/shard_map/solve/pallas_call | solution.py:313
  32.0 18.6 %all_to_all.23 = f32[256,1,128]{2,1,0:T(1,128)S(1)} all-to-all(f32[256,1,128]{2,1,0:T(1,128)S(1)} %bitcast.9), channel_id=1, replica_groups=mesh['tm'=128,'rows'=2] {'tm','rows'}, dimensions={0} | all-to-all | bytes 262144 | tf_op jit(solution)/shard_map/all_to_all | solution.py:319
  50.6 1.0 %unpack.1 = (f32[2,1,8,512]{3,2,1,0:T(8,128)}, f32[2,1,8,512]{3,2,1,0:T(8,128)}, f32[5]{0:T(128)}) custom-call(f32[256,128]{1,0:T(8,128)S(1)} %bitcast.10, f32[2,1,8,512]{3,2,1,0:T(8,128)S(1)} %get-tuple-element.11.resid_ref, bf16[2,2,256,256]{3,2,1,0:T(8,128)(2,1)S(1)} %get-tuple-element.12.tables_ref), custom_call_target="tpu_custom_call" | custom-call | tf_op jit(solution)/shard_map/unpack/pallas_call | solution.py:321
Async XLA Ops:
  0.6 5.5 %collective-permute-start = (f32[4,2,1,8,512]{4,3,2,1,0:T(8,128)}, f32[4,2,1,8,512]{4,3,2,1,0:T(8,128)S(1)}, u32[]{:S(2)}, u32[]{:S(2)}) collective-permute-start(f32[4,2,1,8,512]{4,3,2,1,0:T(8,128)} %basis_hbm.1), channel_id=1, source_target_pairs={{0,2},{1,3}} | collective-permute-start | bytes 393224 | tf_op jit(solution)/shard_map/ppermute | solution.py:294

commit v11 on v10

--- a/solution.py
+++ b/solution.py
@@ -89,22 +89,36 @@
 
 def row_tables():
     wave = sines(np.arange(MODES) + 1, np.arange(MODES), MODES)
-    enter = np.zeros((2, LANES, LANES))
+    enter = np.zeros((2, LANES, GROUP))
     leave = np.zeros((LANES, 2, 2, LANES))
     for h in range(2):
         for row in range(ROWS):
             for dc in range(2):
                 value = wave[:, h * ROWS + row]
                 modes = dc * MODES + np.arange(MODES)
-                for group in range(0, LANES, GROUP):
-                    for c in range(2):
-                        enter[h, dc * SIDE + c * ROWS + row, group + modes] = value
+                enter[h, dc * SIDE + ROWS + row, modes] = value
                 for field, group in enumerate((0, 2, 1, 3)):
                     leave[group * GROUP + modes, 0, h, dc * SIDE + field * ROWS + row] = value
                 for slot in (1, *range(KRYLOV, 2 * KRYLOV)):
                     leave[GROUP + modes, 1, h, dc * SIDE + slot * ROWS + row] = value
+    return enter.reshape(2 * LANES, GROUP), leave.reshape(LANES, 4 * LANES)
+
+
+def cut_up(table, count):
+    pieces = []
+    for _ in range(count):
+        pieces.append(table.astype(jnp.bfloat16))
+        table = table - pieces[-1].astype(np.float64)
+    return pieces
+
+
+def solve_constants(steps):
+    enter, leave = row_tables()
+    pieces = cut_up(enter, 3)
+    enter = np.concatenate([*pieces, np.zeros_like(pieces[0])], 1)
     enter = enter.reshape(4, SIDE, LANES).transpose(1, 0, 2).reshape(SIDE, 4 * LANES)
-    return leave.reshape(LANES, 4 * LANES), enter
+    rows = [*cut_up(time_table(steps), 3), *cut_up(leave, 2), enter]
+    return jnp.asarray(np.concatenate(rows, 0))
 
 
 def halves(value):
@@ -112,9 +126,28 @@
     return high, (value - high.astype(jnp.float32)).astype(jnp.bfloat16)
 
 
-def both_halves(table):
-    high = table.astype(jnp.bfloat16)
-    return jnp.asarray(np.stack([high, (table - high.astype(np.float64)).astype(jnp.bfloat16)]))
+def thirds(value):
+    high, low = halves(value)
+    rest = value - high.astype(jnp.float32) - low.astype(jnp.float32)
+    return high, low, rest.astype(jnp.bfloat16)
+
+
+def third_by_group(value):
+    group = lane_of(value.shape) // GROUP
+    first = value - value.astype(jnp.bfloat16).astype(jnp.float32)
+    second = first - first.astype(jnp.bfloat16).astype(jnp.float32)
+    chosen = jnp.where(group == 0, value, jnp.where(group == 1, first, second))
+    return jnp.where(group == 3, 0.0, chosen).astype(jnp.bfloat16)
+
+
+def groups_added(value):
+    value = value + roll(value, 2 * GROUP, 1)
+    return value + roll(value, GROUP, 1)
+
+
+def thirds_added(value):
+    rows = value.shape[0] // 3
+    return value[:rows] + (value[rows : 2 * rows] + value[2 * rows :])
 
 
 def dot(left, right, contract):
@@ -132,11 +165,19 @@
     mixed = [jnp.where(second, lent[i], basis[i, 0]) for i in range(2)]
     whole = jnp.concatenate([flat] + mixed + [basis[i, 1] for i in range(KRYLOV)], 0)
     left, right = whole[:, :half], reversed_lanes(whole[:, half:])
-    return [halves(left + right), halves(left - right)]
-
-
-def turned_to_modes(fold, table):
-    return product(table, fold, ((1,), (1,)))
+    return [left + right, left - right]
+
+
+def turned_to_modes(folds, tables):
+    turned = []
+    for fold, table in zip(folds, tables):
+        pieces = jnp.concatenate([*thirds(fold), jnp.zeros(fold.shape, jnp.bfloat16)], 0)
+        half = table.shape[1]
+        parts = dot(table.reshape(2 * half, half), pieces, ((1,), (1,)))
+        parts = parts[:half] + parts[half:]
+        parts = parts[:, :LANES] + parts[:, LANES:]
+        turned.append(parts + roll(parts, SIDE, 1))
+    return jnp.where(lane_of(turned[0].shape) < SIDE, *turned)
 
 
 def own_products(flat, basis):
@@ -156,21 +197,24 @@
     steps = parts[0].shape[0]
     shape = (steps, LANES)
     lane, row = lane_of(shape), row_of(shape)
-    is_disp = lane % SIDE < ROWS
-    mixed = [jnp.where(is_disp, x - delayed(x), x) for x in parts]
-    source = product(halves(jnp.concatenate(mixed, 1)), enter)
+    is_velo = lane % SIDE // ROWS == 1
+    mixed = [jnp.where(is_velo, x + roll(x - delayed(x), ROWS, 1), 0.0) for x in parts]
+    pieces = jnp.concatenate(thirds(jnp.concatenate(mixed, 1)), 0)
+    source = groups_added(thirds_added(dot(pieces, enter, ((1,), (0,)))))
     line = lane_of((1, LANES))
-    cut = line // GROUP == 1
-    power, weights = jnp.ones((1, LANES), jnp.float32), []
+    power, stack = jnp.ones((1, LANES), jnp.float32), []
     for m in range(SWEEPS):
-        last = -kappa * power * symbol if m == SWEEPS - 1 else 0.0
-        weights.append(jnp.where(cut, last, power))
+        stack.append(third_by_group(source * power))
         power = power * symbol
-    stack = jnp.concatenate([source * weight for weight in weights], 0)
-    found = product(time, halves(stack))
+    blank = jnp.zeros(((SWEEPS - 1) * steps, LANES), jnp.bfloat16)
+    last = jnp.concatenate([blank, third_by_group(source * (-kappa * power))], 0)
+    stack = jnp.concatenate([jnp.concatenate(stack, 0), last], 1)
+    found = thirds_added(dot(time, stack, ((1,), (0,))))
+    gone = groups_added(found[:, LANES:])
+    found = groups_added(found[:, :LANES])
     late = delayed(found)
     group = lane // GROUP
-    found = jnp.where(group == 2, found - late, found)
+    found = jnp.where(group == 1, gone, jnp.where(group == 2, found - late, found))
     found = jnp.where(group == 3, jnp.where(row == 0, late, 0.0), found)
     spread = product(halves(found), leave)
     at = line % SIDE
@@ -237,28 +281,26 @@
     for copy in copies:
         copy.start()
     second = lax.axis_index("tm") == 1
-    tables = []
     for dc in range(2):
-        tables.append(halves(column_table(tables_ref.shape[2], dc)))
-        for part in range(2):
-            tables_ref[dc, part] = tables[dc][part]
+        for part, table in enumerate(halves(column_table(tables_ref.shape[2], dc))):
+            tables_ref[dc, part] = table
     for copy in copies[:2]:
         copy.wait()
     flat = resid_ref[...].reshape(MODES, resid_ref.shape[-1])
     basis = basis_ref[:, :, 0]
     folds = folded(flat, basis, lent_ref[2:, 0, 0], second)
     own_ref[...] = own_products(flat, basis)
-    sides = [turned_to_modes(folds[dc], tables_ref[dc]) for dc in range(2)]
-    send_ref[...] = jnp.concatenate(sides, 1)
+    send_ref[...] = turned_to_modes(folds, [tables_ref[dc] for dc in range(2)])
     copies[2].wait()
 
 
 def solve_kernel(
     kappa, count, steps, cols, recv_ref, own_ref, tables_ref, send_ref
 ):
-    time, leave = tables_ref[:, :steps], tables_ref[:, steps : steps + LANES]
-    stored = tables_ref[:, steps + LANES :]
-    enter = jnp.concatenate([stored[:, :, at : at + LANES] for at in range(0, 4 * LANES, LANES)], 1)
+    time = tables_ref[: 3 * steps]
+    leave = [tables_ref[at : at + LANES] for at in (3 * steps, 3 * steps + LANES)]
+    stored = tables_ref[3 * steps + 2 * LANES :]
+    enter = jnp.concatenate([stored[:, at : at + LANES] for at in range(0, 4 * LANES, LANES)], 0)
     parts = [recv_ref[pl.ds(h, steps, stride=2), :] for h in range(2)]
     outs = solved(
         parts, own_ref[...], symbol_of(device_index(), cols), time, enter, leave, kappa, count
@@ -286,7 +328,7 @@
         cols = resid.shape[3]
         kappa = coupling(steps)
         count = 2.0 * steps * MODES * cols
-        solve_tables = both_halves(np.concatenate([time_table(steps), *row_tables()], 0))
+        solve_tables = solve_constants(steps)
         vmem = pl.BlockSpec(memory_space=pltpu.VMEM)
         hbm = pl.BlockSpec(memory_space=pltpu.HBM)
         placed = [pltpu.with_memory_space_constraint(a, pltpu.HBM) for a in (resid, basis, solve_tables)]

time: 51.8 us -> 52.2 us (level)
  no operation moved by 1% of the time
where the time goes in v11:
time: 52.2 us; the launch traced here: 52 us
  blocking collectives  42 us (80%)
  waiting for transfers between devices  4.23 us (8%)
  Pallas kernels  3.85 us (7%)
  starting transfers between devices  1.29 us (2%)
  between operations  0.66 us (1%)
    all_to_all x1, blocking collectives, on_device(): recv = lax.all_to_all(send, axes, 0, 0, tiled=True)  23.4 us
    all_to_all x1, blocking collectives, on_device(): home = lax.all_to_all(back, axes, 0, 0, tiled=True)  18.6 us
    ppermute x1, waiting for transfers between devices, on_device(): lent = lax.ppermute(basis, 'tm', [(0, 1)])  4.23 us
    pallas_call x1, Pallas kernels, on_device(): pl.pallas_call(lambda *refs: solve_kernel(kappa, count, steps, cols, *ref...  1.47 us
    pallas_call x1, Pallas kernels, on_device(): pl.pallas_call(pack_kernel, in_specs=[hbm, hbm, hbm, vmem], out_shape=(me...  1.42 us
    ppermute x1, starting transfers between devices, on_device(): lent = lax.ppermute(basis, 'tm', [(0, 1)])  1.29 us
  transfers between devices with their start and end apart: 1, of which 1 were waited for; matrix products, arithmetic and copies ran while one was open for 0% of the time, Pallas kernels for 0%

profile of v11, /device:TPU:1, one launch (start us, length us, event | category | flops | bytes accessed | tf_op | source)
XLA Modules:
  0.0 52.0 jit_solution(1289760360360693579)
XLA Ops:
  0.6 1.3 %collective-permute-start = (f32[4,2,1,8,512]{4,3,2,1,0:T(8,128)}, f32[4,2,1,8,512]{4,3,2,1,0:T(8,128)S(1)}, u32[]{:S(2)}, u32[]{:S(2)}) collective-permute-start(f32[4,2,1,8,512]{4,3,2,1,0:T(8,128)} %basis_hbm.1), channel_id=1, source_target_pairs={{0,2},{1,3}} | collective-permute-start | bytes 393224 | tf_op jit(solution)/shard_map/ppermute | solution.py:336
  1.9 4.2 %collective-permute-done.lent_ref = f32[4,2,1,8,512]{4,3,2,1,0:T(8,128)S(1)} collective-permute-done((f32[4,2,1,8,512]{4,3,2,1,0:T(8,128)}, f32[4,2,1,8,512]{4,3,2,1,0:T(8,128)S(1)}, u32[]{:S(2)}, u32[]{:S(2)}) %collective-permute-start) | collective-permute-done | bytes 131104 | tf_op jit(solution)/shard_map/ppermute | solution.py:336
  6.2 1.4 %pack.1 = (f32[256,128]{1,0:T(8,128)S(1)}, f32[40,128]{1,0:T(8,128)S(1)}, f32[2,1,8,512]{3,2,1,0:T(8,128)S(1)}, bf16[2,2,256,256]{3,2,1,0:T(8,128)(2,1)S(1)}, bf16[704,512]{1,0:T(8,128)(2,1)S(1)}) custom-call(f32[2,1,8,512]{3,2,1,0:T(8,128)} %resid_hbm.1, f32[4,2,1,8,512]{4,3,2,1,0:T(8,128)} %basis_hbm.1, bf16[704,512]{1,0:T(8,128)(2,1)} %constant.2.clone.later_hbm, ...), custom_call_target="tpu_custom_call" | custom-call | tf_op jit(solution)/shard_map/pack/pallas_call | solution.py:337
  7.6 23.4 %all_to_all.22 = f32[256,1,128]{2,1,0:T(1,128)S(1)} all-to-all(f32[256,1,128]{2,1,0:T(1,128)S(1)} %bitcast.11), channel_id=1, replica_groups=mesh['tm'=128,'rows'=2] {'tm','rows'}, dimensions={0} | all-to-all | bytes 262144 | tf_op jit(solution)/shard_map/all_to_all | solution.py:354
  31.0 1.5 %solve.1 = f32[256,128]{1,0:T(8,128)S(1)} custom-call(f32[256,128]{1,0:T(8,128)S(1)} %bitcast.8, f32[40,128]{1,0:T(8,128)S(1)} %get-tuple-element.9.refs_1_, bf16[704,512]{1,0:T(8,128)(2,1)S(1)} %get-tuple-element.10.refs_2_), custom_call_target="tpu_custom_call" | custom-call | tf_op jit(solution)/shard_map/solve/pallas_call | solution.py:355
  32.4 18.6 %all_to_all.23 = f32[256,1,128]{2,1,0:T(1,128)S(1)} all-to-all(f32[256,1,128]{2,1,0:T(1,128)S(1)} %bitcast.9), channel_id=1, replica_groups=mesh['tm'=128,'rows'=2] {'tm','rows'}, dimensions={0} | all-to-all | bytes 262144 | tf_op jit(solution)/shard_map/all_to_all | solution.py:361
  51.1 1.0 %unpack.1 = (f32[2,1,8,512]{3,2,1,0:T(8,128)}, f32[2,1,8,512]{3,2,1,0:T(8,128)}, f32[5]{0:T(128)}) custom-call(f32[256,128]{1,0:T(8,128)S(1)} %bitcast.10, f32[2,1,8,512]{3,2,1,0:T(8,128)S(1)} %get-tuple-element.11.resid_ref, bf16[2,2,256,256]{3,2,1,0:T(8,128)(2,1)S(1)} %get-tuple-element.12.tables_ref), custom_call_target="tpu_custom_call" | custom-call | tf_op jit(solution)/shard_map/unpack/pallas_call | solution.py:363
Async XLA Ops:
  0.6 5.5 %collective-permute-start = (f32[4,2,1,8,512]{4,3,2,1,0:T(8,128)}, f32[4,2,1,8,512]{4,3,2,1,0:T(8,128)S(1)}, u32[]{:S(2)}, u32[]{:S(2)}) collective-permute-start(f32[4,2,1,8,512]{4,3,2,1,0:T(8,128)} %basis_hbm.1), channel_id=1, source_target_pairs={{0,2},{1,3}} | collective-permute-start | bytes 393224 | tf_op jit(solution)/shard_map/ppermute | solution.py:336

commit v12 on v11

--- a/solution.py
+++ b/solution.py
@@ -202,16 +202,15 @@
     pieces = jnp.concatenate(thirds(jnp.concatenate(mixed, 1)), 0)
     source = groups_added(thirds_added(dot(pieces, enter, ((1,), (0,)))))
     line = lane_of((1, LANES))
-    power, stack = jnp.ones((1, LANES), jnp.float32), []
+    source = third_by_group(source)
+    power, found = 1.0, 0.0
     for m in range(SWEEPS):
-        stack.append(third_by_group(source * power))
+        part = dot(time[:, m * steps : (m + 1) * steps], source, ((1,), (0,)))
+        part = thirds_added(part) * power
+        found = found + part
         power = power * symbol
-    blank = jnp.zeros(((SWEEPS - 1) * steps, LANES), jnp.bfloat16)
-    last = jnp.concatenate([blank, third_by_group(source * (-kappa * power))], 0)
-    stack = jnp.concatenate([jnp.concatenate(stack, 0), last], 1)
-    found = thirds_added(dot(time, stack, ((1,), (0,))))
-    gone = groups_added(found[:, LANES:])
-    found = groups_added(found[:, :LANES])
+    gone = groups_added(part * (-kappa * symbol))
+    found = groups_added(found)
     late = delayed(found)
     group = lane // GROUP
     found = jnp.where(group == 1, gone, jnp.where(group == 2, found - late, found))

time: 52.2 us -> 52.1 us (level)
  no operation moved by 1% of the time
where the time goes in v12:
time: 52.1 us; the launch traced here: 52 us
  blocking collectives  42 us (81%)
  waiting for transfers between devices  4.23 us (8%)
  Pallas kernels  3.77 us (7%)
  starting transfers between devices  1.29 us (2%)
  between operations  0.66 us (1%)
    all_to_all x1, blocking collectives, on_device(): recv = lax.all_to_all(send, axes, 0, 0, tiled=True)  23.4 us
    all_to_all x1, blocking collectives, on_device(): home = lax.all_to_all(back, axes, 0, 0, tiled=True)  18.6 us
    ppermute x1, waiting for transfers between devices, on_device(): lent = lax.ppermute(basis, 'tm', [(0, 1)])  4.23 us
    pallas_call x1, Pallas kernels, on_device(): pl.pallas_call(pack_kernel, in_specs=[hbm, hbm, hbm, vmem], out_shape=(me...  1.42 us
    pallas_call x1, Pallas kernels, on_device(): pl.pallas_call(lambda *refs: solve_kernel(kappa, count, steps, cols, *ref...  1.39 us
    ppermute x1, starting transfers between devices, on_device(): lent = lax.ppermute(basis, 'tm', [(0, 1)])  1.29 us
  transfers between devices with their start and end apart: 1, of which 1 were waited for; matrix products, arithmetic and copies ran while one was open for 0% of the time, Pallas kernels for 0%

profile of v12, /device:TPU:1, one launch (start us, length us, event | category | flops | bytes accessed | tf_op | source)
XLA Modules:
  0.0 52.0 jit_solution(2837247774065142476)
XLA Ops:
  0.6 1.3 %collective-permute-start = (f32[4,2,1,8,512]{4,3,2,1,0:T(8,128)}, f32[4,2,1,8,512]{4,3,2,1,0:T(8,128)S(1)}, u32[]{:S(2)}, u32[]{:S(2)}) collective-permute-start(f32[4,2,1,8,512]{4,3,2,1,0:T(8,128)} %basis_hbm.1), channel_id=1, source_target_pairs={{0,2},{1,3}} | collective-permute-start | bytes 393224 | tf_op jit(solution)/shard_map/ppermute | solution.py:335
  1.9 4.2 %collective-permute-done.lent_ref = f32[4,2,1,8,512]{4,3,2,1,0:T(8,128)S(1)} collective-permute-done((f32[4,2,1,8,512]{4,3,2,1,0:T(8,128)}, f32[4,2,1,8,512]{4,3,2,1,0:T(8,128)S(1)}, u32[]{:S(2)}, u32[]{:S(2)}) %collective-permute-start) | collective-permute-done | bytes 131104 | tf_op jit(solution)/shard_map/ppermute | solution.py:335
  6.2 1.4 %pack.1 = (f32[256,128]{1,0:T(8,128)S(1)}, f32[40,128]{1,0:T(8,128)S(1)}, f32[2,1,8,512]{3,2,1,0:T(8,128)S(1)}, bf16[2,2,256,256]{3,2,1,0:T(8,128)(2,1)S(1)}, bf16[704,512]{1,0:T(8,128)(2,1)S(1)}) custom-call(f32[2,1,8,512]{3,2,1,0:T(8,128)} %resid_hbm.1, f32[4,2,1,8,512]{4,3,2,1,0:T(8,128)} %basis_hbm.1, bf16[704,512]{1,0:T(8,128)(2,1)} %constant.2.clone.later_hbm, ...), custom_call_target="tpu_custom_call" | custom-call | tf_op jit(solution)/shard_map/pack/pallas_call | solution.py:336
  7.6 23.4 %all_to_all.22 = f32[256,1,128]{2,1,0:T(1,128)S(1)} all-to-all(f32[256,1,128]{2,1,0:T(1,128)S(1)} %bitcast.11), channel_id=1, replica_groups=mesh['tm'=128,'rows'=2] {'tm','rows'}, dimensions={0} | all-to-all | bytes 262144 | tf_op jit(solution)/shard_map/all_to_all | solution.py:353
  31.0 1.4 %solve.1 = f32[256,128]{1,0:T(8,128)S(1)} custom-call(f32[256,128]{1,0:T(8,128)S(1)} %bitcast.8, f32[40,128]{1,0:T(8,128)S(1)} %get-tuple-element.9.refs_1_, bf16[704,512]{1,0:T(8,128)(2,1)S(1)} %get-tuple-element.10.refs_2_), custom_call_target="tpu_custom_call" | custom-call | tf_op jit(solution)/shard_map/solve/pallas_call | solution.py:354
  32.4 18.6 %all_to_all.23 = f32[256,1,128]{2,1,0:T(1,128)S(1)} all-to-all(f32[256,1,128]{2,1,0:T(1,128)S(1)} %bitcast.9), channel_id=1, replica_groups=mesh['tm'=128,'rows'=2] {'tm','rows'}, dimensions={0} | all-to-all | bytes 262144 | tf_op jit(solution)/shard_map/all_to_all | solution.py:360
  51.0 1.0 %unpack.1 = (f32[2,1,8,512]{3,2,1,0:T(8,128)}, f32[2,1,8,512]{3,2,1,0:T(8,128)}, f32[5]{0:T(128)}) custom-call(f32[256,128]{1,0:T(8,128)S(1)} %bitcast.10, f32[2,1,8,512]{3,2,1,0:T(8,128)S(1)} %get-tuple-element.11.resid_ref, bf16[2,2,256,256]{3,2,1,0:T(8,128)(2,1)S(1)} %get-tuple-element.12.tables_ref), custom_call_target="tpu_custom_call" | custom-call | tf_op jit(solution)/shard_map/unpack/pallas_call | solution.py:362
Async XLA Ops:
  0.6 5.5 %collective-permute-start = (f32[4,2,1,8,512]{4,3,2,1,0:T(8,128)}, f32[4,2,1,8,512]{4,3,2,1,0:T(8,128)S(1)}, u32[]{:S(2)}, u32[]{:S(2)}) collective-permute-start(f32[4,2,1,8,512]{4,3,2,1,0:T(8,128)} %basis_hbm.1), channel_id=1, source_target_pairs={{0,2},{1,3}} | collective-permute-start | bytes 393224 | tf_op jit(solution)/shard_map/ppermute | solution.py:335
